TPU v7x, 128 devices: a whole 4x4x4 slice. The times are simulated.
128 devices in a mesh: ops: 32 (over z, y, core), site: 4 (over x).
Axes of the slice: x: 4, y: 4, z: 4, core: 2. Of those that a mesh axis runs over, the one named last changes fastest.
Arguments:
- wavefunction: bfloat16 [2048, 2048], replicated, may hold values from -6 to 6
- left_blocks: bfloat16 [256, 16, 192, 192], P('ops', 'site'), may hold values from -0.4375 to 0.4375
- right_blocks: bfloat16 [256, 16, 192, 192], P('ops', 'site'), may hold values from -0.078125 to 0.078125
- left_sector: int32 [2048], replicated, may hold values from 0 to 15, as said below
- right_sector: int32 [2048], replicated, may hold values from 0 to 15, as said below
- term_count: int32 [32], P('ops'), may hold values from 1 to 8, as said below
- left_energy: float32 [2048], replicated, may hold values from -1 to 1
- right_energy: float32 [2048], replicated, may hold values from -1 to 1
- subspace: bfloat16 [2, 16, 192, 2048], P(None, 'site'), may hold values from -0.0078125 to 0.0078125
Outputs:
- sigma: bfloat16 [16, 192, 2048], P('site')
- projections: float32 [2], replicated
Inputs may be any that keep to these rules, and one draw needn't show every extreme that they name: `left_sector`: sector ids never fall along the bond; each of the 16 sectors has 1 to 192 states and one has exactly 192. `right_sector`: sector ids never fall along the bond; each of the 16 sectors has 1 to 192 states and one has exactly 192. `term_count`: some group has all 8 slots live.
All inputs are finite; a program needn't handle non-finite values.
Results may differ from a plain program's by a relative error of at most 0.0045.
Values may be sent and summed in bfloat16 or wider, within the bound.
No kernel may reach another device: no remote copies, remote signals or barrier semaphores. Data moves between devices by JAX's collectives and lax.ppermute only.
A program may use at most 192 MiB of HBM per device.

v0:
```python
import functools

import jax
import jax.numpy as jnp
from jax import lax
from jax.experimental import pallas as pl
from jax.experimental.pallas import tpu as pltpu
from jax.sharding import Mesh
from jax.sharding import PartitionSpec as P


OPS = ("z", "y", "core")
CHUNK = 4
WIN_ROWS = 256
WIN_COLS = 384
SLOT_COLS = 256
GROUP_COLS = 4 * SLOT_COLS
EXTRA = 128

MY_START, MY_SIZE, RIGHT_START, RIGHT_SIZE = 0, 4, 8, 24
SITE, CORE, MEMBER = 0, 1, 2
DIAGONAL_ROWS = 32


def params():
    return pltpu.CompilerParams(vmem_limit_bytes=56 * 1024 * 1024)


def pack_one(blocks, slot, half, out, index, at=0):
    out[index + (at,)] = blocks[slot, 2 * half, :, :128]
    out[index + (at + 1,)] = blocks[slot, 2 * half + 1, :, :128]
    out[index + (at + 2,)] = jnp.concatenate(
        [blocks[slot, 2 * half, :, 128:192], blocks[slot, 2 * half + 1, :, 128:192]], axis=1
    )


def pack_early_body(blocks, first, second):
    for slot in range(2):
        pack_one(blocks, slot, 0, first, (slot,))
        pack_one(blocks, slot, 1, second, (slot,))


def pack_late_body(left, right, *outs):
    for k in range(4):

        @pl.when(pl.program_id(0) == k)
        def _():
            for half in range(2):
                pack_one(left, 0, half, outs[k], (), 3 * half)
                pack_one(right, 0, half, outs[k], (), 6 + 3 * half)


def pack_early(blocks):
    spec = pl.BlockSpec((2, 3, 192, 128), lambda i: (i, 0, 0, 0))
    shape = jax.ShapeDtypeStruct((CHUNK, 3, 192, 128), jnp.bfloat16)
    return pl.pallas_call(
        pack_early_body,
        grid=(2,),
        in_specs=[pl.BlockSpec((2, 4, 192, 192), lambda i: (i, 0, 0, 0))],
        out_specs=[spec, spec],
        out_shape=[shape, shape],
        name="pack_early",
    )(blocks)


def pack_late(left, right):
    block = pl.BlockSpec((1, 4, 192, 192), lambda i: (i + CHUNK, 0, 0, 0))
    return pl.pallas_call(
        pack_late_body,
        grid=(4,),
        in_specs=[block, block],
        out_specs=[pl.BlockSpec((12, 192, 128), lambda i: (0, 0, 0))] * 4,
        out_shape=[jax.ShapeDtypeStruct((12, 192, 128), jnp.bfloat16)] * 4,
        cost_estimate=pl.CostEstimate(flops=2 * 10**9, bytes_accessed=2**22, transcendentals=0),
        name="pack_late",
    )(left, right)


def select_body(where, left_sector, right_sector, left_energy, psi, table, rows, cols, energies, window, sems):
    group = pl.program_id(0)

    @pl.when(group == 0)
    def _():
        site = where[SITE]
        left_ids = left_sector[...]
        right_ids = right_sector[...]
        for within in range(4):
            sector = 4 * site + within
            table[MY_START + within] = jnp.sum((left_ids < sector).astype(jnp.int32))
            table[MY_SIZE + within] = jnp.sum((left_ids == sector).astype(jnp.int32))
        before = jnp.int32(0)
        for sector in range(16):
            size = jnp.sum((right_ids == sector).astype(jnp.int32))
            table[RIGHT_START + sector] = before
            table[RIGHT_SIZE + sector] = size
            before = before + size
        copies = []
        shifts = []
        for within in range(4):
            start = table[MY_START + within]
            base = pl.multiple_of(jnp.minimum((start // 16) * 16, psi.shape[0] - WIN_ROWS), 16)
            shifts.append(start - base)
            copies.append(
                pltpu.make_async_copy(psi.at[pl.ds(base, WIN_ROWS), :], window.at[within], sems.at[within])
            )
        for copy in copies:
            copy.start()
        row = lax.broadcasted_iota(jnp.int32, (192, WIN_ROWS), 0)
        col = lax.broadcasted_iota(jnp.int32, (192, WIN_ROWS), 1)
        wide_row = lax.broadcasted_iota(jnp.int32, (192, WIN_COLS), 0)
        wide_col = lax.broadcasted_iota(jnp.int32, (192, WIN_COLS), 1)
        for within in range(4):
            start = table[MY_START + within]
            size = table[MY_SIZE + within]
            base = pl.multiple_of(jnp.minimum((start // 128) * 128, psi.shape[0] - WIN_COLS), 128)
            kept = (wide_col == wide_row + (start - base)) & (wide_row < size)
            near = jnp.where(kept, left_energy[:, pl.ds(base, WIN_COLS)], 0.0)
            energies[pl.ds(within * 192, 192), :] = jnp.sum(near, axis=1, keepdims=True)
        for within in range(4):
            copies[within].wait()
            kept = (col == row + shifts[within]) & (row < table[MY_SIZE + within])
            pick = jnp.where(kept, 1.0, 0.0).astype(jnp.bfloat16)
            got = jnp.dot(pick, window[within], preferred_element_type=jnp.float32)
            rows[pl.ds(within * 192, 192), :] = got.astype(jnp.bfloat16)

    row = lax.broadcasted_iota(jnp.int32, (WIN_COLS, SLOT_COLS), 0)
    lane = lax.broadcasted_iota(jnp.int32, (WIN_COLS, SLOT_COLS), 1)

    def two_sectors(half, carry):
        for odd in range(2):
            start = table[RIGHT_START + 4 * group + 2 * half + odd]
            size = table[RIGHT_SIZE + 4 * group + 2 * half + odd]
            base = pl.multiple_of(jnp.minimum((start // 128) * 128, rows.shape[1] - WIN_COLS), 128)
            at = jnp.where(lane < 128, lane, jnp.where(lane < 192, size, lane - 64)) if odd else lane
            kept = (row == at + (start - base)) & (at < size)
            pick = jnp.where(kept, 1.0, 0.0).astype(jnp.bfloat16)
            got = jnp.dot(rows[:, pl.ds(base, WIN_COLS)], pick, preferred_element_type=jnp.float32)
            where_to = pl.multiple_of(SLOT_COLS * (2 * half + odd), SLOT_COLS)
            cols[0, :, pl.ds(where_to, SLOT_COLS)] = got.astype(jnp.bfloat16)
        return carry

    lax.fori_loop(0, 2, two_sectors, 0)


def select(where, left_sector, right_sector, left_energy, psi):
    bond = psi.shape[1]
    smem = pl.BlockSpec(memory_space=pltpu.SMEM)
    ids = pl.BlockSpec((bond // 128, 128), lambda g: (0, 0))
    return pl.pallas_call(
        select_body,
        grid=(4,),
        in_specs=[smem, ids, ids, pl.BlockSpec((1, bond), lambda g: (0, 0)), pl.BlockSpec(memory_space=pltpu.HBM)],
        out_specs=[
            smem,
            pl.BlockSpec((768, bond), lambda g: (0, 0)),
            pl.BlockSpec((1, 768, GROUP_COLS), lambda g: (g, 0, 0)),
            pl.BlockSpec((768, 1), lambda g: (0, 0)),
        ],
        out_shape=[
            jax.ShapeDtypeStruct((40,), jnp.int32),
            jax.ShapeDtypeStruct((768, bond), jnp.bfloat16),
            jax.ShapeDtypeStruct((4, 768, GROUP_COLS), jnp.bfloat16),
            jax.ShapeDtypeStruct((768, 1), jnp.float32),
        ],
        scratch_shapes=[
            pltpu.VMEM((4, WIN_ROWS, bond), jnp.bfloat16),
            pltpu.SemaphoreType.DMA((4,)),
        ],
        compiler_params=params(),
        cost_estimate=pl.CostEstimate(flops=5 * 10**9, bytes_accessed=2**24, transcendentals=0),
        name="select",
    )(
        where,
        left_sector.reshape(bond // 128, 128),
        right_sector.reshape(bond // 128, 128),
        left_energy[None, :],
        psi,
    )


def multiply_slots(lefts, rights, psi, image, acc, last_live):
    count = len(lefts)
    for u in range(count):
        for within in range(4):
            got = jnp.dot(
                lefts[u](within), psi[within * 192 : (within + 1) * 192, :], preferred_element_type=jnp.float32
            )
            if u == 1:
                got = jnp.where(last_live, got, 0.0)
            image[u, within * 192 : (within + 1) * 192, :] = got.astype(jnp.bfloat16)
    for q in range(4):
        parts = None
        for u in range(count):
            block = jnp.concatenate([rights[u](q), jnp.zeros((64, 256), jnp.bfloat16)], axis=0)
            part = lax.dot_general(
                image[u, :, q * SLOT_COLS : (q + 1) * SLOT_COLS],
                block,
                (((1,), (1,)), ((), ())),
                preferred_element_type=jnp.float32,
            )
            parts = part if parts is None else parts + part
        acc[:, q * SLOT_COLS : (q + 1) * SLOT_COLS] += parts


def products_body(rels, where, count, left, psi, *refs):
    groups = len(rels)
    live = jnp.minimum(count[0], CHUNK)
    rights = [refs[2 * i : 2 * i + 2] for i in range(groups)]
    out, left_v, right_v, psi_v, image, acc_v, sem_left, sem_right, sem_psi, sem_out = refs[2 * groups :]
    site = where[SITE]
    left_copies = [
        pltpu.make_async_copy(left.at[pl.ds(2 * p, 2)], left_v.at[pl.ds(2 * p, 2)], sem_left.at[p])
        for p in range(2)
    ]
    copies = []
    for i in range(groups):
        copies.append(
            [
                pltpu.make_async_copy(rights[i][0], right_v.at[i, 0], sem_right.at[i, 0]),
                pltpu.make_async_copy(rights[i][1], right_v.at[i, 1], sem_right.at[i, 1]),
                pltpu.make_async_copy(psi.at[(site + rels[i]) % 4], psi_v.at[i], sem_psi.at[i]),
            ]
        )
    out_copies = [
        [
            pltpu.make_async_copy(
                acc_v.at[i, pl.ds(192 * w, 192)], out.at[i, pl.ds(192 * w, 192)], sem_out.at[i, w]
            )
            for w in range(4)
        ]
        for i in range(groups)
    ]
    for copy in left_copies + copies[0]:
        copy.start()
    acc_v[0] = jnp.zeros(acc_v.shape[1:], jnp.float32)
    for copy in left_copies:
        copy.wait()

    def one_group(i, carry):
        for j in range(groups):

            @pl.when(i == j)
            def _():
                for copy in copies[j]:
                    copy.wait()
                if j + 1 < groups:
                    for copy in copies[j + 1]:
                        copy.start()
                    acc_v[j + 1] = jnp.zeros(acc_v.shape[1:], jnp.float32)

        def one_pair(p, inner):
            lefts = [lambda within, u=u: left_v[2 * p + u, within] for u in range(2)]
            block = [
                lambda q, u=u: jnp.concatenate(
                    [right_v[i, q // 2, 2 * p + u, q % 2], right_v[i, q // 2, 2 * p + u, 2]], axis=1
                )
                for u in range(2)
            ]
            multiply_slots(lefts, block, psi_v.at[i], image, acc_v.at[i], 2 * p + 1 < live)
            return inner

        lax.fori_loop(0, (live + 1) // 2, one_pair, 0)
        for j in range(groups):

            @pl.when(i == j)
            def _():
                for copy in out_copies[j]:
                    copy.start()

        return carry

    lax.fori_loop(0, groups, one_group, 0)
    for found in out_copies:
        for copy in found:
            copy.wait()


def products(rels, where, count, left, psi, rights):
    groups = len(rels)
    smem = pl.BlockSpec(memory_space=pltpu.SMEM)
    hbm = pl.BlockSpec(memory_space=pltpu.HBM)
    flops = groups * 2 * 1024 * 768 * (192 + 256) * 4
    return pl.pallas_call(
        functools.partial(products_body, tuple(rels)),
        in_specs=[smem, smem, hbm, hbm] + [hbm] * (2 * groups),
        out_specs=hbm,
        out_shape=jax.ShapeDtypeStruct((groups, 768, GROUP_COLS), jnp.float32),
        scratch_shapes=[
            pltpu.VMEM((CHUNK, 4, 192, 192), jnp.bfloat16),
            pltpu.VMEM((groups, 2, CHUNK, 3, 192, 128), jnp.bfloat16),
            pltpu.VMEM((groups, 768, GROUP_COLS), jnp.bfloat16),
            pltpu.VMEM((2, 768, GROUP_COLS), jnp.bfloat16),
            pltpu.VMEM((groups, 768, GROUP_COLS), jnp.float32),
            pltpu.SemaphoreType.DMA((2,)),
            pltpu.SemaphoreType.DMA((groups, 2)),
            pltpu.SemaphoreType.DMA((groups,)),
            pltpu.SemaphoreType.DMA((groups, 4)),
        ],
        compiler_params=params(),
        cost_estimate=pl.CostEstimate(flops=flops, bytes_accessed=8 * 2**20, transcendentals=0),
        name="products",
    )(where, count, left, psi, *[half for halves in rights for half in halves])


def finish_body(slots, where, count, table, own, near, far_a, far_b, left, psi, *refs):
    live = jnp.minimum(count[0], CHUNK)
    rows, subspace, energies, right_energy = refs[:4]
    refs = list(refs[4:])
    if slots:
        counts, extras, moved = refs[:4], refs[4:8], refs[8:11]
        there = [counts[k][0] > CHUNK + k for k in range(4)]
        refs = refs[11:]
    send, mine, proj, left_v, right_v, psi_v, image, acc_v, rows_v, sub_v, total, staged, sums = refs[:13]
    sem_left, sem_right, sem_psi, sem_acc, sem_rows, sem_sub, sem_out = refs[13:20]
    width = subspace.shape[3]
    core = where[CORE]
    site = where[SITE]
    member = where[MEMBER]

    left_copies = [
        pltpu.make_async_copy(left.at[pl.ds(2 * p, 2)], left_v.at[pl.ds(2 * p, 2)], sem_left.at[p])
        for p in range(2)
    ]
    far_copies = [
        pltpu.make_async_copy(far_a, right_v.at[0], sem_right.at[0]),
        pltpu.make_async_copy(far_b, right_v.at[1], sem_right.at[1]),
    ]
    psi_copies = {
        i: pltpu.make_async_copy(psi.at[(site + i) % 4], psi_v.at[i], sem_psi.at[i])
        for i in ((2, 0, 1, 3) if slots else (2,))
    }
    acc_copies = [
        pltpu.make_async_copy(source, acc_v.at[rel], sem_acc.at[rel])
        for rel, source in ((0, own.at[0]), (1, near.at[0]), (3, near.at[1]))
    ]
    their = jnp.minimum(member, 768 // DIAGONAL_ROWS - 1)
    rows_copy = pltpu.make_async_copy(
        rows.at[pl.ds(pl.multiple_of(DIAGONAL_ROWS * their, DIAGONAL_ROWS), DIAGONAL_ROWS)],
        rows_v,
        sem_rows,
    )

    def sub_copies(step):
        within = 2 * ((1 - core) if step < 2 else core) + step % 2
        return [
            pltpu.make_async_copy(subspace.at[k, within], sub_v.at[step, k], sem_sub.at[step, k]) for k in range(2)
        ]

    for copy in left_copies + far_copies:
        copy.start()
    psi_copies[2].start()
    if slots:
        extra_v, moved_v, sem_extra, sem_moved = refs[20:]
        extra_copies = []
        taken = False
        for k in range(4):
            place = 0 if slots == 1 else k
            copy = pltpu.make_async_copy(extras[k], extra_v.at[place], sem_extra.at[place])
            extra_copies.append((there[k] & jnp.logical_not(taken) if slots == 1 else there[k], copy))
            taken = there[k] | taken
        moved_copies = [
            pltpu.make_async_copy(moved[i], moved_v.at[i + 1], sem_moved.at[i]) for i in range(3)
        ]
    acc_v[2] = jnp.zeros(acc_v.shape[1:], jnp.float32)
    for copy in left_copies + far_copies:
        copy.wait()
    psi_copies[2].wait()

    for copy in acc_copies:
        copy.start()
    if slots:
        for wanted, copy in extra_copies:

            @pl.when(wanted)
            def _():
                copy.start()

        for i in (0, 1, 3):
            psi_copies[i].start()
        for copy in moved_copies:
            copy.start()
    else:
        rows_copy.start()
        for step in range(4):
            for copy in sub_copies(step):
                copy.start()

    def one_pair(p, inner):
        lefts = [lambda within, u=u: left_v[2 * p + u, within] for u in range(2)]
        blocks = [
            lambda q, u=u: jnp.concatenate(
                [right_v[q // 2, 2 * p + u, q % 2], right_v[q // 2, 2 * p + u, 2]], axis=1
            )
            for u in range(2)
        ]
        multiply_slots(lefts, blocks, psi_v.at[2], image, acc_v.at[2], 2 * p + 1 < live)
        return inner

    lax.fori_loop(0, (live + 1) // 2, one_pair, 0)
    for copy in acc_copies:
        copy.wait()
    if slots:
        for wanted, copy in extra_copies:

            @pl.when(wanted)
            def _():
                copy.wait()

        for i in (0, 1, 3):
            psi_copies[i].wait()
        for copy in moved_copies:
            copy.wait()
        rows_copy.start()
        for step in range(4):
            for copy in sub_copies(step):
                copy.start()
        moved_v[0] = extra_v[:, 6:12]
        alive = [jnp.int32(1)] if slots == 1 else [one.astype(jnp.int32) for one in there]

        def one_group(i, carry):
            def one_slot(n, inner):
                wanted = alive[0]
                for k in range(1, slots):
                    wanted = jnp.where(n == k, alive[k], wanted)

                @pl.when(wanted > 0)
                def _():
                    def left_block(within):
                        at = 3 * (within // 2)
                        lane = 64 * (within % 2)
                        high = extra_v[n, at + 2]
                        return jnp.concatenate([extra_v[n, at + within % 2], high[:, lane : lane + 64]], axis=1)

                    def right_block(q):
                        at = 3 * (q // 2)
                        return jnp.concatenate([moved_v[i, n, at + q % 2], moved_v[i, n, at + 2]], axis=1)

                    multiply_slots([left_block], [right_block], psi_v.at[i], image, acc_v.at[i], None)

                return inner

            lax.fori_loop(0, slots, one_slot, 0)
            return carry

        lax.fori_loop(0, 4, one_group, 0)
    rows_copy.wait()

    lane = lax.broadcasted_iota(jnp.int32, (192, 128), 1)
    row = lax.broadcasted_iota(jnp.int32, (192, width), 0)
    sums[...] = jnp.zeros(sums.shape, jnp.float32)

    def out_copy(step):
        out = send if step < 2 else mine
        return pltpu.make_async_copy(staged.at[step], out.at[pl.ds(192 * (step % 2), 192)], sem_out.at[step])

    def one_block(step, carry):
        for j in range(4):

            @pl.when(step == j)
            def _():
                for copy in sub_copies(j):
                    copy.wait()

        within = 2 * jnp.where(step < 2, 1 - core, core) + step % 2
        here = pl.ds(pl.multiple_of(192 * within, 192), 192)

        def one_site(i, inner):
            rel = (i + 4 - site) % 4
            for q in range(4):
                start = table[RIGHT_START + 4 * i + q]
                base = pl.multiple_of((start // 128) * 128, 128)
                shift = start - base
                first = pltpu.roll(acc_v[rel, here, q * SLOT_COLS : q * SLOT_COLS + 128], shift, 1)
                second = pltpu.roll(acc_v[rel, here, q * SLOT_COLS + 128 : (q + 1) * SLOT_COLS], shift, 1)
                low = lane < shift
                total[:, pl.ds(base, 128)] = jnp.where(low, total[:, pl.ds(base, 128)], first)
                total[:, pl.ds(base + 128, 128)] = jnp.where(low, first, second)
                total[:, pl.ds(base + 256, 128)] = second
            return inner

        lax.fori_loop(0, 4, one_site, 0)
        per = 192 // DIAGONAL_ROWS

        @pl.when(member // per == within)
        def _():
            at = pl.multiple_of(DIAGONAL_ROWS * (member % per), DIAGONAL_ROWS)
            part = pl.ds(at, DIAGONAL_ROWS)
            energy = energies[pl.ds(pl.multiple_of(192 * within + at, DIAGONAL_ROWS), DIAGONAL_ROWS), :]
            total[part, :width] += (energy + right_energy[...]) * rows_v[...].astype(jnp.float32)

        kept = jnp.where(row < table[MY_SIZE + within], total[:, :width], 0.0)
        for k in range(2):
            part = sub_v[step, k].astype(jnp.float32) * kept
            sums[k] += jnp.sum(part.reshape(24, 8, width), axis=0)
        staged[step] = kept.astype(jnp.bfloat16)
        for j in range(4):

            @pl.when(step == j)
            def _():
                out_copy(j).start()

        return carry

    lax.fori_loop(0, 4, one_block, 0)
    for k in range(2):
        added = sums[k, :, :128]
        for j in range(1, width // 128):
            added = added + sums[k, :, 128 * j : 128 * (j + 1)]
        proj[k] = added
    for j in range(4):
        out_copy(j).wait()


def finish(slots, where, count, table, own, near, far, left, psi, rows, subspace, energies, right_energy, late=()):
    width = rows.shape[1]
    smem = pl.BlockSpec(memory_space=pltpu.SMEM)
    hbm = pl.BlockSpec(memory_space=pltpu.HBM)
    vmem = pl.BlockSpec(memory_space=pltpu.VMEM)
    half = jax.ShapeDtypeStruct((384, width), jnp.bfloat16)
    scratch = [
        pltpu.VMEM((CHUNK, 4, 192, 192), jnp.bfloat16),
        pltpu.VMEM((2, CHUNK, 3, 192, 128), jnp.bfloat16),
        pltpu.VMEM((4, 768, GROUP_COLS), jnp.bfloat16),
        pltpu.VMEM((2, 768, GROUP_COLS), jnp.bfloat16),
        pltpu.VMEM((4, 768, GROUP_COLS), jnp.float32),
        pltpu.VMEM((DIAGONAL_ROWS, width), jnp.bfloat16),
        pltpu.VMEM((4, 2, 192, width), jnp.bfloat16),
        pltpu.VMEM((192, width + 256), jnp.float32),
        pltpu.VMEM((4, 192, width), jnp.bfloat16),
        pltpu.VMEM((2, 8, width), jnp.float32),
        pltpu.SemaphoreType.DMA((2,)),
        pltpu.SemaphoreType.DMA((2,)),
        pltpu.SemaphoreType.DMA((4,)),
        pltpu.SemaphoreType.DMA((4,)),
        pltpu.SemaphoreType.DMA(()),
        pltpu.SemaphoreType.DMA((4, 2)),
        pltpu.SemaphoreType.DMA((4,)),
    ]
    if slots:
        scratch += [
            pltpu.VMEM((slots, 12, 192, 128), jnp.bfloat16),
            pltpu.VMEM((4, slots, 6, 192, 128), jnp.bfloat16),
            pltpu.SemaphoreType.DMA((4,)),
            pltpu.SemaphoreType.DMA((3,)),
        ]
    return pl.pallas_call(
        functools.partial(finish_body, slots),
        in_specs=[smem] * 3 + [hbm] * 8 + [vmem, vmem] + ([smem] * 4 + [hbm] * 7 if slots else []),
        out_specs=[hbm, hbm, vmem],
        out_shape=[half, half, jax.ShapeDtypeStruct((2, 8, 128), jnp.float32)],
        scratch_shapes=scratch,
        compiler_params=params(),
        cost_estimate=pl.CostEstimate(flops=8 * 10**9, bytes_accessed=30 * 2**20, transcendentals=0),
        name="finish",
    )(where, count, table, own, near, *far, left, psi, rows, subspace, energies, right_energy, *late)


def place_body(which, where, half, *rest):
    out, sems = rest[-2:]
    core = where[CORE] if which == 0 else 1 - where[CORE]
    copies = [
        pltpu.make_async_copy(
            half.at[n // 2, pl.ds(96 * (n % 2), 96)],
            out.at[2 * core + n // 2, pl.ds(96 * (n % 2), 96)],
            sems.at[n],
        )
        for n in range(4)
    ]
    for copy in copies:
        copy.start()
    for copy in copies:
        copy.wait()


def place(which, where, half, whole=None):
    hbm = pl.BlockSpec(memory_space=pltpu.HBM)
    args = (where, half) if whole is None else (where, half, whole)
    return pl.pallas_call(
        functools.partial(place_body, which),
        in_specs=[pl.BlockSpec(memory_space=pltpu.SMEM), pl.BlockSpec(memory_space=pltpu.VMEM)]
        + [hbm] * (len(args) - 2),
        out_specs=hbm,
        out_shape=jax.ShapeDtypeStruct((4,) + half.shape[1:], half.dtype),
        scratch_shapes=[pltpu.SemaphoreType.DMA((4,))],
        input_output_aliases={} if whole is None else {2: 0},
        cost_estimate=pl.CostEstimate(flops=10**9, bytes_accessed=2**22, transcendentals=0),
        name="place",
    )(*args)


def shifted(value, axis, by):
    size = lax.axis_size(axis)
    return lax.ppermute(value, axis, [(i, (i + by) % size) for i in range(size)])


def small_sum(value, axis):
    size = lax.axis_size(axis)
    me = lax.axis_index(axis)
    got = [value] + [shifted(value, axis, k) for k in range(1, size)]
    total = None
    for source in range(size):
        one = sum(jnp.where((me - source) % size == k, got[k], 0.0) for k in range(size))
        total = one if total is None else total + one
    return total


def local(
    wavefunction,
    left_blocks,
    right_blocks,
    left_sector,
    right_sector,
    term_count,
    left_energy,
    right_energy,
    subspace,
):
    bond = wavefunction.shape[0]
    site = lax.axis_index("site")
    core = lax.axis_index("core")
    mine_early = pack_early(right_blocks)
    prev = [shifted(half, "site", 1) for half in mine_early]
    following = [shifted(half, "site", -1) for half in mine_early]
    left_later, right_later, count_later, _ = lax.optimization_barrier(
        (left_blocks, right_blocks, term_count, mine_early[0])
    )

    ways = (("y", 1), ("y", -1), ("z", 1), ("z", -1))
    late = pack_late(left_later, right_later)
    extras = [shifted(late[k], axis, by) for k, (axis, by) in enumerate(ways)]
    counts = [shifted(count_later, axis, by) for axis, by in ways]
    there = [counts[k][0] > CHUNK + k for k in range(4)]
    number = sum(one.astype(jnp.int32) for one in there)

    where = jnp.stack([site, core, lax.axis_index(OPS)])
    table, rows, psi, energies = select(where, left_sector, right_sector, left_energy, wavefunction)
    own = products((0,), where, term_count, left_blocks, psi, [mine_early])

    def rest(slots, going, prev, following):
        far = (shifted(prev[0], "site", 1), shifted(following[1], "site", -1))
        arrived = []
        if slots:
            arrived = [*counts, *extras] + [shifted(going, "site", by) for by in (-1, 2, 1)]
        near = products((1, 3), where, term_count, left_blocks, psi, [following, prev])
        return tuple(
            finish(
                slots,
                where,
                term_count,
                table,
                own,
                near,
                far,
                left_blocks,
                psi,
                rows,
                subspace,
                energies,
                right_energy[None, :],
                late=arrived,
            )
        )

    def none(*moved):
        return rest(0, None, *moved)

    def one(*moved):
        going = extras[3][6:12]
        for k in (2, 1, 0):
            going = jnp.where(there[k], extras[k][6:12], going)
        return rest(1, going[None], *moved)

    def many(*moved):
        return rest(4, jnp.stack([one[6:12] for one in extras]), *moved)

    send, mine, proj = lax.switch(jnp.minimum(number, 2), [none, one, many], prev, following)
    swap = [(0, 1), (1, 0)]
    away = lax.ppermute(send, "core", swap)
    proj = small_sum(jnp.broadcast_to(jnp.sum(proj, axis=(1, 2))[None, :], (8, 2)), "site")[0]
    both = (mine.astype(jnp.float32) + away.astype(jnp.float32)).astype(jnp.bfloat16)

    high = lax.reduce_precision(proj, 8, 7)
    middle = lax.reduce_precision(proj - high, 8, 7)
    thirds = jnp.concatenate([high, middle, proj - high - middle]).astype(jnp.bfloat16)
    plane = lax.axis_size(("z", "y"))
    half = both.shape[0]
    share = half // plane
    extra = jnp.broadcast_to(jnp.pad(thirds, (0, EXTRA - 6))[None, :], (half, EXTRA))
    both = jnp.concatenate([both, extra], axis=1)

    pieces = lax.all_to_all(both.reshape(plane, share, bond + EXTRA), ("z", "y"), 0, 0, tiled=True)
    added = jnp.sum(pieces.astype(jnp.float32), axis=0)
    summed = added[:, :bond].astype(jnp.bfloat16)
    gathered = lax.all_to_all(
        jnp.broadcast_to(summed[None], (plane, share, bond)), ("z", "y"), 0, 0, tiled=True
    ).reshape(half, bond)
    whole = added[:8, bond : bond + 2] + added[:8, bond + 2 : bond + 4] + added[:8, bond + 4 : bond + 6]
    gathered = gathered.reshape(2, 192, bond)
    other = lax.ppermute(gathered, "core", swap)
    placed = place(0, where, gathered)
    projections = whole + lax.ppermute(whole, "core", swap)
    sigma = place(1, where, other, placed)
    return sigma, projections[0]


def solution(mesh):
    shape = dict(mesh.shape)
    ops = shape["ops"]
    parts = Mesh(mesh.devices.reshape(4, ops // 8, 2, shape["site"]), ("z", "y", "core", "site"))
    in_specs = (
        P(),
        P(OPS, "site", None, None),
        P(OPS, "site", None, None),
        P(),
        P(),
        P(OPS),
        P(),
        P(),
        P(None, "site", None, None),
    )
    out_specs = (P("site", None, None), P())
    return jax.shard_map(local, mesh=parts, in_specs=in_specs, out_specs=out_specs, check_vma=False)
```

profile of v0, /device:TPU:1, one launch (start us, length us, event | category | flops | bytes accessed | tf_op | source)
XLA Modules:
  0.0 173.9 jit_solution(15303953501497074841)
XLA Ops:
  0.6 2.5 %pack_early.1 = (bf16[4,3,192,128]{3,2,1,0:T(8,128)(2,1)}, bf16[4,3,192,128]{3,2,1,0:T(8,128)(2,1)}) custom-call(bf16[8,4,192,192]{3,2,1,0:T(8,128)(2,1)} %right), custom_call_target="tpu_custom_call" | custom-call | tf_op jit(solution)/shard_map/pack_early/pallas_call | solution.py:56
  3.1 3.9 %pack_late.1 = (bf16[12,192,128]{2,1,0:T(8,128)(2,1)}, bf16[12,192,128]{2,1,0:T(8,128)(2,1)}, bf16[12,192,128]{2,1,0:T(8,128)(2,1)}, bf16[12,192,128]{2,1,0:T(8,128)(2,1)}) custom-call(bf16[8,4,192,192]{3,2,1,0:T(8,128)(2,1)S(1)} %copy-done.2, bf16[8,4,192,192]{3,2,1,0:T(8,128)(2,1)} %right), custom_call_target="tpu_custom_call" | custom-call | flops 2000000000 | bytes 4194304 | tf_op jit(solution)/shard_map/pack_late/pallas_call | solution.py:68
  7.0 2.1 %collective-permute-start.20 = (bf16[12,192,128]{2,1,0:T(8,128)(2,1)}, bf16[12,192,128]{2,1,0:T(8,128)(2,1)S(1)}, u32[]{:S(2)}, u32[]{:S(2)}) collective-permute-start(bf16[12,192,128]{2,1,0:T(8,128)(2,1)} %get-tuple-element.225), channel_id=1, source_target_pairs={{0,8},{8,16},{16,24},{24,0},{1,9},{9,17},{17,25},{25,1},{2,10},{10... | collective-permute-start | bytes 1769480 | tf_op jit(solution)/shard_map/ppermute | solution.py:593
  9.1 1.4 collective-permute-start.21
  10.6 1.6 collective-permute-start.22
  12.2 2.7 %collective-permute-start.13 = (s32[1]{0:T(128)}, s32[1]{0:T(128)}, u32[]{:S(2)}, u32[]{:S(2)}) collective-permute-start(s32[1]{0:T(128)} %param.17), channel_id=1, source_target_pairs={{0,24},{8,0},{16,8},{24,16},{1,25},{9,1},{17,9},{25,17},{2,26},{10... | collective-permute-start | bytes 20 | tf_op jit(solution)/shard_map/ppermute | solution.py:593
  15.7 8.1 %collective-permute-done.12 = s32[1]{0:T(128)} collective-permute-done((s32[1]{0:T(128)}, s32[1]{0:T(128)}, u32[]{:S(2)}, u32[]{:S(2)}) %collective-permute-start.12) | collective-permute-done | bytes 36 | tf_op jit(solution)/shard_map/ppermute | solution.py:593
  23.7 1.5 collective-permute-start.14
  25.2 2.1 %collective-permute-start.15 = (s32[1]{0:T(128)}, s32[1]{0:T(128)}, u32[]{:S(2)}, u32[]{:S(2)}) collective-permute-start(s32[1]{0:T(128)} %param.17), channel_id=1, source_target_pairs={{0,96},{32,0},{64,32},{96,64},{1,97},{33,1},{65,33},{97,65},{2,98}... | collective-permute-start | bytes 20 | tf_op jit(solution)/shard_map/ppermute | solution.py:593
  27.4 1.1 collective-permute-done.14
  28.4 2.5 %collective-permute-start.16 = (bf16[4,3,192,128]{3,2,1,0:T(8,128)(2,1)}, bf16[4,3,192,128]{3,2,1,0:T(8,128)(2,1)}, u32[]{:S(2)}, u32[]{:S(2)}) collective-permute-start(bf16[4,3,192,128]{3,2,1,0:T(8,128)(2,1)} %get-tuple-element.216.refs_0_), channel_id=1, source_target_pairs={{0,3},{1,0},{2,1},{3,2},{4,7},{5,4},{6,5},{7,6},{8,11},{9,8},{10,9... | collective-permute-start | bytes 1769480 | tf_op jit(solution)/shard_map/ppermute | solution.py:593
  30.9 2.7 %collective-permute-start.17 = (bf16[4,3,192,128]{3,2,1,0:T(8,128)(2,1)}, bf16[4,3,192,128]{3,2,1,0:T(8,128)(2,1)}, u32[]{:S(2)}, u32[]{:S(2)}) collective-permute-start(bf16[4,3,192,128]{3,2,1,0:T(8,128)(2,1)} %get-tuple-element.219.refs_1_), channel_id=1, source_target_pairs={{0,3},{1,0},{2,1},{3,2},{4,7},{5,4},{6,5},{7,6},{8,11},{9,8},{10,9... | collective-permute-start | bytes 1769480 | tf_op jit(solution)/shard_map/ppermute | solution.py:593
  33.6 1.5 collective-permute-start.23
  35.1 10.9 %select.20 = (s32[40]{0:T(128)S(1)}, bf16[768,2048]{1,0:T(8,128)(2,1)}, bf16[4,768,1024]{2,1,0:T(8,128)(2,1)S(1)}, f32[768,1]{1,0:T(8,128)}) custom-call(s32[3]{0:T(128)S(1)} %pad_add_fusion.where, s32[16,128]{1,0:T(8,128)} %bitcast.44, s32[16,128]{1,0:T(8,128)} %bitcast.45, f32[1,2048]{1,0:T(1,128)} %bitcast.46, bf16[2048,2048]{1,0:T(8,128)(2,1)} %psi.1), custom_call_target="tpu_custom_call" | custom-call | flops 5000000000 | bytes 16777216 | tf_op jit(solution)/shard_map/select/pallas_call | solution.py:149
  46.0 7.4 %products.7 = f32[1,768,1024]{2,1,0:T(8,128)} custom-call(s32[3]{0:T(128)S(1)} %pad_add_fusion.where, s32[1]{0:T(128)S(6)} %copy.22.count, bf16[8,4,192,192]{3,2,1,0:T(8,128)(2,1)} %left.2, bf16[4,768,1024]{2,1,0:T(8,128)(2,1)S(1)} %get-tuple-element.218.psi, bf16[4,3,192,128]{3,2,1,0:T(8,128)(2,1)} %get-tuple-element.216.refs_0_, ...), custom_call_target="tpu_custom_call" | custom-call | flops 2818572288 | bytes 8388608 | tf_op jit(solution)/shard_map/products/pallas_call | solution.py:283
  56.1 1.1 collective-permute-done.19
  57.2 30.1 %conditional.1 = ((bf16[384,2048]{1,0:T(8,128)(2,1)}, bf16[384,2048]{1,0:T(8,128)(2,1)}, f32[2,8,128]{2,1,0:T(8,128)S(1)})) conditional(s32[]{:T(128)} %clamp.3, (s32[3]{0:T(128)S(1)}, s32[1]{0:T(128)}, bf16[8,4,192,192]{3,2,1,0:T(8,128)(2,1)}, bf16[4,768,1024]{2,1,0:T(8,128)(2,1)}, bf16[4,3,192,128]{3,2,1,0:T(8,128)(2,1)}, ...), branch_computations={%region_0.0_spmd, %region_1.2_spmd, %region_2.3_spmd} | conditional | flops 13638914048 | bytes 82313472 | solution.py:676
  57.2 2.7 %collective-permute-start.1 = (bf16[4,3,192,128]{3,2,1,0:T(8,128)(2,1)}, bf16[4,3,192,128]{3,2,1,0:T(8,128)(2,1)S(1)}, u32[]{:S(2)}, u32[]{:S(2)}) collective-permute-start(bf16[4,3,192,128]{3,2,1,0:T(8,128)(2,1)} %get-tuple-element.144.refs_1_), channel_id=1, source_target_pairs={{0,3},{1,0},{2,1},{3,2},{4,7},{5,4},{6,5},{7,6},{8,11},{9,8},{10,9... | collective-permute-start | bytes 1769480 | tf_op jit(solution)/shard_map/cond/branch_0_fun/ppermute | solution.py:593
  59.9 9.9 %products.4.near = f32[2,768,1024]{2,1,0:T(8,128)} custom-call(s32[3]{0:T(128)S(1)} %get-tuple-element.137.where, s32[1]{0:T(128)} %get-tuple-element.138.count, bf16[8,4,192,192]{3,2,1,0:T(8,128)(2,1)} %get-tuple-element.141.left, bf16[4,768,1024]{2,1,0:T(8,128)(2,1)} %get-tuple-element.142.psi, bf16[4,3,192,128]{3,2,1,0:T(8,128)(2,1)} %get-tuple-element.143.refs_0_, ...), custom_call_target="tpu_custom_call" | custom-call | flops 5637144576 | bytes 8388608 | tf_op jit(solution)/shard_map/cond/branch_0_fun/products/pallas_call | solution.py:283
  71.0 15.7 %finish.3 = (bf16[384,2048]{1,0:T(8,128)(2,1)}, bf16[384,2048]{1,0:T(8,128)(2,1)}, f32[2,8,128]{2,1,0:T(8,128)S(1)}) custom-call(s32[3]{0:T(128)S(1)} %get-tuple-element.137.where, s32[1]{0:T(128)} %get-tuple-element.138.count, s32[40]{0:T(128)S(1)} %get-tuple-element.139.table, f32[1,768,1024]{2,1,0:T(8,128)} %get-tuple-element.140.own, ...), custom_call_target="tpu_custom_call" | custom-call | flops 8000000000 | bytes 31457280 | tf_op jit(solution)/shard_map/cond/branch_0_fun/finish/pallas_call | solution.py:546
  87.2 15.5 %collective-permute-start.24 = (bf16[384,2048]{1,0:T(8,128)(2,1)}, bf16[384,2048]{1,0:T(8,128)(2,1)S(1)}, u32[]{:S(2)}, u32[]{:S(2)}) collective-permute-start(bf16[384,2048]{1,0:T(8,128)(2,1)} %get-tuple-element.246), channel_id=1, source_target_pairs={{0,4},{4,0},{1,5},{5,1},{2,6},{6,2},{3,7},{7,3},{8,12},{12,8},{9,1... | collective-permute-start | bytes 4718600 | tf_op jit(solution)/shard_map/ppermute | solution.py:678
  103.9 2.9 %collective-permute-start.26 = (f32[8,2]{1,0:T(8,128)S(1)}, f32[8,2]{1,0:T(8,128)S(1)}, u32[]{:S(2)}, u32[]{:S(2)}) collective-permute-start(f32[8,2]{1,0:T(8,128)S(1)} %broadcast_in_dim.65), channel_id=1, source_target_pairs={{0,2},{1,3},{2,0},{3,1},{4,6},{5,7},{6,4},{7,5},{8,10},{9,11},{10,... | collective-permute-start | bytes 200 | tf_op jit(solution)/shard_map/ppermute | solution.py:593
  106.8 1.1 collective-permute-done.26
  107.9 1.4 collective-permute-done.27
  109.3 2.0 %fusion = bf16[384,2048]{1,0:T(8,128)(2,1)S(1)} fusion(bf16[384,2048]{1,0:T(8,128)(2,1)} %get-tuple-element.245, bf16[384,2048]{1,0:T(8,128)(2,1)S(1)} %collective-permute-done.24), kind=kLoop, calls=%fused_computation.8 | loop fusion | flops 3145728 | bytes 4718592 | tf_op jit(solution)/shard_map/convert_element_type | solution.py:680
  111.7 24.9 %all_to_all.10 = bf16[16,24,2176]{2,1,0:T(8,128)(2,1)S(1)} all-to-all(bf16[16,24,2176]{2,1,0:T(8,128)(2,1)S(1)} %bitcast.38), channel_id=1, replica_groups=mesh['z'=4,'y'=4,'core'=2,'site'=4] {'z','y'}, dimensions={0} | all-to-all | bytes 3342336 | tf_op jit(solution)/shard_map/all_to_all | solution.py:691
  137.0 22.6 %all_to_all.11 = bf16[16,24,2048]{2,1,0:T(8,128)(2,1)S(1)} all-to-all(bf16[16,24,2048]{2,1,0:T(8,128)(2,1)S(1)} %broadcast_in_dim.71), channel_id=1, replica_groups=mesh['z'=4,'y'=4,'core'=2,'site'=4] {'z','y'}, dimensions={0} | all-to-all | bytes 3145728 | tf_op jit(solution)/shard_map/all_to_all | solution.py:694
  159.6 4.1 %collective-permute-start.28 = (bf16[2,192,2048]{2,1,0:T(8,128)(2,1)S(1)}, bf16[2,192,2048]{2,1,0:T(8,128)(2,1)S(1)}, u32[]{:S(2)}, u32[]{:S(2)}) collective-permute-start(bf16[2,192,2048]{2,1,0:T(8,128)(2,1)S(1)} %bitcast.39), channel_id=1, source_target_pairs={{0,4},{4,0},{1,5},{5,1},{2,6},{6,2},{3,7},{7,3},{8,12},{12,8},{9,1... | collective-permute-start | bytes 4718600 | tf_op jit(solution)/shard_map/ppermute | solution.py:699
  163.8 2.9 %collective-permute-done.29 = f32[8,2]{1,0:T(8,128)S(1)} collective-permute-done((f32[8,2]{1,0:T(8,128)S(1)}, f32[8,2]{1,0:T(8,128)S(1)}, u32[]{:S(2)}, u32[]{:S(2)}) %collective-permute-start.29) | collective-permute-done | bytes 96 | tf_op jit(solution)/shard_map/ppermute | solution.py:701
  167.3 2.6 %place.2.rest_0_ = bf16[4,192,2048]{2,1,0:T(8,128)(2,1)} custom-call(s32[3]{0:T(128)S(1)} %pad_add_fusion.where, bf16[2,192,2048]{2,1,0:T(8,128)(2,1)} %bitcast.40), custom_call_target="tpu_custom_call" | custom-call | flops 1000000000 | bytes 4194304 | tf_op jit(solution)/shard_map/place/pallas_call | solution.py:578
  169.9 1.2 copy-done.5
  171.1 2.6 %place.3 = bf16[4,192,2048]{2,1,0:T(8,128)(2,1)} custom-call(s32[3]{0:T(128)S(1)} %pad_add_fusion.where, bf16[2,192,2048]{2,1,0:T(8,128)(2,1)} %copy-done.5, bf16[4,192,2048]{2,1,0:T(8,128)(2,1)} %place.2.rest_0_), custom_call_target="tpu_custom_call", output_to_operand_aliasing={{}: (2, {})} | custom-call | flops 1000000000 | bytes 4194304 | tf_op jit(solution)/shard_map/place/pallas_call | solution.py:578
  (53 shorter events, 4.1 us)
Async XLA Ops:
  0.6 2.5 %copy-start.2 = (bf16[8,4,192,192]{3,2,1,0:T(8,128)(2,1)S(1)}, bf16[8,4,192,192]{3,2,1,0:T(8,128)(2,1)}, u32[]{:S(2)}) copy-start(bf16[8,4,192,192]{3,2,1,0:T(8,128)(2,1)} %left.2) | copy-start | bytes 7077892
  7.0 23.9 %collective-permute-start.20 = (bf16[12,192,128]{2,1,0:T(8,128)(2,1)}, bf16[12,192,128]{2,1,0:T(8,128)(2,1)S(1)}, u32[]{:S(2)}, u32[]{:S(2)}) collective-permute-start(bf16[12,192,128]{2,1,0:T(8,128)(2,1)} %get-tuple-element.225), channel_id=1, source_target_pairs={{0,8},{8,16},{16,24},{24,0},{1,9},{9,17},{17,25},{25,1},{2,10},{10... | collective-permute-start | bytes 1769480 | tf_op jit(solution)/shard_map/ppermute | solution.py:593
  9.1 24.5 %collective-permute-start.21 = (bf16[12,192,128]{2,1,0:T(8,128)(2,1)}, bf16[12,192,128]{2,1,0:T(8,128)(2,1)S(1)}, u32[]{:S(2)}, u32[]{:S(2)}) collective-permute-start(bf16[12,192,128]{2,1,0:T(8,128)(2,1)} %get-tuple-element.226), channel_id=1, source_target_pairs={{0,24},{8,0},{16,8},{24,16},{1,25},{9,1},{17,9},{25,17},{2,26},{10... | collective-permute-start | bytes 1769480 | tf_op jit(solution)/shard_map/ppermute | solution.py:593
  10.6 23.0 %collective-permute-start.22 = (bf16[12,192,128]{2,1,0:T(8,128)(2,1)}, bf16[12,192,128]{2,1,0:T(8,128)(2,1)S(1)}, u32[]{:S(2)}, u32[]{:S(2)}) collective-permute-start(bf16[12,192,128]{2,1,0:T(8,128)(2,1)} %get-tuple-element.227), channel_id=1, source_target_pairs={{0,32},{32,64},{64,96},{96,0},{1,33},{33,65},{65,97},{97,1},{2,34}... | collective-permute-start | bytes 1769480 | tf_op jit(solution)/shard_map/ppermute | solution.py:593
  12.2 11.5 %collective-permute-start.12 = (s32[1]{0:T(128)}, s32[1]{0:T(128)}, u32[]{:S(2)}, u32[]{:S(2)}) collective-permute-start(s32[1]{0:T(128)} %param.17), channel_id=1, source_target_pairs={{0,8},{8,16},{16,24},{24,0},{1,9},{9,17},{17,25},{25,1},{2,10},{10... | collective-permute-start | bytes 20 | tf_op jit(solution)/shard_map/ppermute | solution.py:593
  12.2 13.0 %collective-permute-start.13 = (s32[1]{0:T(128)}, s32[1]{0:T(128)}, u32[]{:S(2)}, u32[]{:S(2)}) collective-permute-start(s32[1]{0:T(128)} %param.17), channel_id=1, source_target_pairs={{0,24},{8,0},{16,8},{24,16},{1,25},{9,1},{17,9},{25,17},{2,26},{10... | collective-permute-start | bytes 20 | tf_op jit(solution)/shard_map/ppermute | solution.py:593
  23.7 4.7 %collective-permute-start.14 = (s32[1]{0:T(128)}, s32[1]{0:T(128)}, u32[]{:S(2)}, u32[]{:S(2)}) collective-permute-start(s32[1]{0:T(128)} %param.17), channel_id=1, source_target_pairs={{0,32},{32,64},{64,96},{96,0},{1,33},{33,65},{65,97},{97,1},{2,34}... | collective-permute-start | bytes 20 | tf_op jit(solution)/shard_map/ppermute | solution.py:593
  25.2 5.7 %collective-permute-start.15 = (s32[1]{0:T(128)}, s32[1]{0:T(128)}, u32[]{:S(2)}, u32[]{:S(2)}) collective-permute-start(s32[1]{0:T(128)} %param.17), channel_id=1, source_target_pairs={{0,96},{32,0},{64,32},{96,64},{1,97},{33,1},{65,33},{97,65},{2,98}... | collective-permute-start | bytes 20 | tf_op jit(solution)/shard_map/ppermute | solution.py:593
  28.4 27.7 %collective-permute-start.16 = (bf16[4,3,192,128]{3,2,1,0:T(8,128)(2,1)}, bf16[4,3,192,128]{3,2,1,0:T(8,128)(2,1)}, u32[]{:S(2)}, u32[]{:S(2)}) collective-permute-start(bf16[4,3,192,128]{3,2,1,0:T(8,128)(2,1)} %get-tuple-element.216.refs_0_), channel_id=1, source_target_pairs={{0,3},{1,0},{2,1},{3,2},{4,7},{5,4},{6,5},{7,6},{8,11},{9,8},{10,9... | collective-permute-start | bytes 1769480 | tf_op jit(solution)/shard_map/ppermute | solution.py:593
  30.9 25.2 %collective-permute-start.18 = (bf16[4,3,192,128]{3,2,1,0:T(8,128)(2,1)}, bf16[4,3,192,128]{3,2,1,0:T(8,128)(2,1)}, u32[]{:S(2)}, u32[]{:S(2)}) collective-permute-start(bf16[4,3,192,128]{3,2,1,0:T(8,128)(2,1)} %get-tuple-element.216.refs_0_), channel_id=1, source_target_pairs={{0,1},{1,2},{2,3},{3,0},{4,5},{5,6},{6,7},{7,4},{8,9},{9,10},{10,1... | collective-permute-start | bytes 1769480 | tf_op jit(solution)/shard_map/ppermute | solution.py:593
  30.9 25.2 %collective-permute-start.17 = (bf16[4,3,192,128]{3,2,1,0:T(8,128)(2,1)}, bf16[4,3,192,128]{3,2,1,0:T(8,128)(2,1)}, u32[]{:S(2)}, u32[]{:S(2)}) collective-permute-start(bf16[4,3,192,128]{3,2,1,0:T(8,128)(2,1)} %get-tuple-element.219.refs_1_), channel_id=1, source_target_pairs={{0,3},{1,0},{2,1},{3,2},{4,7},{5,4},{6,5},{7,6},{8,11},{9,8},{10,9... | collective-permute-start | bytes 1769480 | tf_op jit(solution)/shard_map/ppermute | solution.py:593
  33.6 23.6 %collective-permute-start.19 = (bf16[4,3,192,128]{3,2,1,0:T(8,128)(2,1)}, bf16[4,3,192,128]{3,2,1,0:T(8,128)(2,1)}, u32[]{:S(2)}, u32[]{:S(2)}) collective-permute-start(bf16[4,3,192,128]{3,2,1,0:T(8,128)(2,1)} %get-tuple-element.219.refs_1_), channel_id=1, source_target_pairs={{0,1},{1,2},{2,3},{3,0},{4,5},{5,6},{6,7},{7,4},{8,9},{9,10},{10,1... | collective-permute-start | bytes 1769480 | tf_op jit(solution)/shard_map/ppermute | solution.py:593
  33.6 22.5 %collective-permute-start.23 = (bf16[12,192,128]{2,1,0:T(8,128)(2,1)}, bf16[12,192,128]{2,1,0:T(8,128)(2,1)}, u32[]{:S(2)}, u32[]{:S(2)}) collective-permute-start(bf16[12,192,128]{2,1,0:T(8,128)(2,1)} %get-tuple-element.228), channel_id=1, source_target_pairs={{0,96},{32,0},{64,32},{96,64},{1,97},{33,1},{65,33},{97,65},{2,98}... | collective-permute-start | bytes 1769480 | tf_op jit(solution)/shard_map/ppermute | solution.py:593
  46.0 7.5 %copy-start = (bf16[4,768,1024]{2,1,0:T(8,128)(2,1)}, bf16[4,768,1024]{2,1,0:T(8,128)(2,1)S(1)}, u32[]{:S(2)}) copy-start(bf16[4,768,1024]{2,1,0:T(8,128)(2,1)S(1)} %get-tuple-element.218.psi) | copy-start | bytes 18874372
  46.0 11.2 %copy-start.8 = (f32[2048]{0:T(1024)S(1)}, f32[2048]{0:T(1024)}, u32[]{:S(2)}) copy-start(f32[2048]{0:T(1024)} %param.19) | copy-start | bytes 24580
  57.2 12.8 %collective-permute-start = (bf16[4,3,192,128]{3,2,1,0:T(8,128)(2,1)}, bf16[4,3,192,128]{3,2,1,0:T(8,128)(2,1)S(1)}, u32[]{:S(2)}, u32[]{:S(2)}) collective-permute-start(bf16[4,3,192,128]{3,2,1,0:T(8,128)(2,1)} %get-tuple-element.145.refs_2_), channel_id=1, source_target_pairs={{0,1},{1,2},{2,3},{3,0},{4,5},{5,6},{6,7},{7,4},{8,9},{9,10},{10,1... | collective-permute-start | bytes 1769480 | tf_op jit(solution)/shard_map/cond/branch_0_fun/ppermute | solution.py:593
  57.2 12.8 %collective-permute-start.1 = (bf16[4,3,192,128]{3,2,1,0:T(8,128)(2,1)}, bf16[4,3,192,128]{3,2,1,0:T(8,128)(2,1)S(1)}, u32[]{:S(2)}, u32[]{:S(2)}) collective-permute-start(bf16[4,3,192,128]{3,2,1,0:T(8,128)(2,1)} %get-tuple-element.144.refs_1_), channel_id=1, source_target_pairs={{0,3},{1,0},{2,1},{3,2},{4,7},{5,4},{6,5},{7,6},{8,11},{9,8},{10,9... | collective-permute-start | bytes 1769480 | tf_op jit(solution)/shard_map/cond/branch_0_fun/ppermute | solution.py:593
  59.9 11.1 %copy-start.1 = (bf16[4,768,1024]{2,1,0:T(8,128)(2,1)S(1)}, bf16[4,768,1024]{2,1,0:T(8,128)(2,1)}, u32[]{:S(2)}) copy-start(bf16[4,768,1024]{2,1,0:T(8,128)(2,1)} %get-tuple-element.142.psi) | copy-start | bytes 18874372 | tf_op jit(solution)/shard_map/cond
  59.9 11.1 %copy-start.4 = (f32[768,1]{1,0:T(8,128)S(1)}, f32[768,1]{1,0:T(8,128)}, u32[]{:S(2)}) copy-start(f32[768,1]{1,0:T(8,128)} %get-tuple-element.149.refs_2_) | copy-start | bytes 9220 | tf_op jit(solution)/shard_map/cond
  70.0 0.8 copy-start.6
  70.0 1.0 copy-start.7
  87.2 22.1 %collective-permute-start.24 = (bf16[384,2048]{1,0:T(8,128)(2,1)}, bf16[384,2048]{1,0:T(8,128)(2,1)S(1)}, u32[]{:S(2)}, u32[]{:S(2)}) collective-permute-start(bf16[384,2048]{1,0:T(8,128)(2,1)} %get-tuple-element.246), channel_id=1, source_target_pairs={{0,4},{4,0},{1,5},{5,1},{2,6},{6,2},{3,7},{7,3},{8,12},{12,8},{9,1... | collective-permute-start | bytes 4718600 | tf_op jit(solution)/shard_map/ppermute | solution.py:678
  102.9 3.9 %collective-permute-start.25 = (f32[8,2]{1,0:T(8,128)S(1)}, f32[8,2]{1,0:T(8,128)S(1)}, u32[]{:S(2)}, u32[]{:S(2)}) collective-permute-start(f32[8,2]{1,0:T(8,128)S(1)} %broadcast_in_dim.65), channel_id=1, source_target_pairs={{0,1},{1,2},{2,3},{3,0},{4,5},{5,6},{6,7},{7,4},{8,9},{9,10},{10,1... | collective-permute-start | bytes 200 | tf_op jit(solution)/shard_map/ppermute | solution.py:593
  103.9 4.0 %collective-permute-start.26 = (f32[8,2]{1,0:T(8,128)S(1)}, f32[8,2]{1,0:T(8,128)S(1)}, u32[]{:S(2)}, u32[]{:S(2)}) collective-permute-start(f32[8,2]{1,0:T(8,128)S(1)} %broadcast_in_dim.65), channel_id=1, source_target_pairs={{0,2},{1,3},{2,0},{3,1},{4,6},{5,7},{6,4},{7,5},{8,10},{9,11},{10,... | collective-permute-start | bytes 200 | tf_op jit(solution)/shard_map/ppermute | solution.py:593
  106.8 2.5 %collective-permute-start.27 = (f32[8,2]{1,0:T(8,128)S(1)}, f32[8,2]{1,0:T(8,128)S(1)}, u32[]{:S(2)}, u32[]{:S(2)}) collective-permute-start(f32[8,2]{1,0:T(8,128)S(1)} %broadcast_in_dim.65), channel_id=1, source_target_pairs={{0,3},{1,0},{2,1},{3,2},{4,7},{5,4},{6,5},{7,6},{8,11},{9,8},{10,9... | collective-permute-start | bytes 200 | tf_op jit(solution)/shard_map/ppermute | solution.py:593
  159.6 7.7 %copy-start.3 = (bf16[16,24,2048]{2,1,0:T(8,128)(2,1)}, bf16[16,24,2048]{2,1,0:T(8,128)(2,1)S(1)}, u32[]{:S(2)}) copy-start(bf16[16,24,2048]{2,1,0:T(8,128)(2,1)S(1)} %all_to_all.11) | copy-start | bytes 4718596
  159.6 10.3 %collective-permute-start.28 = (bf16[2,192,2048]{2,1,0:T(8,128)(2,1)S(1)}, bf16[2,192,2048]{2,1,0:T(8,128)(2,1)S(1)}, u32[]{:S(2)}, u32[]{:S(2)}) collective-permute-start(bf16[2,192,2048]{2,1,0:T(8,128)(2,1)S(1)} %bitcast.39), channel_id=1, source_target_pairs={{0,4},{4,0},{1,5},{5,1},{2,6},{6,2},{3,7},{7,3},{8,12},{12,8},{9,1... | collective-permute-start | bytes 4718600 | tf_op jit(solution)/shard_map/ppermute | solution.py:699
  163.8 3.0 %collective-permute-start.29 = (f32[8,2]{1,0:T(8,128)S(1)}, f32[8,2]{1,0:T(8,128)S(1)}, u32[]{:S(2)}, u32[]{:S(2)}) collective-permute-start(f32[8,2]{1,0:T(8,128)S(1)} %slice_add_fusion), channel_id=1, source_target_pairs={{0,4},{4,0},{1,5},{5,1},{2,6},{6,2},{3,7},{7,3},{8,12},{12,8},{9,1... | collective-permute-start | bytes 200 | tf_op jit(solution)/shard_map/ppermute | solution.py:701
  169.9 1.2 copy-start.5
where the time goes:
time: 175 us; the launch traced here: 174 us
  Pallas kernels  55.4 us (32%)
  blocking collectives  47.5 us (27%)
  starting transfers between devices  44.4 us (25%)
  waiting for transfers between devices  15.8 us (9%)
  between operations  4.32 us (2%)
  other arithmetic  2.99 us (2%)
  local copies, waits for them, and re-layouts  2.92 us (2%)
    all_to_all x1, blocking collectives, local(): lax.all_to_all(both.reshape(plane, share, bond + EXTRA), ('z', 'y'), 0, 0...  24.9 us
    ppermute x17, starting transfers between devices, shifted(): lax.ppermute(value, axis, [(i, (i + by) % size) for i in range(size)])  24.8 us
    all_to_all x1, blocking collectives, local(): lax.all_to_all(jnp.broadcast_to(summed[None], (plane, share, bond)), ('z'...  22.6 us
    pallas_call x2, Pallas kernels, products(): pl.pallas_call(functools.partial(products_body, tuple(rels)), in_specs=[s...  17.3 us
    pallas_call x1, Pallas kernels, finish(): pl.pallas_call(functools.partial(finish_body, slots), in_specs=[smem] * 3...  15.7 us
    ppermute x1, starting transfers between devices, local(): away = lax.ppermute(send, 'core', swap)  15.5 us
    ppermute x17, waiting for transfers between devices, shifted(): lax.ppermute(value, axis, [(i, (i + by) % size) for i in range(size)])  12.9 us
    pallas_call x1, Pallas kernels, select(): pl.pallas_call(select_body, grid=(4,), in_specs=[smem, ids, ids, pl.Block...  10.9 us
  transfers between devices with their start and end apart: 20, of which 7 were waited for; matrix products, arithmetic and copies ran while one was open for 1% of the time, Pallas kernels for 18%

commit v1 on v0

--- a/solution.py
+++ b/solution.py
@@ -125,21 +125,18 @@
 
     row = lax.broadcasted_iota(jnp.int32, (WIN_COLS, SLOT_COLS), 0)
     lane = lax.broadcasted_iota(jnp.int32, (WIN_COLS, SLOT_COLS), 1)
-
-    def two_sectors(half, carry):
-        for odd in range(2):
-            start = table[RIGHT_START + 4 * group + 2 * half + odd]
-            size = table[RIGHT_SIZE + 4 * group + 2 * half + odd]
-            base = pl.multiple_of(jnp.minimum((start // 128) * 128, rows.shape[1] - WIN_COLS), 128)
-            at = jnp.where(lane < 128, lane, jnp.where(lane < 192, size, lane - 64)) if odd else lane
-            kept = (row == at + (start - base)) & (at < size)
-            pick = jnp.where(kept, 1.0, 0.0).astype(jnp.bfloat16)
-            got = jnp.dot(rows[:, pl.ds(base, WIN_COLS)], pick, preferred_element_type=jnp.float32)
-            where_to = pl.multiple_of(SLOT_COLS * (2 * half + odd), SLOT_COLS)
-            cols[0, :, pl.ds(where_to, SLOT_COLS)] = got.astype(jnp.bfloat16)
-        return carry
-
-    lax.fori_loop(0, 2, two_sectors, 0)
+    for q in range(4):
+        start = table[RIGHT_START + 4 * group + q]
+        size = table[RIGHT_SIZE + 4 * group + q]
+        base = pl.multiple_of(jnp.minimum((start // 128) * 128, rows.shape[1] - WIN_COLS), 128)
+        if q % 2:
+            at = jnp.where(lane < 128, lane, jnp.where(lane < 192, size, lane - 64))
+        else:
+            at = lane
+        kept = (row == at + (start - base)) & (at < size)
+        pick = jnp.where(kept, 1.0, 0.0).astype(jnp.bfloat16)
+        got = jnp.dot(rows[:, pl.ds(base, WIN_COLS)], pick, preferred_element_type=jnp.float32)
+        cols[0, :, q * SLOT_COLS : (q + 1) * SLOT_COLS] = got.astype(jnp.bfloat16)
 
 
 def select(where, left_sector, right_sector, left_energy, psi):
@@ -636,12 +633,14 @@
     table, rows, psi, energies = select(where, left_sector, right_sector, left_energy, wavefunction)
     own = products((0,), where, term_count, left_blocks, psi, [mine_early])
 
-    def rest(slots, going, prev, following):
-        far = (shifted(prev[0], "site", 1), shifted(following[1], "site", -1))
-        arrived = []
-        if slots:
-            arrived = [*counts, *extras] + [shifted(going, "site", by) for by in (-1, 2, 1)]
-        near = products((1, 3), where, term_count, left_blocks, psi, [following, prev])
+    far = (shifted(prev[0], "site", 1), shifted(following[1], "site", -1))
+    going = extras[3][6:12]
+    for k in (2, 1, 0):
+        going = jnp.where(there[k], extras[k][6:12], going)
+    moved = [shifted(going[None], "site", by) for by in (-1, 2, 1)]
+    near = products((1, 3), where, term_count, left_blocks, psi, [following, prev])
+
+    def rest(slots, late):
         return tuple(
             finish(
                 slots,
@@ -657,23 +656,21 @@
                 subspace,
                 energies,
                 right_energy[None, :],
-                late=arrived,
+                late=late,
             )
         )
 
-    def none(*moved):
-        return rest(0, None, *moved)
-
-    def one(*moved):
-        going = extras[3][6:12]
-        for k in (2, 1, 0):
-            going = jnp.where(there[k], extras[k][6:12], going)
-        return rest(1, going[None], *moved)
-
-    def many(*moved):
-        return rest(4, jnp.stack([one[6:12] for one in extras]), *moved)
-
-    send, mine, proj = lax.switch(jnp.minimum(number, 2), [none, one, many], prev, following)
+    def none():
+        return rest(0, [])
+
+    def one():
+        return rest(1, [*counts, *extras, *moved])
+
+    def many():
+        every = jnp.stack([one[6:12] for one in extras])
+        return rest(4, [*counts, *extras] + [shifted(every, "site", by) for by in (-1, 2, 1)])
+
+    send, mine, proj = lax.switch(jnp.minimum(number, 2), [none, one, many])
     swap = [(0, 1), (1, 0)]
     away = lax.ppermute(send, "core", swap)
     proj = small_sum(jnp.broadcast_to(jnp.sum(proj, axis=(1, 2))[None, :], (8, 2)), "site")[0]
@@ -698,7 +695,8 @@
     gathered = gathered.reshape(2, 192, bond)
     other = lax.ppermute(gathered, "core", swap)
     placed = place(0, where, gathered)
-    projections = whole + lax.ppermute(whole, "core", swap)
+    whole_beside = lax.ppermute(whole, "core", swap)
+    projections = whole + whole_beside
     sigma = place(1, where, other, placed)
     return sigma, projections[0]
 

time: 175 us -> 186 us (1.063)
  waiting for transfers between devices: 15.8 us -> 27.8 us
  Pallas kernels: 55.4 us -> 51.5 us
  other arithmetic: 2.99 us -> 4.88 us
    ppermute x17 -> x20, waiting for transfers between devices: 12.9 us -> 24.9 us  [shifted(): lax.ppermute(value, axis, [(i, (i + by) % size) for i in range(size)])]
    ppermute x17 -> x20, starting transfers between devices: 24.8 us -> 27.4 us  [shifted(): lax.ppermute(value, axis, [(i, (i + by) % size) for i in range(size)])]
    pallas_call x1, Pallas kernels: 10.9 us -> 8.66 us  [select(): pl.pallas_call(select_body, grid=(4,), in_specs=[smem, ids, ids, pl.Block...]
    pallas_call x2, Pallas kernels: 17.3 us -> 15.2 us  [products(): pl.pallas_call(functools.partial(products_body, tuple(rels)), in_specs=[s...]
    broadcast_in_dim x0 -> x1, other arithmetic: none -> 1.89 us  [local(): moved = [shifted(going[None], 'site', by) for by in (-1, 2, 1)]]
  transfers between devices with their start and end apart: 20 -> 23, of which waited for: 7 -> 10; matrix products, arithmetic and copies ran while one was open for 1% -> 2% of each run, Pallas kernels for 18% -> 16%
where the time goes in v1:
time: 186 us; the launch traced here: 185 us
  Pallas kernels  51.5 us (28%)
  blocking collectives  49 us (26%)
  starting transfers between devices  45.5 us (24%)
  waiting for transfers between devices  27.8 us (15%)
  other arithmetic  4.88 us (3%)
  between operations  4.15 us (2%)
  local copies, waits for them, and re-layouts  1.92 us (1%)
    ppermute x20, starting transfers between devices, shifted(): lax.ppermute(value, axis, [(i, (i + by) % size) for i in range(size)])  27.4 us
    all_to_all x1, blocking collectives, local(): lax.all_to_all(both.reshape(plane, share, bond + EXTRA), ('z', 'y'), 0, 0...  26.3 us
    ppermute x20, waiting for transfers between devices, shifted(): lax.ppermute(value, axis, [(i, (i + by) % size) for i in range(size)])  24.9 us
    all_to_all x1, blocking collectives, local(): lax.all_to_all(jnp.broadcast_to(summed[None], (plane, share, bond)), ('z'...  22.8 us
    pallas_call x1, Pallas kernels, finish(): pl.pallas_call(functools.partial(finish_body, slots), in_specs=[smem] * 3...  16.2 us
    pallas_call x2, Pallas kernels, products(): pl.pallas_call(functools.partial(products_body, tuple(rels)), in_specs=[s...  15.2 us
    ppermute x1, starting transfers between devices, local(): away = lax.ppermute(send, 'core', swap)  14.2 us
    pallas_call x1, Pallas kernels, select(): pl.pallas_call(select_body, grid=(4,), in_specs=[smem, ids, ids, pl.Block...  8.66 us
  transfers between devices with their start and end apart: 23, of which 10 were waited for; matrix products, arithmetic and copies ran while one was open for 2% of the time, Pallas kernels for 16%

profile of v1, /device:TPU:1, one launch (start us, length us, event | category | flops | bytes accessed | tf_op | source)
XLA Modules:
  0.0 185.1 jit_solution(5981897309419986360)
XLA Ops:
  0.6 2.5 %pack_early.1 = (bf16[4,3,192,128]{3,2,1,0:T(8,128)(2,1)}, bf16[4,3,192,128]{3,2,1,0:T(8,128)(2,1)}) custom-call(bf16[8,4,192,192]{3,2,1,0:T(8,128)(2,1)} %right), custom_call_target="tpu_custom_call" | custom-call | tf_op jit(solution)/shard_map/pack_early/pallas_call | solution.py:56
  3.1 2.0 %collective-permute-start.9 = (bf16[4,3,192,128]{3,2,1,0:T(8,128)(2,1)}, bf16[4,3,192,128]{3,2,1,0:T(8,128)(2,1)}, u32[]{:S(2)}, u32[]{:S(2)}) collective-permute-start(bf16[4,3,192,128]{3,2,1,0:T(8,128)(2,1)} %get-tuple-element.207.refs_0_), channel_id=1, source_target_pairs={{0,1},{1,2},{2,3},{3,0},{4,5},{5,6},{6,7},{7,4},{8,9},{9,10},{10,1... | collective-permute-start | bytes 1769480 | tf_op jit(solution)/shard_map/ppermute | solution.py:590
  6.4 3.9 %pack_late.1 = (bf16[12,192,128]{2,1,0:T(8,128)(2,1)}, bf16[12,192,128]{2,1,0:T(8,128)(2,1)}, bf16[12,192,128]{2,1,0:T(8,128)(2,1)}, bf16[12,192,128]{2,1,0:T(8,128)(2,1)}) custom-call(bf16[8,4,192,192]{3,2,1,0:T(8,128)(2,1)S(1)} %copy-done.1, bf16[8,4,192,192]{3,2,1,0:T(8,128)(2,1)} %right), custom_call_target="tpu_custom_call" | custom-call | flops 2000000000 | bytes 4194304 | tf_op jit(solution)/shard_map/pack_late/pallas_call | solution.py:68
  10.3 1.5 collective-permute-start.13
  14.4 11.4 %collective-permute-done.3 = s32[1]{0:T(128)} collective-permute-done((s32[1]{0:T(128)}, s32[1]{0:T(128)}, u32[]{:S(2)}, u32[]{:S(2)}) %collective-permute-start.3) | collective-permute-done | bytes 36 | tf_op jit(solution)/shard_map/ppermute | solution.py:590
  25.8 1.4 collective-permute-start.4
  27.2 1.6 collective-permute-done.4
  28.7 1.5 collective-permute-start.5
  30.3 3.2 %collective-permute-done.5 = s32[1]{0:T(128)} collective-permute-done((s32[1]{0:T(128)}, s32[1]{0:T(128)}, u32[]{:S(2)}, u32[]{:S(2)}) %collective-permute-start.5) | collective-permute-done | bytes 36 | tf_op jit(solution)/shard_map/ppermute | solution.py:590
  33.4 1.9 %collective-permute-start.6 = (s32[1]{0:T(128)}, s32[1]{0:T(128)}, u32[]{:S(2)}, u32[]{:S(2)}) collective-permute-start(s32[1]{0:T(128)} %param.17), channel_id=1, source_target_pairs={{0,96},{32,0},{64,32},{96,64},{1,97},{33,1},{65,33},{97,65},{2,98}... | collective-permute-start | bytes 20 | tf_op jit(solution)/shard_map/ppermute | solution.py:590
  36.2 2.4 %collective-permute-start.14 = (bf16[12,192,128]{2,1,0:T(8,128)(2,1)}, bf16[12,192,128]{2,1,0:T(8,128)(2,1)S(1)}, u32[]{:S(2)}, u32[]{:S(2)}) collective-permute-start(bf16[12,192,128]{2,1,0:T(8,128)(2,1)} %get-tuple-element.217), channel_id=1, source_target_pairs={{0,24},{8,0},{16,8},{24,16},{1,25},{9,1},{17,9},{25,17},{2,26},{10... | collective-permute-start | bytes 1769480 | tf_op jit(solution)/shard_map/ppermute | solution.py:590
  38.8 2.9 %collective-permute-start.16 = (bf16[12,192,128]{2,1,0:T(8,128)(2,1)}, bf16[12,192,128]{2,1,0:T(8,128)(2,1)}, u32[]{:S(2)}, u32[]{:S(2)}) collective-permute-start(bf16[12,192,128]{2,1,0:T(8,128)(2,1)} %get-tuple-element.219), channel_id=1, source_target_pairs={{0,96},{32,0},{64,32},{96,64},{1,97},{33,1},{65,33},{97,65},{2,98}... | collective-permute-start | bytes 1769480 | tf_op jit(solution)/shard_map/ppermute | solution.py:590
  41.7 8.7 %select.20 = (s32[40]{0:T(128)S(1)}, bf16[768,2048]{1,0:T(8,128)(2,1)}, bf16[4,768,1024]{2,1,0:T(8,128)(2,1)S(1)}, f32[768,1]{1,0:T(8,128)}) custom-call(s32[3]{0:T(128)S(1)} %pad_add_fusion.where, s32[16,128]{1,0:T(8,128)} %bitcast.42, s32[16,128]{1,0:T(8,128)} %bitcast.43, f32[1,2048]{1,0:T(1,128)} %bitcast.44, bf16[2048,2048]{1,0:T(8,128)(2,1)} %psi.1), custom_call_target="tpu_custom_call" | custom-call | flops 5000000000 | bytes 16777216 | tf_op jit(solution)/shard_map/select/pallas_call | solution.py:146
  51.1 6.7 %products.2 = f32[1,768,1024]{2,1,0:T(8,128)} custom-call(s32[3]{0:T(128)S(1)} %pad_add_fusion.where, s32[1]{0:T(128)S(6)} %copy.22.count, bf16[8,4,192,192]{3,2,1,0:T(8,128)(2,1)} %left.4, bf16[4,768,1024]{2,1,0:T(8,128)(2,1)S(1)} %get-tuple-element.210.psi, bf16[4,3,192,128]{3,2,1,0:T(8,128)(2,1)} %get-tuple-element.207.refs_0_, ...), custom_call_target="tpu_custom_call" | custom-call | flops 2818572288 | bytes 8388608 | tf_op jit(solution)/shard_map/products/pallas_call | solution.py:280
  61.7 1.5 collective-permute-start.12
  63.2 1.9 %fusion.3 = bf16[1,6,192,128]{3,2,1,0:T(8,128)(2,1)} fusion(bf16[12,192,128]{2,1,0:T(8,128)(2,1)} %collective-permute-done.16, bf16[12,192,128]{2,1,0:T(8,128)(2,1)S(1)} %collective-permute-done.15, bf16[12,192,128]{2,1,0:T(8,128)(2,1)S(1)} %collective-permute-done.14, bf16[12,192,128]{2,1,0:T(8,128)(2,1)S(1)} %collective-permute-done.13, pred[]{:T(512)} %bitcast.12, ...), kind=kLoop, calls=%fused_computation.12 | loop fusion | flops 442368 | bytes 1474563 | tf_op jit(solution)/shard_map/broadcast_in_dim | solution.py:640
  65.1 1.4 collective-permute-start.17
  67.4 8.4 %products.3 = f32[2,768,1024]{2,1,0:T(8,128)} custom-call(s32[3]{0:T(128)S(1)} %pad_add_fusion.where, s32[1]{0:T(128)S(6)} %copy.22.count, bf16[8,4,192,192]{3,2,1,0:T(8,128)(2,1)} %left.4, bf16[4,768,1024]{2,1,0:T(8,128)(2,1)} %copy-done, bf16[4,3,192,128]{3,2,1,0:T(8,128)(2,1)} %collective-permute-done.7.refs_0_, ...), custom_call_target="tpu_custom_call" | custom-call | flops 5637144576 | bytes 8388608 | tf_op jit(solution)/shard_map/products/pallas_call | solution.py:280
  78.2 3.3 %collective-permute-done.19 = bf16[1,6,192,128]{3,2,1,0:T(8,128)(2,1)} collective-permute-done((bf16[1,6,192,128]{3,2,1,0:T(8,128)(2,1)}, bf16[1,6,192,128]{3,2,1,0:T(8,128)(2,1)}, u32[]{:S(2)}, u32[]{:S(2)}) %collective-permute-start.19) | collective-permute-done | bytes 294944 | tf_op jit(solution)/shard_map/ppermute | solution.py:590
  81.6 16.4 %conditional.1 = ((bf16[384,2048]{1,0:T(8,128)(2,1)}, bf16[384,2048]{1,0:T(8,128)(2,1)}, f32[2,8,128]{2,1,0:T(8,128)S(1)})) conditional(s32[]{:T(128)} %clamp.3, (f32[2048]{0:T(1024)S(1)}, s32[3]{0:T(128)S(1)}, s32[1]{0:T(128)}, s32[40]{0:T(128)S(1)}, f32[1,768,1024]{2,1,0:T(8,128)}, /*index=5*/f32[2,768,1024]{2,1,0:T(8,128)}, ...), branch_computations={%region_0.1_spmd, %region_1.2_spmd, %region_2.3_spmd} | conditional | flops 8001769472 | bytes 50331776 | solution.py:673
  81.6 16.2 %finish.3 = (bf16[384,2048]{1,0:T(8,128)(2,1)}, bf16[384,2048]{1,0:T(8,128)(2,1)}, f32[2,8,128]{2,1,0:T(8,128)S(1)}) custom-call(s32[3]{0:T(128)S(1)} %get-tuple-element.131.where, s32[1]{0:T(128)} %get-tuple-element.132.count, s32[40]{0:T(128)S(1)} %get-tuple-element.133.table, f32[1,768,1024]{2,1,0:T(8,128)} %get-tuple-element.134.own, ...), custom_call_target="tpu_custom_call" | custom-call | flops 8000000000 | bytes 31457280 | tf_op jit(solution)/shard_map/cond/branch_0_fun/finish/pallas_call | solution.py:543
  98.0 14.2 %collective-permute-start.20 = (bf16[384,2048]{1,0:T(8,128)(2,1)}, bf16[384,2048]{1,0:T(8,128)(2,1)S(1)}, u32[]{:S(2)}, u32[]{:S(2)}) collective-permute-start(bf16[384,2048]{1,0:T(8,128)(2,1)} %get-tuple-element.237), channel_id=1, source_target_pairs={{0,4},{4,0},{1,5},{5,1},{2,6},{6,2},{3,7},{7,3},{8,12},{12,8},{9,1... | collective-permute-start | bytes 4718600 | tf_op jit(solution)/shard_map/ppermute | solution.py:675
  112.2 2.1 %collective-permute-start.21 = (f32[8,2]{1,0:T(8,128)S(1)}, f32[8,2]{1,0:T(8,128)S(1)}, u32[]{:S(2)}, u32[]{:S(2)}) collective-permute-start(f32[8,2]{1,0:T(8,128)S(1)} %broadcast_in_dim.68), channel_id=1, source_target_pairs={{0,1},{1,2},{2,3},{3,0},{4,5},{5,6},{6,7},{7,4},{8,9},{9,10},{10,1... | collective-permute-start | bytes 200 | tf_op jit(solution)/shard_map/ppermute | solution.py:590
  114.3 1.9 %collective-permute-start.22 = (f32[8,2]{1,0:T(8,128)S(1)}, f32[8,2]{1,0:T(8,128)S(1)}, u32[]{:S(2)}, u32[]{:S(2)}) collective-permute-start(f32[8,2]{1,0:T(8,128)S(1)} %broadcast_in_dim.68), channel_id=1, source_target_pairs={{0,2},{1,3},{2,0},{3,1},{4,6},{5,7},{6,4},{7,5},{8,10},{9,11},{10,... | collective-permute-start | bytes 200 | tf_op jit(solution)/shard_map/ppermute | solution.py:590
  116.8 1.5 collective-permute-done.22
  119.1 2.0 %fusion = bf16[384,2048]{1,0:T(8,128)(2,1)S(1)} fusion(bf16[384,2048]{1,0:T(8,128)(2,1)} %get-tuple-element.236, bf16[384,2048]{1,0:T(8,128)(2,1)S(1)} %collective-permute-done.20), kind=kLoop, calls=%fused_computation.7 | loop fusion | flops 3145728 | bytes 4718592 | tf_op jit(solution)/shard_map/convert_element_type | solution.py:677
  121.4 26.3 %all_to_all.10 = bf16[16,24,2176]{2,1,0:T(8,128)(2,1)S(1)} all-to-all(bf16[16,24,2176]{2,1,0:T(8,128)(2,1)S(1)} %bitcast.36), channel_id=1, replica_groups=mesh['z'=4,'y'=4,'core'=2,'site'=4] {'z','y'}, dimensions={0} | all-to-all | bytes 3342336 | tf_op jit(solution)/shard_map/all_to_all | solution.py:688
  148.2 22.8 %all_to_all.11 = bf16[16,24,2048]{2,1,0:T(8,128)(2,1)S(1)} all-to-all(bf16[16,24,2048]{2,1,0:T(8,128)(2,1)S(1)} %broadcast_in_dim.74), channel_id=1, replica_groups=mesh['z'=4,'y'=4,'core'=2,'site'=4] {'z','y'}, dimensions={0} | all-to-all | bytes 3145728 | tf_op jit(solution)/shard_map/all_to_all | solution.py:691
  170.9 4.0 %collective-permute-start.24 = (bf16[2,192,2048]{2,1,0:T(8,128)(2,1)S(1)}, bf16[2,192,2048]{2,1,0:T(8,128)(2,1)S(1)}, u32[]{:S(2)}, u32[]{:S(2)}) collective-permute-start(bf16[2,192,2048]{2,1,0:T(8,128)(2,1)S(1)} %bitcast.37), channel_id=1, source_target_pairs={{0,4},{4,0},{1,5},{5,1},{2,6},{6,2},{3,7},{7,3},{8,12},{12,8},{9,1... | collective-permute-start | bytes 4718600 | tf_op jit(solution)/shard_map/ppermute | solution.py:696
  175.0 2.9 %collective-permute-done.25 = f32[8,2]{1,0:T(8,128)S(1)} collective-permute-done((f32[8,2]{1,0:T(8,128)S(1)}, f32[8,2]{1,0:T(8,128)S(1)}, u32[]{:S(2)}, u32[]{:S(2)}) %collective-permute-start.25) | collective-permute-done | bytes 96 | tf_op jit(solution)/shard_map/ppermute | solution.py:698
  178.5 2.6 %place.2.rest_0_ = bf16[4,192,2048]{2,1,0:T(8,128)(2,1)} custom-call(s32[3]{0:T(128)S(1)} %pad_add_fusion.where, bf16[2,192,2048]{2,1,0:T(8,128)(2,1)} %bitcast.38), custom_call_target="tpu_custom_call" | custom-call | flops 1000000000 | bytes 4194304 | tf_op jit(solution)/shard_map/place/pallas_call | solution.py:575
  182.3 2.6 %place.3 = bf16[4,192,2048]{2,1,0:T(8,128)(2,1)} custom-call(s32[3]{0:T(128)S(1)} %pad_add_fusion.where, bf16[2,192,2048]{2,1,0:T(8,128)(2,1)} %copy-done.3, bf16[4,192,2048]{2,1,0:T(8,128)(2,1)} %place.2.rest_0_), custom_call_target="tpu_custom_call", output_to_operand_aliasing={{}: (2, {})} | custom-call | flops 1000000000 | bytes 4194304 | tf_op jit(solution)/shard_map/place/pallas_call | solution.py:575
  (57 shorter events, 13.7 us)
Async XLA Ops:
  0.6 5.8 %copy-start.1 = (bf16[8,4,192,192]{3,2,1,0:T(8,128)(2,1)S(1)}, bf16[8,4,192,192]{3,2,1,0:T(8,128)(2,1)}, u32[]{:S(2)}) copy-start(bf16[8,4,192,192]{3,2,1,0:T(8,128)(2,1)} %left.4) | copy-start | bytes 7077892
  3.1 33.1 %collective-permute-start.9 = (bf16[4,3,192,128]{3,2,1,0:T(8,128)(2,1)}, bf16[4,3,192,128]{3,2,1,0:T(8,128)(2,1)}, u32[]{:S(2)}, u32[]{:S(2)}) collective-permute-start(bf16[4,3,192,128]{3,2,1,0:T(8,128)(2,1)} %get-tuple-element.207.refs_0_), channel_id=1, source_target_pairs={{0,1},{1,2},{2,3},{3,0},{4,5},{5,6},{6,7},{7,4},{8,9},{9,10},{10,1... | collective-permute-start | bytes 1769480 | tf_op jit(solution)/shard_map/ppermute | solution.py:590
  5.1 33.5 %collective-permute-start.8 = (bf16[4,3,192,128]{3,2,1,0:T(8,128)(2,1)}, bf16[4,3,192,128]{3,2,1,0:T(8,128)(2,1)}, u32[]{:S(2)}, u32[]{:S(2)}) collective-permute-start(bf16[4,3,192,128]{3,2,1,0:T(8,128)(2,1)} %get-tuple-element.211.refs_1_), channel_id=1, source_target_pairs={{0,3},{1,0},{2,1},{3,2},{4,7},{5,4},{6,5},{7,6},{8,11},{9,8},{10,9... | collective-permute-start | bytes 1769480 | tf_op jit(solution)/shard_map/ppermute | solution.py:590
  10.3 28.5 %collective-permute-start.13 = (bf16[12,192,128]{2,1,0:T(8,128)(2,1)}, bf16[12,192,128]{2,1,0:T(8,128)(2,1)S(1)}, u32[]{:S(2)}, u32[]{:S(2)}) collective-permute-start(bf16[12,192,128]{2,1,0:T(8,128)(2,1)} %get-tuple-element.216), channel_id=1, source_target_pairs={{0,8},{8,16},{16,24},{24,0},{1,9},{9,17},{17,25},{25,1},{2,10},{10... | collective-permute-start | bytes 1769480 | tf_op jit(solution)/shard_map/ppermute | solution.py:590
  11.8 54.7 %collective-permute-start.7 = (bf16[4,3,192,128]{3,2,1,0:T(8,128)(2,1)}, bf16[4,3,192,128]{3,2,1,0:T(8,128)(2,1)}, u32[]{:S(2)}, u32[]{:S(2)}) collective-permute-start(bf16[4,3,192,128]{3,2,1,0:T(8,128)(2,1)} %get-tuple-element.207.refs_0_), channel_id=1, source_target_pairs={{0,3},{1,0},{2,1},{3,2},{4,7},{5,4},{6,5},{7,6},{8,11},{9,8},{10,9... | collective-permute-start | bytes 1769480 | tf_op jit(solution)/shard_map/ppermute | solution.py:590
  13.0 12.8 %collective-permute-start.3 = (s32[1]{0:T(128)}, s32[1]{0:T(128)}, u32[]{:S(2)}, u32[]{:S(2)}) collective-permute-start(s32[1]{0:T(128)} %param.17), channel_id=1, source_target_pairs={{0,8},{8,16},{16,24},{24,0},{1,9},{9,17},{17,25},{25,1},{2,10},{10... | collective-permute-start | bytes 20 | tf_op jit(solution)/shard_map/ppermute | solution.py:590
  25.8 3.0 %collective-permute-start.4 = (s32[1]{0:T(128)}, s32[1]{0:T(128)}, u32[]{:S(2)}, u32[]{:S(2)}) collective-permute-start(s32[1]{0:T(128)} %param.17), channel_id=1, source_target_pairs={{0,24},{8,0},{16,8},{24,16},{1,25},{9,1},{17,9},{25,17},{2,26},{10... | collective-permute-start | bytes 20 | tf_op jit(solution)/shard_map/ppermute | solution.py:590
  28.7 4.7 %collective-permute-start.5 = (s32[1]{0:T(128)}, s32[1]{0:T(128)}, u32[]{:S(2)}, u32[]{:S(2)}) collective-permute-start(s32[1]{0:T(128)} %param.17), channel_id=1, source_target_pairs={{0,32},{32,64},{64,96},{96,0},{1,33},{33,65},{65,97},{97,1},{2,34}... | collective-permute-start | bytes 20 | tf_op jit(solution)/shard_map/ppermute | solution.py:590
  33.4 2.8 %collective-permute-start.6 = (s32[1]{0:T(128)}, s32[1]{0:T(128)}, u32[]{:S(2)}, u32[]{:S(2)}) collective-permute-start(s32[1]{0:T(128)} %param.17), channel_id=1, source_target_pairs={{0,96},{32,0},{64,32},{96,64},{1,97},{33,1},{65,33},{97,65},{2,98}... | collective-permute-start | bytes 20 | tf_op jit(solution)/shard_map/ppermute | solution.py:590
  36.2 30.6 %collective-permute-start.10 = (bf16[4,3,192,128]{3,2,1,0:T(8,128)(2,1)}, bf16[4,3,192,128]{3,2,1,0:T(8,128)(2,1)}, u32[]{:S(2)}, u32[]{:S(2)}) collective-permute-start(bf16[4,3,192,128]{3,2,1,0:T(8,128)(2,1)} %get-tuple-element.211.refs_1_), channel_id=1, source_target_pairs={{0,1},{1,2},{2,3},{3,0},{4,5},{5,6},{6,7},{7,4},{8,9},{9,10},{10,1... | collective-permute-start | bytes 1769480 | tf_op jit(solution)/shard_map/ppermute | solution.py:590
  36.2 24.1 %collective-permute-start.14 = (bf16[12,192,128]{2,1,0:T(8,128)(2,1)}, bf16[12,192,128]{2,1,0:T(8,128)(2,1)S(1)}, u32[]{:S(2)}, u32[]{:S(2)}) collective-permute-start(bf16[12,192,128]{2,1,0:T(8,128)(2,1)} %get-tuple-element.217), channel_id=1, source_target_pairs={{0,24},{8,0},{16,8},{24,16},{1,25},{9,1},{17,9},{25,17},{2,26},{10... | collective-permute-start | bytes 1769480 | tf_op jit(solution)/shard_map/ppermute | solution.py:590
  38.6 23.0 %collective-permute-start.15 = (bf16[12,192,128]{2,1,0:T(8,128)(2,1)}, bf16[12,192,128]{2,1,0:T(8,128)(2,1)S(1)}, u32[]{:S(2)}, u32[]{:S(2)}) collective-permute-start(bf16[12,192,128]{2,1,0:T(8,128)(2,1)} %get-tuple-element.218), channel_id=1, source_target_pairs={{0,32},{32,64},{64,96},{96,0},{1,33},{33,65},{65,97},{97,1},{2,34}... | collective-permute-start | bytes 1769480 | tf_op jit(solution)/shard_map/ppermute | solution.py:590
  38.8 24.4 %collective-permute-start.16 = (bf16[12,192,128]{2,1,0:T(8,128)(2,1)}, bf16[12,192,128]{2,1,0:T(8,128)(2,1)}, u32[]{:S(2)}, u32[]{:S(2)}) collective-permute-start(bf16[12,192,128]{2,1,0:T(8,128)(2,1)} %get-tuple-element.219), channel_id=1, source_target_pairs={{0,96},{32,0},{64,32},{96,64},{1,97},{33,1},{65,33},{97,65},{2,98}... | collective-permute-start | bytes 1769480 | tf_op jit(solution)/shard_map/ppermute | solution.py:590
  50.4 7.4 %copy-start = (bf16[4,768,1024]{2,1,0:T(8,128)(2,1)}, bf16[4,768,1024]{2,1,0:T(8,128)(2,1)S(1)}, u32[]{:S(2)}) copy-start(bf16[4,768,1024]{2,1,0:T(8,128)(2,1)S(1)} %get-tuple-element.210.psi) | copy-start | bytes 18874372
  60.3 15.5 %collective-permute-start.11 = (bf16[4,3,192,128]{3,2,1,0:T(8,128)(2,1)}, bf16[4,3,192,128]{3,2,1,0:T(8,128)(2,1)}, u32[]{:S(2)}, u32[]{:S(2)}) collective-permute-start(bf16[4,3,192,128]{3,2,1,0:T(8,128)(2,1)} %collective-permute-done.9.refs_2_), channel_id=1, source_target_pairs={{0,1},{1,2},{2,3},{3,0},{4,5},{5,6},{6,7},{7,4},{8,9},{9,10},{10,1... | collective-permute-start | bytes 1769480 | tf_op jit(solution)/shard_map/ppermute | solution.py:590
  61.7 14.2 %collective-permute-start.12 = (bf16[4,3,192,128]{3,2,1,0:T(8,128)(2,1)}, bf16[4,3,192,128]{3,2,1,0:T(8,128)(2,1)}, u32[]{:S(2)}, u32[]{:S(2)}) collective-permute-start(bf16[4,3,192,128]{3,2,1,0:T(8,128)(2,1)} %collective-permute-done.8.refs_1_), channel_id=1, source_target_pairs={{0,3},{1,0},{2,1},{3,2},{4,7},{5,4},{6,5},{7,6},{8,11},{9,8},{10,9... | collective-permute-start | bytes 1769480 | tf_op jit(solution)/shard_map/ppermute | solution.py:590
  63.2 18.4 %slice-start = ((s8[6291456]{0:T(1024)(128)(4,1)}), s8[4194304]{0:T(1024)(128)(4,1)S(1)}, s32[]{:S(2)}) async-start(s8[6291456]{0:T(1024)(128)(4,1)} %bitcast.34), calls=%async_computation.2 | async-start | bytes 8388608
  65.1 16.5 %slice-start.1 = ((s8[6291456]{0:T(1024)(128)(4,1)}), s8[2097152]{0:T(1024)(128)(4,1)S(1)}, s32[]{:S(2)}) async-start(s8[6291456]{0:T(1024)(128)(4,1)} %bitcast.34), calls=%async_computation.3 | async-start | bytes 4194304
  65.1 16.5 %copy-start.4 = (f32[2048]{0:T(1024)S(1)}, f32[2048]{0:T(1024)}, u32[]{:S(2)}) copy-start(f32[2048]{0:T(1024)} %param.19) | copy-start | bytes 24580
  65.1 12.1 %collective-permute-start.17 = (bf16[1,6,192,128]{3,2,1,0:T(8,128)(2,1)}, bf16[1,6,192,128]{3,2,1,0:T(8,128)(2,1)}, u32[]{:S(2)}, u32[]{:S(2)}) collective-permute-start(bf16[1,6,192,128]{3,2,1,0:T(8,128)(2,1)} %fusion.3), channel_id=1, source_target_pairs={{0,3},{1,0},{2,1},{3,2},{4,7},{5,4},{6,5},{7,6},{8,11},{9,8},{10,9... | collective-permute-start | bytes 884744 | tf_op jit(solution)/shard_map/ppermute | solution.py:590
  66.5 11.8 %collective-permute-start.18 = (bf16[1,6,192,128]{3,2,1,0:T(8,128)(2,1)}, bf16[1,6,192,128]{3,2,1,0:T(8,128)(2,1)}, u32[]{:S(2)}, u32[]{:S(2)}) collective-permute-start(bf16[1,6,192,128]{3,2,1,0:T(8,128)(2,1)} %fusion.3), channel_id=1, source_target_pairs={{0,2},{1,3},{2,0},{3,1},{4,6},{5,7},{6,4},{7,5},{8,10},{9,11},{10,... | collective-permute-start | bytes 884744 | tf_op jit(solution)/shard_map/ppermute | solution.py:590
  66.8 14.7 %collective-permute-start.19 = (bf16[1,6,192,128]{3,2,1,0:T(8,128)(2,1)}, bf16[1,6,192,128]{3,2,1,0:T(8,128)(2,1)}, u32[]{:S(2)}, u32[]{:S(2)}) collective-permute-start(bf16[1,6,192,128]{3,2,1,0:T(8,128)(2,1)} %fusion.3), channel_id=1, source_target_pairs={{0,1},{1,2},{2,3},{3,0},{4,5},{5,6},{6,7},{7,4},{8,9},{9,10},{10,1... | collective-permute-start | bytes 884744 | tf_op jit(solution)/shard_map/ppermute | solution.py:590
  98.0 21.1 %collective-permute-start.20 = (bf16[384,2048]{1,0:T(8,128)(2,1)}, bf16[384,2048]{1,0:T(8,128)(2,1)S(1)}, u32[]{:S(2)}, u32[]{:S(2)}) collective-permute-start(bf16[384,2048]{1,0:T(8,128)(2,1)} %get-tuple-element.237), channel_id=1, source_target_pairs={{0,4},{4,0},{1,5},{5,1},{2,6},{6,2},{3,7},{7,3},{8,12},{12,8},{9,1... | collective-permute-start | bytes 4718600 | tf_op jit(solution)/shard_map/ppermute | solution.py:675
  112.2 4.5 %collective-permute-start.21 = (f32[8,2]{1,0:T(8,128)S(1)}, f32[8,2]{1,0:T(8,128)S(1)}, u32[]{:S(2)}, u32[]{:S(2)}) collective-permute-start(f32[8,2]{1,0:T(8,128)S(1)} %broadcast_in_dim.68), channel_id=1, source_target_pairs={{0,1},{1,2},{2,3},{3,0},{4,5},{5,6},{6,7},{7,4},{8,9},{9,10},{10,1... | collective-permute-start | bytes 200 | tf_op jit(solution)/shard_map/ppermute | solution.py:590
  114.3 4.0 %collective-permute-start.22 = (f32[8,2]{1,0:T(8,128)S(1)}, f32[8,2]{1,0:T(8,128)S(1)}, u32[]{:S(2)}, u32[]{:S(2)}) collective-permute-start(f32[8,2]{1,0:T(8,128)S(1)} %broadcast_in_dim.68), channel_id=1, source_target_pairs={{0,2},{1,3},{2,0},{3,1},{4,6},{5,7},{6,4},{7,5},{8,10},{9,11},{10,... | collective-permute-start | bytes 200 | tf_op jit(solution)/shard_map/ppermute | solution.py:590
  116.2 2.8 %collective-permute-start.23 = (f32[8,2]{1,0:T(8,128)S(1)}, f32[8,2]{1,0:T(8,128)S(1)}, u32[]{:S(2)}, u32[]{:S(2)}) collective-permute-start(f32[8,2]{1,0:T(8,128)S(1)} %broadcast_in_dim.68), channel_id=1, source_target_pairs={{0,3},{1,0},{2,1},{3,2},{4,7},{5,4},{6,5},{7,6},{8,11},{9,8},{10,9... | collective-permute-start | bytes 200 | tf_op jit(solution)/shard_map/ppermute | solution.py:590
  170.9 7.6 %copy-start.2 = (bf16[16,24,2048]{2,1,0:T(8,128)(2,1)}, bf16[16,24,2048]{2,1,0:T(8,128)(2,1)S(1)}, u32[]{:S(2)}) copy-start(bf16[16,24,2048]{2,1,0:T(8,128)(2,1)S(1)} %all_to_all.11) | copy-start | bytes 4718596
  170.9 10.2 %collective-permute-start.24 = (bf16[2,192,2048]{2,1,0:T(8,128)(2,1)S(1)}, bf16[2,192,2048]{2,1,0:T(8,128)(2,1)S(1)}, u32[]{:S(2)}, u32[]{:S(2)}) collective-permute-start(bf16[2,192,2048]{2,1,0:T(8,128)(2,1)S(1)} %bitcast.37), channel_id=1, source_target_pairs={{0,4},{4,0},{1,5},{5,1},{2,6},{6,2},{3,7},{7,3},{8,12},{12,8},{9,1... | collective-permute-start | bytes 4718600 | tf_op jit(solution)/shard_map/ppermute | solution.py:696
  175.0 3.0 %collective-permute-start.25 = (f32[8,2]{1,0:T(8,128)S(1)}, f32[8,2]{1,0:T(8,128)S(1)}, u32[]{:S(2)}, u32[]{:S(2)}) collective-permute-start(f32[8,2]{1,0:T(8,128)S(1)} %slice_add_fusion), channel_id=1, source_target_pairs={{0,4},{4,0},{1,5},{5,1},{2,6},{6,2},{3,7},{7,3},{8,12},{12,8},{9,1... | collective-permute-start | bytes 200 | tf_op jit(solution)/shard_map/ppermute | solution.py:698
  181.1 1.2 copy-start.3

commit v2 on v1

--- a/solution.py
+++ b/solution.py
@@ -40,7 +40,7 @@
         pack_one(blocks, slot, 1, second, (slot,))
 
 
-def pack_late_body(left, right, *outs):
+def pack_late_body(count, left, right, *outs):
     for k in range(4):
 
         @pl.when(pl.program_id(0) == k)
@@ -48,6 +48,7 @@
             for half in range(2):
                 pack_one(left, 0, half, outs[k], (), 3 * half)
                 pack_one(right, 0, half, outs[k], (), 6 + 3 * half)
+            outs[k][12] = jnp.full((192, 128), count[0].astype(jnp.float32)).astype(jnp.bfloat16)
 
 
 def pack_early(blocks):
@@ -63,17 +64,59 @@
     )(blocks)
 
 
-def pack_late(left, right):
+def pack_late(count, left, right):
     block = pl.BlockSpec((1, 4, 192, 192), lambda i: (i + CHUNK, 0, 0, 0))
     return pl.pallas_call(
         pack_late_body,
         grid=(4,),
-        in_specs=[block, block],
-        out_specs=[pl.BlockSpec((12, 192, 128), lambda i: (0, 0, 0))] * 4,
-        out_shape=[jax.ShapeDtypeStruct((12, 192, 128), jnp.bfloat16)] * 4,
+        in_specs=[pl.BlockSpec(memory_space=pltpu.SMEM), block, block],
+        out_specs=[pl.BlockSpec((13, 192, 128), lambda i: (0, 0, 0))] * 4,
+        out_shape=[jax.ShapeDtypeStruct((13, 192, 128), jnp.bfloat16)] * 4,
         cost_estimate=pl.CostEstimate(flops=2 * 10**9, bytes_accessed=2**22, transcendentals=0),
         name="pack_late",
-    )(left, right)
+    )(count, left, right)
+
+
+def pick_body(*refs):
+    extras = refs[:4]
+    flags, going, tiles, sem_tile, sem_going = refs[4:]
+    copies = [pltpu.make_async_copy(extras[k].at[12, pl.ds(0, 16)], tiles.at[k], sem_tile.at[k]) for k in range(4)]
+    for copy in copies:
+        copy.start()
+    for copy in copies:
+        copy.wait()
+    number = jnp.int32(0)
+    first = jnp.int32(3)
+    for k in (3, 2, 1, 0):
+        count = jnp.max(tiles[k].astype(jnp.float32)).astype(jnp.int32)
+        there = count > CHUNK + k
+        flags[k] = there.astype(jnp.int32)
+        number = number + there.astype(jnp.int32)
+        first = jnp.where(there, k, first)
+    flags[4] = jnp.minimum(number, 2)
+    flags[5] = first
+    for k in range(4):
+
+        @pl.when(first == k)
+        def _():
+            copy = pltpu.make_async_copy(extras[k].at[pl.ds(6, 6)], going.at[0], sem_going)
+            copy.start()
+            copy.wait()
+
+
+def pick(extras):
+    return pl.pallas_call(
+        pick_body,
+        in_specs=[pl.BlockSpec(memory_space=pltpu.HBM)] * 4,
+        out_specs=[pl.BlockSpec(memory_space=pltpu.SMEM), pl.BlockSpec(memory_space=pltpu.VMEM)],
+        out_shape=[jax.ShapeDtypeStruct((6,), jnp.int32), jax.ShapeDtypeStruct((1, 6, 192, 128), jnp.bfloat16)],
+        scratch_shapes=[
+            pltpu.VMEM((4, 16, 128), jnp.bfloat16),
+            pltpu.SemaphoreType.DMA((4,)),
+            pltpu.SemaphoreType.DMA(()),
+        ],
+        name="pick",
+    )(*extras)
 
 
 def select_body(where, left_sector, right_sector, left_energy, psi, table, rows, cols, energies, window, sems):
@@ -304,9 +347,9 @@
     rows, subspace, energies, right_energy = refs[:4]
     refs = list(refs[4:])
     if slots:
-        counts, extras, moved = refs[:4], refs[4:8], refs[8:11]
-        there = [counts[k][0] > CHUNK + k for k in range(4)]
-        refs = refs[11:]
+        flags, extras, moved = refs[0], refs[1:5], refs[5:8]
+        there = [flags[k] > 0 for k in range(4)]
+        refs = refs[8:]
     send, mine, proj, left_v, right_v, psi_v, image, acc_v, rows_v, sub_v, total, staged, sums = refs[:13]
     sem_left, sem_right, sem_psi, sem_acc, sem_rows, sem_sub, sem_out = refs[13:20]
     width = subspace.shape[3]
@@ -349,12 +392,11 @@
     if slots:
         extra_v, moved_v, sem_extra, sem_moved = refs[20:]
         extra_copies = []
-        taken = False
         for k in range(4):
             place = 0 if slots == 1 else k
-            copy = pltpu.make_async_copy(extras[k], extra_v.at[place], sem_extra.at[place])
-            extra_copies.append((there[k] & jnp.logical_not(taken) if slots == 1 else there[k], copy))
-            taken = there[k] | taken
+            source = extras[k].at[pl.ds(0, 12)]
+            copy = pltpu.make_async_copy(source, extra_v.at[place], sem_extra.at[place])
+            extra_copies.append((flags[5] == k if slots == 1 else there[k], copy))
         moved_copies = [
             pltpu.make_async_copy(moved[i], moved_v.at[i + 1], sem_moved.at[i]) for i in range(3)
         ]
@@ -542,7 +584,7 @@
         ]
     return pl.pallas_call(
         functools.partial(finish_body, slots),
-        in_specs=[smem] * 3 + [hbm] * 8 + [vmem, vmem] + ([smem] * 4 + [hbm] * 7 if slots else []),
+        in_specs=[smem] * 3 + [hbm] * 8 + [vmem, vmem] + ([smem] + [hbm] * 7 if slots else []),
         out_specs=[hbm, hbm, vmem],
         out_shape=[half, half, jax.ShapeDtypeStruct((2, 8, 128), jnp.float32)],
         scratch_shapes=scratch,
@@ -618,26 +660,19 @@
     mine_early = pack_early(right_blocks)
     prev = [shifted(half, "site", 1) for half in mine_early]
     following = [shifted(half, "site", -1) for half in mine_early]
-    left_later, right_later, count_later, _ = lax.optimization_barrier(
-        (left_blocks, right_blocks, term_count, mine_early[0])
-    )
+    left_later, right_later, _ = lax.optimization_barrier((left_blocks, right_blocks, mine_early[0]))
 
     ways = (("y", 1), ("y", -1), ("z", 1), ("z", -1))
-    late = pack_late(left_later, right_later)
+    late = pack_late(term_count, left_later, right_later)
     extras = [shifted(late[k], axis, by) for k, (axis, by) in enumerate(ways)]
-    counts = [shifted(count_later, axis, by) for axis, by in ways]
-    there = [counts[k][0] > CHUNK + k for k in range(4)]
-    number = sum(one.astype(jnp.int32) for one in there)
+    flags, going = pick(extras)
 
     where = jnp.stack([site, core, lax.axis_index(OPS)])
     table, rows, psi, energies = select(where, left_sector, right_sector, left_energy, wavefunction)
     own = products((0,), where, term_count, left_blocks, psi, [mine_early])
 
     far = (shifted(prev[0], "site", 1), shifted(following[1], "site", -1))
-    going = extras[3][6:12]
-    for k in (2, 1, 0):
-        going = jnp.where(there[k], extras[k][6:12], going)
-    moved = [shifted(going[None], "site", by) for by in (-1, 2, 1)]
+    moved = [shifted(going, "site", by) for by in (-1, 2, 1)]
     near = products((1, 3), where, term_count, left_blocks, psi, [following, prev])
 
     def rest(slots, late):
@@ -664,13 +699,13 @@
         return rest(0, [])
 
     def one():
-        return rest(1, [*counts, *extras, *moved])
+        return rest(1, [flags, *extras, *moved])
 
     def many():
         every = jnp.stack([one[6:12] for one in extras])
-        return rest(4, [*counts, *extras] + [shifted(every, "site", by) for by in (-1, 2, 1)])
-
-    send, mine, proj = lax.switch(jnp.minimum(number, 2), [none, one, many])
+        return rest(4, [flags, *extras] + [shifted(every, "site", by) for by in (-1, 2, 1)])
+
+    send, mine, proj = lax.switch(flags[4], [none, one, many])
     swap = [(0, 1), (1, 0)]
     away = lax.ppermute(send, "core", swap)
     proj = small_sum(jnp.broadcast_to(jnp.sum(proj, axis=(1, 2))[None, :], (8, 2)), "site")[0]

time: 186 us -> 161 us (0.87)
  starting transfers between devices: 45.5 us -> 30.4 us
  waiting for transfers between devices: 27.8 us -> 20.5 us
  other arithmetic: 4.88 us -> 2.99 us
    ppermute x1, starting transfers between devices: 14.2 us -> 4.31 us  [local(): away = lax.ppermute(send, 'core', swap)]
    ppermute x20 -> x16, waiting for transfers between devices: 24.9 us -> 17.6 us  [shifted(): lax.ppermute(value, axis, [(i, (i + by) % size) for i in range(size)])]
    ppermute x20 -> x16, starting transfers between devices: 27.4 us -> 22.1 us  [shifted(): lax.ppermute(value, axis, [(i, (i + by) % size) for i in range(size)])]
    pallas_call x1 -> x2, Pallas kernels: 3.87 us -> 6.53 us  [the longest x1 3.97 us: pack_late(): pl.pallas_call(pack_late_body, grid=(4,), in_specs=[pl.BlockSpec(memory_s...]
    broadcast_in_dim x1 -> x0, other arithmetic: 1.89 us -> none  [local(): moved = [shifted(going[None], 'site', by) for by in (-1, 2, 1)]]
  transfers between devices with their start and end apart: 23 -> 19, of which waited for: 10 -> 5; matrix products, arithmetic and copies ran while one was open for 2% -> 1% of each run, Pallas kernels for 16% -> 18%
where the time goes in v2:
time: 161 us; the launch traced here: 160 us
  Pallas kernels  53.3 us (33%)
  blocking collectives  47.7 us (30%)
  starting transfers between devices  30.4 us (19%)
  waiting for transfers between devices  20.5 us (13%)
  other arithmetic  2.99 us (2%)
  local copies, waits for them, and re-layouts  2.52 us (2%)
  between operations  2.36 us (1%)
    all_to_all x1, blocking collectives, local(): lax.all_to_all(both.reshape(plane, share, bond + EXTRA), ('z', 'y'), 0, 0...  24.9 us
    all_to_all x1, blocking collectives, local(): lax.all_to_all(jnp.broadcast_to(summed[None], (plane, share, bond)), ('z'...  22.8 us
    ppermute x16, starting transfers between devices, shifted(): lax.ppermute(value, axis, [(i, (i + by) % size) for i in range(size)])  22.1 us
    ppermute x16, waiting for transfers between devices, shifted(): lax.ppermute(value, axis, [(i, (i + by) % size) for i in range(size)])  17.6 us
    pallas_call x1, Pallas kernels, finish(): pl.pallas_call(functools.partial(finish_body, slots), in_specs=[smem] * 3...  16.2 us
    pallas_call x2, Pallas kernels, products(): pl.pallas_call(functools.partial(products_body, tuple(rels)), in_specs=[s...  14.2 us
    pallas_call x1, Pallas kernels, select(): pl.pallas_call(select_body, grid=(4,), in_specs=[smem, ids, ids, pl.Block...  8.68 us
    pallas_call x2, Pallas kernels, place(): pl.pallas_call(functools.partial(place_body, which), in_specs=[pl.BlockSp...  5.17 us
  transfers between devices with their start and end apart: 19, of which 5 were waited for; matrix products, arithmetic and copies ran while one was open for 1% of the time, Pallas kernels for 18%

profile of v2, /device:TPU:1, one launch (start us, length us, event | category | flops | bytes accessed | tf_op | source)
XLA Modules:
  0.0 160.1 jit_solution(3875857078699666594)
XLA Ops:
  0.6 2.5 %pack_early.1 = (bf16[4,3,192,128]{3,2,1,0:T(8,128)(2,1)}, bf16[4,3,192,128]{3,2,1,0:T(8,128)(2,1)}) custom-call(bf16[8,4,192,192]{3,2,1,0:T(8,128)(2,1)} %right), custom_call_target="tpu_custom_call" | custom-call | tf_op jit(solution)/shard_map/pack_early/pallas_call | solution.py:57
  3.8 4.0 %pack_late.1 = (bf16[13,192,128]{2,1,0:T(8,128)(2,1)}, bf16[13,192,128]{2,1,0:T(8,128)(2,1)}, bf16[13,192,128]{2,1,0:T(8,128)(2,1)}, bf16[13,192,128]{2,1,0:T(8,128)(2,1)}) custom-call(s32[1]{0:T(128)S(6)} %copy.22.count, bf16[8,4,192,192]{3,2,1,0:T(8,128)(2,1)S(1)} %copy-done.1, bf16[8,4,192,192]{3,2,1,0:T(8,128)(2,1)} %right), custom_call_target="tpu_custom_call" | custom-call | flops 2000000000 | bytes 4194304 | tf_op jit(solution)/shard_map/pack_late/pallas_call | solution.py:69
  7.7 2.1 %collective-permute-start.3 = (bf16[13,192,128]{2,1,0:T(8,128)(2,1)}, bf16[13,192,128]{2,1,0:T(8,128)(2,1)S(1)}, u32[]{:S(2)}, u32[]{:S(2)}) collective-permute-start(bf16[13,192,128]{2,1,0:T(8,128)(2,1)} %get-tuple-element.193), channel_id=1, source_target_pairs={{0,8},{8,16},{16,24},{24,0},{1,9},{9,17},{17,25},{25,1},{2,10},{10... | collective-permute-start | bytes 1916936 | tf_op jit(solution)/shard_map/ppermute | solution.py:632
  9.9 1.2 collective-permute-start.9
  11.1 1.5 collective-permute-start.8
  12.5 1.4 collective-permute-start.4
  14.0 1.6 %collective-permute-start.5 = (bf16[13,192,128]{2,1,0:T(8,128)(2,1)}, bf16[13,192,128]{2,1,0:T(8,128)(2,1)S(1)}, u32[]{:S(2)}, u32[]{:S(2)}) collective-permute-start(bf16[13,192,128]{2,1,0:T(8,128)(2,1)} %get-tuple-element.195), channel_id=1, source_target_pairs={{0,32},{32,64},{64,96},{96,0},{1,33},{33,65},{65,97},{97,1},{2,34}... | collective-permute-start | bytes 1916936 | tf_op jit(solution)/shard_map/ppermute | solution.py:632
  15.7 9.5 %collective-permute-done.9.refs_2_ = bf16[4,3,192,128]{3,2,1,0:T(8,128)(2,1)S(1)} collective-permute-done((bf16[4,3,192,128]{3,2,1,0:T(8,128)(2,1)}, bf16[4,3,192,128]{3,2,1,0:T(8,128)(2,1)S(1)}, u32[]{:S(2)}, u32[]{:S(2)}) %collective-permute-start.9) | collective-permute-done | bytes 589856 | tf_op jit(solution)/shard_map/ppermute | solution.py:632
  25.2 1.3 collective-permute-start.7
  26.7 3.8 %collective-permute-start.6 = (bf16[13,192,128]{2,1,0:T(8,128)(2,1)}, bf16[13,192,128]{2,1,0:T(8,128)(2,1)}, u32[]{:S(2)}, u32[]{:S(2)}) collective-permute-start(bf16[13,192,128]{2,1,0:T(8,128)(2,1)} %get-tuple-element.196), channel_id=1, source_target_pairs={{0,96},{32,0},{64,32},{96,64},{1,97},{33,1},{65,33},{97,65},{2,98}... | collective-permute-start | bytes 1916936 | tf_op jit(solution)/shard_map/ppermute | solution.py:632
  30.5 8.7 %select.20 = (s32[40]{0:T(128)S(1)}, bf16[768,2048]{1,0:T(8,128)(2,1)}, bf16[4,768,1024]{2,1,0:T(8,128)(2,1)S(1)}, f32[768,1]{1,0:T(8,128)}) custom-call(s32[3]{0:T(128)S(1)} %pad_add_fusion.where, s32[16,128]{1,0:T(8,128)} %bitcast.37, s32[16,128]{1,0:T(8,128)} %bitcast.38, f32[1,2048]{1,0:T(1,128)} %bitcast.39, bf16[2048,2048]{1,0:T(8,128)(2,1)} %psi.1), custom_call_target="tpu_custom_call" | custom-call | flops 5000000000 | bytes 16777216 | tf_op jit(solution)/shard_map/select/pallas_call | solution.py:189
  39.7 2.2 %collective-permute-start.12 = (bf16[4,3,192,128]{3,2,1,0:T(8,128)(2,1)}, bf16[4,3,192,128]{3,2,1,0:T(8,128)(2,1)}, u32[]{:S(2)}, u32[]{:S(2)}) collective-permute-start(bf16[4,3,192,128]{3,2,1,0:T(8,128)(2,1)} %copy-done.6), channel_id=1, source_target_pairs={{0,3},{1,0},{2,1},{3,2},{4,7},{5,4},{6,5},{7,6},{8,11},{9,8},{10,9... | collective-permute-start | bytes 1769480 | tf_op jit(solution)/shard_map/ppermute | solution.py:632
  41.9 5.8 %products.2 = f32[1,768,1024]{2,1,0:T(8,128)} custom-call(s32[3]{0:T(128)S(1)} %pad_add_fusion.where, s32[1]{0:T(128)S(6)} %copy.22.count, bf16[8,4,192,192]{3,2,1,0:T(8,128)(2,1)} %left.4, bf16[4,768,1024]{2,1,0:T(8,128)(2,1)S(1)} %get-tuple-element.199.psi, bf16[4,3,192,128]{3,2,1,0:T(8,128)(2,1)} %get-tuple-element.190.refs_0_, ...), custom_call_target="tpu_custom_call" | custom-call | flops 2818572288 | bytes 8388608 | tf_op jit(solution)/shard_map/products/pallas_call | solution.py:323
  47.7 2.6 %pick.1 = (s32[6]{0:T(128)S(1)}, bf16[1,6,192,128]{3,2,1,0:T(8,128)(2,1)}) custom-call(bf16[13,192,128]{2,1,0:T(8,128)(2,1)S(1)} %collective-permute-done.3.refs_0_, bf16[13,192,128]{2,1,0:T(8,128)(2,1)S(1)} %collective-permute-done.4.refs_1_, bf16[13,192,128]{2,1,0:T(8,128)(2,1)S(1)} %collective-permute-done.5.refs_2_, ...), custom_call_target="tpu_custom_call" | custom-call | tf_op jit(solution)/shard_map/pick/pallas_call | solution.py:108
  50.3 1.3 collective-permute-start.13
  52.4 8.4 %products.3 = f32[2,768,1024]{2,1,0:T(8,128)} custom-call(s32[3]{0:T(128)S(1)} %pad_add_fusion.where, s32[1]{0:T(128)S(6)} %copy.22.count, bf16[8,4,192,192]{3,2,1,0:T(8,128)(2,1)} %left.4, bf16[4,768,1024]{2,1,0:T(8,128)(2,1)} %copy-done, bf16[4,3,192,128]{3,2,1,0:T(8,128)(2,1)} %collective-permute-done.7.refs_0_, bf16[4,3,192,128]{3,2,1,0:T(8,128)(2,1)} %copy-done.6, ...), custom_call_target="tpu_custom_call" | custom-call | flops 5637144576 | bytes 8388608 | tf_op jit(solution)/shard_map/products/pallas_call | solution.py:323
  62.1 5.7 %collective-permute-done.15 = bf16[1,6,192,128]{3,2,1,0:T(8,128)(2,1)} collective-permute-done((bf16[1,6,192,128]{3,2,1,0:T(8,128)(2,1)}, bf16[1,6,192,128]{3,2,1,0:T(8,128)(2,1)}, u32[]{:S(2)}, u32[]{:S(2)}) %collective-permute-start.15) | collective-permute-done | bytes 294944 | tf_op jit(solution)/shard_map/ppermute | solution.py:632
  67.8 16.4 %conditional.1 = ((bf16[384,2048]{1,0:T(8,128)(2,1)}, bf16[384,2048]{1,0:T(8,128)(2,1)}, f32[2,8,128]{2,1,0:T(8,128)S(1)})) conditional(s32[]{:T(128)} %bitcast.10, (f32[2048]{0:T(1024)S(1)}, s32[3]{0:T(128)S(1)}, s32[1]{0:T(128)}, s32[40]{0:T(128)S(1)}, f32[1,768,1024]{2,1,0:T(8,128)}, /*index=5*/f32[2,768,1024]{2,1,0:T(8,128)}, ...), branch_computations={%region_0.0_spmd, %region_1.0_spmd, %region_2.0_spmd} | conditional | flops 8001769472 | bytes 50331776 | solution.py:708
  67.8 16.2 %finish.3 = (bf16[384,2048]{1,0:T(8,128)(2,1)}, bf16[384,2048]{1,0:T(8,128)(2,1)}, f32[2,8,128]{2,1,0:T(8,128)S(1)}) custom-call(s32[3]{0:T(128)S(1)} %get-tuple-element.119.where, s32[1]{0:T(128)} %get-tuple-element.120.count, s32[40]{0:T(128)S(1)} %get-tuple-element.121.table, f32[1,768,1024]{2,1,0:T(8,128)} %get-tuple-element.122.own, ...), custom_call_target="tpu_custom_call" | custom-call | flops 8000000000 | bytes 31457280 | tf_op jit(solution)/shard_map/cond/branch_0_fun/finish/pallas_call | solution.py:585
  84.2 4.3 %collective-permute-start.16 = (bf16[384,2048]{1,0:T(8,128)(2,1)}, bf16[384,2048]{1,0:T(8,128)(2,1)S(1)}, u32[]{:S(2)}, u32[]{:S(2)}) collective-permute-start(bf16[384,2048]{1,0:T(8,128)(2,1)} %get-tuple-element.221), channel_id=1, source_target_pairs={{0,4},{4,0},{1,5},{5,1},{2,6},{6,2},{3,7},{7,3},{8,12},{12,8},{9,1... | collective-permute-start | bytes 4718600 | tf_op jit(solution)/shard_map/ppermute | solution.py:710
  88.7 1.8 %collective-permute-start.17 = (f32[8,2]{1,0:T(8,128)S(1)}, f32[8,2]{1,0:T(8,128)S(1)}, u32[]{:S(2)}, u32[]{:S(2)}) collective-permute-start(f32[8,2]{1,0:T(8,128)S(1)} %broadcast_in_dim.62), channel_id=1, source_target_pairs={{0,1},{1,2},{2,3},{3,0},{4,5},{5,6},{6,7},{7,4},{8,9},{9,10},{10,1... | collective-permute-start | bytes 200 | tf_op jit(solution)/shard_map/ppermute | solution.py:632
  90.5 2.0 %collective-permute-start.18 = (f32[8,2]{1,0:T(8,128)S(1)}, f32[8,2]{1,0:T(8,128)S(1)}, u32[]{:S(2)}, u32[]{:S(2)}) collective-permute-start(f32[8,2]{1,0:T(8,128)S(1)} %broadcast_in_dim.62), channel_id=1, source_target_pairs={{0,2},{1,3},{2,0},{3,1},{4,6},{5,7},{6,4},{7,5},{8,10},{9,11},{10,... | collective-permute-start | bytes 200 | tf_op jit(solution)/shard_map/ppermute | solution.py:632
  92.9 1.5 collective-permute-done.18
  94.4 0.8 collective-permute-done.19
  95.4 2.0 %fusion = bf16[384,2048]{1,0:T(8,128)(2,1)S(1)} fusion(bf16[384,2048]{1,0:T(8,128)(2,1)} %get-tuple-element.220, bf16[384,2048]{1,0:T(8,128)(2,1)S(1)} %collective-permute-done.16), kind=kLoop, calls=%fused_computation.7 | loop fusion | flops 3145728 | bytes 4718592 | tf_op jit(solution)/shard_map/convert_element_type | solution.py:712
  97.7 24.9 %all_to_all.10 = bf16[16,24,2176]{2,1,0:T(8,128)(2,1)S(1)} all-to-all(bf16[16,24,2176]{2,1,0:T(8,128)(2,1)S(1)} %bitcast.31), channel_id=1, replica_groups=mesh['z'=4,'y'=4,'core'=2,'site'=4] {'z','y'}, dimensions={0} | all-to-all | bytes 3342336 | tf_op jit(solution)/shard_map/all_to_all | solution.py:723
  123.1 22.8 %all_to_all.11 = bf16[16,24,2048]{2,1,0:T(8,128)(2,1)S(1)} all-to-all(bf16[16,24,2048]{2,1,0:T(8,128)(2,1)S(1)} %broadcast_in_dim.68), channel_id=1, replica_groups=mesh['z'=4,'y'=4,'core'=2,'site'=4] {'z','y'}, dimensions={0} | all-to-all | bytes 3145728 | tf_op jit(solution)/shard_map/all_to_all | solution.py:726
  145.9 4.0 %collective-permute-start.20 = (bf16[2,192,2048]{2,1,0:T(8,128)(2,1)S(1)}, bf16[2,192,2048]{2,1,0:T(8,128)(2,1)S(1)}, u32[]{:S(2)}, u32[]{:S(2)}) collective-permute-start(bf16[2,192,2048]{2,1,0:T(8,128)(2,1)S(1)} %bitcast.32), channel_id=1, source_target_pairs={{0,4},{4,0},{1,5},{5,1},{2,6},{6,2},{3,7},{7,3},{8,12},{12,8},{9,1... | collective-permute-start | bytes 4718600 | tf_op jit(solution)/shard_map/ppermute | solution.py:731
  150.0 2.9 %collective-permute-done.21 = f32[8,2]{1,0:T(8,128)S(1)} collective-permute-done((f32[8,2]{1,0:T(8,128)S(1)}, f32[8,2]{1,0:T(8,128)S(1)}, u32[]{:S(2)}, u32[]{:S(2)}) %collective-permute-start.21) | collective-permute-done | bytes 96 | tf_op jit(solution)/shard_map/ppermute | solution.py:733
  153.5 2.6 %place.2.rest_0_ = bf16[4,192,2048]{2,1,0:T(8,128)(2,1)} custom-call(s32[3]{0:T(128)S(1)} %pad_add_fusion.where, bf16[2,192,2048]{2,1,0:T(8,128)(2,1)} %bitcast.33), custom_call_target="tpu_custom_call" | custom-call | flops 1000000000 | bytes 4194304 | tf_op jit(solution)/shard_map/place/pallas_call | solution.py:617
  156.1 1.2 copy-done.3
  157.3 2.6 %place.3 = bf16[4,192,2048]{2,1,0:T(8,128)(2,1)} custom-call(s32[3]{0:T(128)S(1)} %pad_add_fusion.where, bf16[2,192,2048]{2,1,0:T(8,128)(2,1)} %copy-done.3, bf16[4,192,2048]{2,1,0:T(8,128)(2,1)} %place.2.rest_0_), custom_call_target="tpu_custom_call", output_to_operand_aliasing={{}: (2, {})} | custom-call | flops 1000000000 | bytes 4194304 | tf_op jit(solution)/shard_map/place/pallas_call | solution.py:617
  (54 shorter events, 4.2 us)
Async XLA Ops:
  0.6 3.1 %copy-start.1 = (bf16[8,4,192,192]{3,2,1,0:T(8,128)(2,1)S(1)}, bf16[8,4,192,192]{3,2,1,0:T(8,128)(2,1)}, u32[]{:S(2)}) copy-start(bf16[8,4,192,192]{3,2,1,0:T(8,128)(2,1)} %left.4) | copy-start | bytes 7077892
  7.7 18.9 %collective-permute-start.3 = (bf16[13,192,128]{2,1,0:T(8,128)(2,1)}, bf16[13,192,128]{2,1,0:T(8,128)(2,1)S(1)}, u32[]{:S(2)}, u32[]{:S(2)}) collective-permute-start(bf16[13,192,128]{2,1,0:T(8,128)(2,1)} %get-tuple-element.193), channel_id=1, source_target_pairs={{0,8},{8,16},{16,24},{24,0},{1,9},{9,17},{17,25},{25,1},{2,10},{10... | collective-permute-start | bytes 1916936 | tf_op jit(solution)/shard_map/ppermute | solution.py:632
  9.9 15.4 %collective-permute-start.9 = (bf16[4,3,192,128]{3,2,1,0:T(8,128)(2,1)}, bf16[4,3,192,128]{3,2,1,0:T(8,128)(2,1)S(1)}, u32[]{:S(2)}, u32[]{:S(2)}) collective-permute-start(bf16[4,3,192,128]{3,2,1,0:T(8,128)(2,1)} %get-tuple-element.190.refs_0_), channel_id=1, source_target_pairs={{0,1},{1,2},{2,3},{3,0},{4,5},{5,6},{6,7},{7,4},{8,9},{9,10},{10,1... | collective-permute-start | bytes 1769480 | tf_op jit(solution)/shard_map/ppermute | solution.py:632
  11.1 15.4 %collective-permute-start.8 = (bf16[4,3,192,128]{3,2,1,0:T(8,128)(2,1)}, bf16[4,3,192,128]{3,2,1,0:T(8,128)(2,1)S(1)}, u32[]{:S(2)}, u32[]{:S(2)}) collective-permute-start(bf16[4,3,192,128]{3,2,1,0:T(8,128)(2,1)} %get-tuple-element.200.refs_1_), channel_id=1, source_target_pairs={{0,3},{1,0},{2,1},{3,2},{4,7},{5,4},{6,5},{7,6},{8,11},{9,8},{10,9... | collective-permute-start | bytes 1769480 | tf_op jit(solution)/shard_map/ppermute | solution.py:632
  12.5 26.6 %collective-permute-start.4 = (bf16[13,192,128]{2,1,0:T(8,128)(2,1)}, bf16[13,192,128]{2,1,0:T(8,128)(2,1)S(1)}, u32[]{:S(2)}, u32[]{:S(2)}) collective-permute-start(bf16[13,192,128]{2,1,0:T(8,128)(2,1)} %get-tuple-element.194), channel_id=1, source_target_pairs={{0,24},{8,0},{16,8},{24,16},{1,25},{9,1},{17,9},{25,17},{2,26},{10... | collective-permute-start | bytes 1916936 | tf_op jit(solution)/shard_map/ppermute | solution.py:632
  14.0 25.7 %collective-permute-start.5 = (bf16[13,192,128]{2,1,0:T(8,128)(2,1)}, bf16[13,192,128]{2,1,0:T(8,128)(2,1)S(1)}, u32[]{:S(2)}, u32[]{:S(2)}) collective-permute-start(bf16[13,192,128]{2,1,0:T(8,128)(2,1)} %get-tuple-element.195), channel_id=1, source_target_pairs={{0,32},{32,64},{64,96},{96,0},{1,33},{33,65},{65,97},{97,1},{2,34}... | collective-permute-start | bytes 1916936 | tf_op jit(solution)/shard_map/ppermute | solution.py:632
  25.2 5.2 %copy-start.5 = (bf16[4,3,192,128]{3,2,1,0:T(8,128)(2,1)}, bf16[4,3,192,128]{3,2,1,0:T(8,128)(2,1)S(1)}, u32[]{:S(2)}) copy-start(bf16[4,3,192,128]{3,2,1,0:T(8,128)(2,1)S(1)} %collective-permute-done.9.refs_2_) | copy-start | bytes 1769476
  25.2 26.5 %collective-permute-start.7 = (bf16[4,3,192,128]{3,2,1,0:T(8,128)(2,1)}, bf16[4,3,192,128]{3,2,1,0:T(8,128)(2,1)}, u32[]{:S(2)}, u32[]{:S(2)}) collective-permute-start(bf16[4,3,192,128]{3,2,1,0:T(8,128)(2,1)} %get-tuple-element.190.refs_0_), channel_id=1, source_target_pairs={{0,3},{1,0},{2,1},{3,2},{4,7},{5,4},{6,5},{7,6},{8,11},{9,8},{10,9... | collective-permute-start | bytes 1769480 | tf_op jit(solution)/shard_map/ppermute | solution.py:632
  26.5 4.0 %copy-start.6 = (bf16[4,3,192,128]{3,2,1,0:T(8,128)(2,1)}, bf16[4,3,192,128]{3,2,1,0:T(8,128)(2,1)S(1)}, u32[]{:S(2)}) copy-start(bf16[4,3,192,128]{3,2,1,0:T(8,128)(2,1)S(1)} %collective-permute-done.8.refs_1_) | copy-start | bytes 1769476
  26.5 25.2 %collective-permute-start.10 = (bf16[4,3,192,128]{3,2,1,0:T(8,128)(2,1)}, bf16[4,3,192,128]{3,2,1,0:T(8,128)(2,1)}, u32[]{:S(2)}, u32[]{:S(2)}) collective-permute-start(bf16[4,3,192,128]{3,2,1,0:T(8,128)(2,1)} %get-tuple-element.200.refs_1_), channel_id=1, source_target_pairs={{0,1},{1,2},{2,3},{3,0},{4,5},{5,6},{6,7},{7,4},{8,9},{9,10},{10,1... | collective-permute-start | bytes 1769480 | tf_op jit(solution)/shard_map/ppermute | solution.py:632
  26.7 21.0 %collective-permute-start.6 = (bf16[13,192,128]{2,1,0:T(8,128)(2,1)}, bf16[13,192,128]{2,1,0:T(8,128)(2,1)}, u32[]{:S(2)}, u32[]{:S(2)}) collective-permute-start(bf16[13,192,128]{2,1,0:T(8,128)(2,1)} %get-tuple-element.196), channel_id=1, source_target_pairs={{0,96},{32,0},{64,32},{96,64},{1,97},{33,1},{65,33},{97,65},{2,98}... | collective-permute-start | bytes 1916936 | tf_op jit(solution)/shard_map/ppermute | solution.py:632
  39.1 8.6 %copy-start = (bf16[4,768,1024]{2,1,0:T(8,128)(2,1)}, bf16[4,768,1024]{2,1,0:T(8,128)(2,1)S(1)}, u32[]{:S(2)}) copy-start(bf16[4,768,1024]{2,1,0:T(8,128)(2,1)S(1)} %get-tuple-element.199.psi) | copy-start | bytes 18874372
  39.2 22.9 %collective-permute-start.11 = (bf16[4,3,192,128]{3,2,1,0:T(8,128)(2,1)}, bf16[4,3,192,128]{3,2,1,0:T(8,128)(2,1)}, u32[]{:S(2)}, u32[]{:S(2)}) collective-permute-start(bf16[4,3,192,128]{3,2,1,0:T(8,128)(2,1)} %copy-done.5), channel_id=1, source_target_pairs={{0,1},{1,2},{2,3},{3,0},{4,5},{5,6},{6,7},{7,4},{8,9},{9,10},{10,1... | collective-permute-start | bytes 1769480 | tf_op jit(solution)/shard_map/ppermute | solution.py:632
  39.7 22.4 %collective-permute-start.12 = (bf16[4,3,192,128]{3,2,1,0:T(8,128)(2,1)}, bf16[4,3,192,128]{3,2,1,0:T(8,128)(2,1)}, u32[]{:S(2)}, u32[]{:S(2)}) collective-permute-start(bf16[4,3,192,128]{3,2,1,0:T(8,128)(2,1)} %copy-done.6), channel_id=1, source_target_pairs={{0,3},{1,0},{2,1},{3,2},{4,7},{5,4},{6,5},{7,6},{8,11},{9,8},{10,9... | collective-permute-start | bytes 1769480 | tf_op jit(solution)/shard_map/ppermute | solution.py:632
  50.3 17.5 %slice-start = ((s8[6291456]{0:T(1024)(128)(4,1)}), s8[4194304]{0:T(1024)(128)(4,1)S(1)}, s32[]{:S(2)}) async-start(s8[6291456]{0:T(1024)(128)(4,1)} %bitcast.29), calls=%async_computation.2 | async-start | bytes 8388608
  50.3 17.5 %slice-start.1 = ((s8[6291456]{0:T(1024)(128)(4,1)}), s8[2097152]{0:T(1024)(128)(4,1)S(1)}, s32[]{:S(2)}) async-start(s8[6291456]{0:T(1024)(128)(4,1)} %bitcast.29), calls=%async_computation.3 | async-start | bytes 4194304
  50.3 17.5 %copy-start.4 = (f32[2048]{0:T(1024)S(1)}, f32[2048]{0:T(1024)}, u32[]{:S(2)}) copy-start(f32[2048]{0:T(1024)} %param.19) | copy-start | bytes 24580
  50.3 11.7 %collective-permute-start.13 = (bf16[1,6,192,128]{3,2,1,0:T(8,128)(2,1)}, bf16[1,6,192,128]{3,2,1,0:T(8,128)(2,1)}, u32[]{:S(2)}, u32[]{:S(2)}) collective-permute-start(bf16[1,6,192,128]{3,2,1,0:T(8,128)(2,1)} %get-tuple-element.203), channel_id=1, source_target_pairs={{0,3},{1,0},{2,1},{3,2},{4,7},{5,4},{6,5},{7,6},{8,11},{9,8},{10,9... | collective-permute-start | bytes 884744 | tf_op jit(solution)/shard_map/ppermute | solution.py:632
  51.7 10.4 %collective-permute-start.14 = (bf16[1,6,192,128]{3,2,1,0:T(8,128)(2,1)}, bf16[1,6,192,128]{3,2,1,0:T(8,128)(2,1)}, u32[]{:S(2)}, u32[]{:S(2)}) collective-permute-start(bf16[1,6,192,128]{3,2,1,0:T(8,128)(2,1)} %get-tuple-element.203), channel_id=1, source_target_pairs={{0,2},{1,3},{2,0},{3,1},{4,6},{5,7},{6,4},{7,5},{8,10},{9,11},{10,... | collective-permute-start | bytes 884744 | tf_op jit(solution)/shard_map/ppermute | solution.py:632
  51.7 16.1 %collective-permute-start.15 = (bf16[1,6,192,128]{3,2,1,0:T(8,128)(2,1)}, bf16[1,6,192,128]{3,2,1,0:T(8,128)(2,1)}, u32[]{:S(2)}, u32[]{:S(2)}) collective-permute-start(bf16[1,6,192,128]{3,2,1,0:T(8,128)(2,1)} %get-tuple-element.203), channel_id=1, source_target_pairs={{0,1},{1,2},{2,3},{3,0},{4,5},{5,6},{6,7},{7,4},{8,9},{9,10},{10,1... | collective-permute-start | bytes 884744 | tf_op jit(solution)/shard_map/ppermute | solution.py:632
  84.2 11.1 %collective-permute-start.16 = (bf16[384,2048]{1,0:T(8,128)(2,1)}, bf16[384,2048]{1,0:T(8,128)(2,1)S(1)}, u32[]{:S(2)}, u32[]{:S(2)}) collective-permute-start(bf16[384,2048]{1,0:T(8,128)(2,1)} %get-tuple-element.221), channel_id=1, source_target_pairs={{0,4},{4,0},{1,5},{5,1},{2,6},{6,2},{3,7},{7,3},{8,12},{12,8},{9,1... | collective-permute-start | bytes 4718600 | tf_op jit(solution)/shard_map/ppermute | solution.py:710
  88.7 4.3 %collective-permute-start.17 = (f32[8,2]{1,0:T(8,128)S(1)}, f32[8,2]{1,0:T(8,128)S(1)}, u32[]{:S(2)}, u32[]{:S(2)}) collective-permute-start(f32[8,2]{1,0:T(8,128)S(1)} %broadcast_in_dim.62), channel_id=1, source_target_pairs={{0,1},{1,2},{2,3},{3,0},{4,5},{5,6},{6,7},{7,4},{8,9},{9,10},{10,1... | collective-permute-start | bytes 200 | tf_op jit(solution)/shard_map/ppermute | solution.py:632
  90.5 4.0 %collective-permute-start.18 = (f32[8,2]{1,0:T(8,128)S(1)}, f32[8,2]{1,0:T(8,128)S(1)}, u32[]{:S(2)}, u32[]{:S(2)}) collective-permute-start(f32[8,2]{1,0:T(8,128)S(1)} %broadcast_in_dim.62), channel_id=1, source_target_pairs={{0,2},{1,3},{2,0},{3,1},{4,6},{5,7},{6,4},{7,5},{8,10},{9,11},{10,... | collective-permute-start | bytes 200 | tf_op jit(solution)/shard_map/ppermute | solution.py:632
  92.5 2.8 %collective-permute-start.19 = (f32[8,2]{1,0:T(8,128)S(1)}, f32[8,2]{1,0:T(8,128)S(1)}, u32[]{:S(2)}, u32[]{:S(2)}) collective-permute-start(f32[8,2]{1,0:T(8,128)S(1)} %broadcast_in_dim.62), channel_id=1, source_target_pairs={{0,3},{1,0},{2,1},{3,2},{4,7},{5,4},{6,5},{7,6},{8,11},{9,8},{10,9... | collective-permute-start | bytes 200 | tf_op jit(solution)/shard_map/ppermute | solution.py:632
  145.9 7.6 %copy-start.2 = (bf16[16,24,2048]{2,1,0:T(8,128)(2,1)}, bf16[16,24,2048]{2,1,0:T(8,128)(2,1)S(1)}, u32[]{:S(2)}) copy-start(bf16[16,24,2048]{2,1,0:T(8,128)(2,1)S(1)} %all_to_all.11) | copy-start | bytes 4718596
  145.9 10.2 %collective-permute-start.20 = (bf16[2,192,2048]{2,1,0:T(8,128)(2,1)S(1)}, bf16[2,192,2048]{2,1,0:T(8,128)(2,1)S(1)}, u32[]{:S(2)}, u32[]{:S(2)}) collective-permute-start(bf16[2,192,2048]{2,1,0:T(8,128)(2,1)S(1)} %bitcast.32), channel_id=1, source_target_pairs={{0,4},{4,0},{1,5},{5,1},{2,6},{6,2},{3,7},{7,3},{8,12},{12,8},{9,1... | collective-permute-start | bytes 4718600 | tf_op jit(solution)/shard_map/ppermute | solution.py:731
  149.9 3.0 %collective-permute-start.21 = (f32[8,2]{1,0:T(8,128)S(1)}, f32[8,2]{1,0:T(8,128)S(1)}, u32[]{:S(2)}, u32[]{:S(2)}) collective-permute-start(f32[8,2]{1,0:T(8,128)S(1)} %slice_add_fusion), channel_id=1, source_target_pairs={{0,4},{4,0},{1,5},{5,1},{2,6},{6,2},{3,7},{7,3},{8,12},{12,8},{9,1... | collective-permute-start | bytes 200 | tf_op jit(solution)/shard_map/ppermute | solution.py:733
  156.1 1.2 copy-start.3

commit v3 on v2

--- a/solution.py
+++ b/solution.py
@@ -79,7 +79,7 @@
 
 def pick_body(*refs):
     extras = refs[:4]
-    flags, going, tiles, sem_tile, sem_going = refs[4:]
+    flags, branch, going, tiles, sem_tile, sem_going = refs[4:]
     copies = [pltpu.make_async_copy(extras[k].at[12, pl.ds(0, 16)], tiles.at[k], sem_tile.at[k]) for k in range(4)]
     for copy in copies:
         copy.start()
@@ -93,8 +93,8 @@
         flags[k] = there.astype(jnp.int32)
         number = number + there.astype(jnp.int32)
         first = jnp.where(there, k, first)
-    flags[4] = jnp.minimum(number, 2)
-    flags[5] = first
+    flags[4] = first
+    branch[0] = jnp.minimum(number, 2)
     for k in range(4):
 
         @pl.when(first == k)
@@ -108,8 +108,8 @@
     return pl.pallas_call(
         pick_body,
         in_specs=[pl.BlockSpec(memory_space=pltpu.HBM)] * 4,
-        out_specs=[pl.BlockSpec(memory_space=pltpu.SMEM), pl.BlockSpec(memory_space=pltpu.VMEM)],
-        out_shape=[jax.ShapeDtypeStruct((6,), jnp.int32), jax.ShapeDtypeStruct((1, 6, 192, 128), jnp.bfloat16)],
+        out_specs=[pl.BlockSpec(memory_space=pltpu.SMEM)] * 2 + [pl.BlockSpec(memory_space=pltpu.VMEM)],
+        out_shape=[jax.ShapeDtypeStruct((5,), jnp.int32), jax.ShapeDtypeStruct((1,), jnp.int32), jax.ShapeDtypeStruct((1, 6, 192, 128), jnp.bfloat16)],
         scratch_shapes=[
             pltpu.VMEM((4, 16, 128), jnp.bfloat16),
             pltpu.SemaphoreType.DMA((4,)),
@@ -396,7 +396,7 @@
             place = 0 if slots == 1 else k
             source = extras[k].at[pl.ds(0, 12)]
             copy = pltpu.make_async_copy(source, extra_v.at[place], sem_extra.at[place])
-            extra_copies.append((flags[5] == k if slots == 1 else there[k], copy))
+            extra_copies.append((flags[4] == k if slots == 1 else there[k], copy))
         moved_copies = [
             pltpu.make_async_copy(moved[i], moved_v.at[i + 1], sem_moved.at[i]) for i in range(3)
         ]
@@ -658,14 +658,17 @@
     site = lax.axis_index("site")
     core = lax.axis_index("core")
     mine_early = pack_early(right_blocks)
-    prev = [shifted(half, "site", 1) for half in mine_early]
-    following = [shifted(half, "site", -1) for half in mine_early]
+    prev_first = shifted(mine_early[0], "site", 1)
+    next_second = shifted(mine_early[1], "site", -1)
+    second_after, first_after, _, _ = lax.optimization_barrier((mine_early[1], mine_early[0], left_blocks, term_count))
+    prev = [prev_first, shifted(second_after, "site", 1)]
+    following = [shifted(first_after, "site", -1), next_second]
     left_later, right_later, _ = lax.optimization_barrier((left_blocks, right_blocks, mine_early[0]))
 
     ways = (("y", 1), ("y", -1), ("z", 1), ("z", -1))
     late = pack_late(term_count, left_later, right_later)
     extras = [shifted(late[k], axis, by) for k, (axis, by) in enumerate(ways)]
-    flags, going = pick(extras)
+    flags, branch, going = pick(extras)
 
     where = jnp.stack([site, core, lax.axis_index(OPS)])
     table, rows, psi, energies = select(where, left_sector, right_sector, left_energy, wavefunction)
@@ -705,7 +708,7 @@
         every = jnp.stack([one[6:12] for one in extras])
         return rest(4, [flags, *extras] + [shifted(every, "site", by) for by in (-1, 2, 1)])
 
-    send, mine, proj = lax.switch(flags[4], [none, one, many])
+    send, mine, proj = lax.switch(branch[0], [none, one, many])
     swap = [(0, 1), (1, 0)]
     away = lax.ppermute(send, "core", swap)
     proj = small_sum(jnp.broadcast_to(jnp.sum(proj, axis=(1, 2))[None, :], (8, 2)), "site")[0]

time: 161 us -> 161 us (level)
  transfers between devices with their start and end apart: 19 -> 19, of which waited for: 5 -> 5; matrix products, arithmetic and copies ran while one was open for 1% -> 1% of each run, Pallas kernels for 18% -> 17%
where the time goes in v3:
time: 161 us
  Pallas kernels  53.3 us (33%)
  blocking collectives  47.5 us (30%)
  starting transfers between devices  31 us (19%)
  waiting for transfers between devices  21.5 us (13%)
  other arithmetic  2.99 us (2%)
  between operations  2.4 us (1%)
  local copies, waits for them, and re-layouts  1.94 us (1%)
    all_to_all x1, blocking collectives, local(): lax.all_to_all(both.reshape(plane, share, bond + EXTRA), ('z', 'y'), 0, 0...  24.9 us
    ppermute x16, starting transfers between devices, shifted(): lax.ppermute(value, axis, [(i, (i + by) % size) for i in range(size)])  22.7 us
    all_to_all x1, blocking collectives, local(): lax.all_to_all(jnp.broadcast_to(summed[None], (plane, share, bond)), ('z'...  22.6 us
    ppermute x16, waiting for transfers between devices, shifted(): lax.ppermute(value, axis, [(i, (i + by) % size) for i in range(size)])  18.5 us
    pallas_call x1, Pallas kernels, finish(): pl.pallas_call(functools.partial(finish_body, slots), in_specs=[smem] * 3...  16.2 us
    pallas_call x2, Pallas kernels, products(): pl.pallas_call(functools.partial(products_body, tuple(rels)), in_specs=[s...  14.2 us
    pallas_call x1, Pallas kernels, select(): pl.pallas_call(select_body, grid=(4,), in_specs=[smem, ids, ids, pl.Block...  8.68 us
    pallas_call x2, Pallas kernels, place(): pl.pallas_call(functools.partial(place_body, which), in_specs=[pl.BlockSp...  5.17 us
  transfers between devices with their start and end apart: 19, of which 5 were waited for; matrix products, arithmetic and copies ran while one was open for 1% of the time, Pallas kernels for 17%

profile of v3, /device:TPU:1, one launch (start us, length us, event | category | flops | bytes accessed | tf_op | source)
XLA Modules:
  0.0 160.8 jit_solution(5104449943719634694)
XLA Ops:
  0.6 2.5 %pack_early.1 = (bf16[4,3,192,128]{3,2,1,0:T(8,128)(2,1)}, bf16[4,3,192,128]{3,2,1,0:T(8,128)(2,1)}) custom-call(bf16[8,4,192,192]{3,2,1,0:T(8,128)(2,1)} %right), custom_call_target="tpu_custom_call" | custom-call | tf_op jit(solution)/shard_map/pack_early/pallas_call | solution.py:57
  3.8 4.0 %pack_late.1 = (bf16[13,192,128]{2,1,0:T(8,128)(2,1)}, bf16[13,192,128]{2,1,0:T(8,128)(2,1)}, bf16[13,192,128]{2,1,0:T(8,128)(2,1)}, bf16[13,192,128]{2,1,0:T(8,128)(2,1)}) custom-call(s32[1]{0:T(128)S(6)} %copy.22.count, bf16[8,4,192,192]{3,2,1,0:T(8,128)(2,1)S(1)} %copy-done.1, bf16[8,4,192,192]{3,2,1,0:T(8,128)(2,1)} %right), custom_call_target="tpu_custom_call" | custom-call | flops 2000000000 | bytes 4194304 | tf_op jit(solution)/shard_map/pack_late/pallas_call | solution.py:69
  7.7 2.1 %collective-permute-start.3 = (bf16[13,192,128]{2,1,0:T(8,128)(2,1)}, bf16[13,192,128]{2,1,0:T(8,128)(2,1)S(1)}, u32[]{:S(2)}, u32[]{:S(2)}) collective-permute-start(bf16[13,192,128]{2,1,0:T(8,128)(2,1)} %get-tuple-element.196), channel_id=1, source_target_pairs={{0,8},{8,16},{16,24},{24,0},{1,9},{9,17},{17,25},{25,1},{2,10},{10... | collective-permute-start | bytes 1916936 | tf_op jit(solution)/shard_map/ppermute | solution.py:632
  9.9 1.2 collective-permute-start.9
  11.1 1.5 collective-permute-start.8
  12.5 1.4 collective-permute-start.4
  14.0 1.6 %collective-permute-start.5 = (bf16[13,192,128]{2,1,0:T(8,128)(2,1)}, bf16[13,192,128]{2,1,0:T(8,128)(2,1)S(1)}, u32[]{:S(2)}, u32[]{:S(2)}) collective-permute-start(bf16[13,192,128]{2,1,0:T(8,128)(2,1)} %get-tuple-element.198), channel_id=1, source_target_pairs={{0,32},{32,64},{64,96},{96,0},{1,33},{33,65},{65,97},{97,1},{2,34}... | collective-permute-start | bytes 1916936 | tf_op jit(solution)/shard_map/ppermute | solution.py:632
  15.7 9.5 %collective-permute-done.9.refs_2_ = bf16[4,3,192,128]{3,2,1,0:T(8,128)(2,1)S(1)} collective-permute-done((bf16[4,3,192,128]{3,2,1,0:T(8,128)(2,1)}, bf16[4,3,192,128]{3,2,1,0:T(8,128)(2,1)S(1)}, u32[]{:S(2)}, u32[]{:S(2)}) %collective-permute-start.9) | collective-permute-done | bytes 589856 | tf_op jit(solution)/shard_map/ppermute | solution.py:632
  25.2 2.7 %collective-permute-start.7 = (bf16[4,3,192,128]{3,2,1,0:T(8,128)(2,1)}, bf16[4,3,192,128]{3,2,1,0:T(8,128)(2,1)}, u32[]{:S(2)}, u32[]{:S(2)}) collective-permute-start(bf16[4,3,192,128]{3,2,1,0:T(8,128)(2,1)} %get-tuple-element.204.refs_0_), channel_id=1, source_target_pairs={{0,3},{1,0},{2,1},{3,2},{4,7},{5,4},{6,5},{7,6},{8,11},{9,8},{10,9... | collective-permute-start | bytes 1769480 | tf_op jit(solution)/shard_map/ppermute | solution.py:632
  27.9 3.8 %collective-permute-start.6 = (bf16[13,192,128]{2,1,0:T(8,128)(2,1)}, bf16[13,192,128]{2,1,0:T(8,128)(2,1)}, u32[]{:S(2)}, u32[]{:S(2)}) collective-permute-start(bf16[13,192,128]{2,1,0:T(8,128)(2,1)} %get-tuple-element.199), channel_id=1, source_target_pairs={{0,96},{32,0},{64,32},{96,64},{1,97},{33,1},{65,33},{97,65},{2,98}... | collective-permute-start | bytes 1916936 | tf_op jit(solution)/shard_map/ppermute | solution.py:632
  31.7 8.7 %select.20 = (s32[40]{0:T(128)S(1)}, bf16[768,2048]{1,0:T(8,128)(2,1)}, bf16[4,768,1024]{2,1,0:T(8,128)(2,1)S(1)}, f32[768,1]{1,0:T(8,128)}) custom-call(s32[3]{0:T(128)S(1)} %pad_add_fusion.where, s32[16,128]{1,0:T(8,128)} %bitcast.37, s32[16,128]{1,0:T(8,128)} %bitcast.38, f32[1,2048]{1,0:T(1,128)} %bitcast.39, bf16[2048,2048]{1,0:T(8,128)(2,1)} %psi.1), custom_call_target="tpu_custom_call" | custom-call | flops 5000000000 | bytes 16777216 | tf_op jit(solution)/shard_map/select/pallas_call | solution.py:189
  40.5 2.7 %collective-permute-start.12 = (bf16[4,3,192,128]{3,2,1,0:T(8,128)(2,1)}, bf16[4,3,192,128]{3,2,1,0:T(8,128)(2,1)}, u32[]{:S(2)}, u32[]{:S(2)}) collective-permute-start(bf16[4,3,192,128]{3,2,1,0:T(8,128)(2,1)} %copy-done.6), channel_id=1, source_target_pairs={{0,3},{1,0},{2,1},{3,2},{4,7},{5,4},{6,5},{7,6},{8,11},{9,8},{10,9... | collective-permute-start | bytes 1769480 | tf_op jit(solution)/shard_map/ppermute | solution.py:632
  43.1 5.8 %products.2 = f32[1,768,1024]{2,1,0:T(8,128)} custom-call(s32[3]{0:T(128)S(1)} %pad_add_fusion.where, s32[1]{0:T(128)S(6)} %copy.22.count, bf16[8,4,192,192]{3,2,1,0:T(8,128)(2,1)} %left.4, bf16[4,768,1024]{2,1,0:T(8,128)(2,1)S(1)} %get-tuple-element.202.psi, bf16[4,3,192,128]{3,2,1,0:T(8,128)(2,1)} %get-tuple-element.204.refs_0_, ...), custom_call_target="tpu_custom_call" | custom-call | flops 2818572288 | bytes 8388608 | tf_op jit(solution)/shard_map/products/pallas_call | solution.py:323
  49.0 2.6 %pick.1 = (s32[5]{0:T(128)S(1)}, s32[1]{0:T(128)}, bf16[1,6,192,128]{3,2,1,0:T(8,128)(2,1)}) custom-call(bf16[13,192,128]{2,1,0:T(8,128)(2,1)S(1)} %collective-permute-done.3.refs_0_, bf16[13,192,128]{2,1,0:T(8,128)(2,1)S(1)} %collective-permute-done.4.refs_1_, bf16[13,192,128]{2,1,0:T(8,128)(2,1)S(1)} %collective-permute-done.5.refs_2_, ...), custom_call_target="tpu_custom_call" | custom-call | tf_op jit(solution)/shard_map/pick/pallas_call | solution.py:108
  51.6 0.6 collective-permute-start.14
  52.3 1.1 collective-permute-start.15
  53.4 8.4 %products.3 = f32[2,768,1024]{2,1,0:T(8,128)} custom-call(s32[3]{0:T(128)S(1)} %pad_add_fusion.where, s32[1]{0:T(128)S(6)} %copy.22.count, bf16[8,4,192,192]{3,2,1,0:T(8,128)(2,1)} %left.4, bf16[4,768,1024]{2,1,0:T(8,128)(2,1)} %copy-done, bf16[4,3,192,128]{3,2,1,0:T(8,128)(2,1)} %collective-permute-done.7.refs_0_, bf16[4,3,192,128]{3,2,1,0:T(8,128)(2,1)} %copy-done.6, ...), custom_call_target="tpu_custom_call" | custom-call | flops 5637144576 | bytes 8388608 | tf_op jit(solution)/shard_map/products/pallas_call | solution.py:323
  62.5 6.5 %collective-permute-done.15 = bf16[1,6,192,128]{3,2,1,0:T(8,128)(2,1)} collective-permute-done((bf16[1,6,192,128]{3,2,1,0:T(8,128)(2,1)}, bf16[1,6,192,128]{3,2,1,0:T(8,128)(2,1)}, u32[]{:S(2)}, u32[]{:S(2)}) %collective-permute-start.15) | collective-permute-done | bytes 294944 | tf_op jit(solution)/shard_map/ppermute | solution.py:632
  69.0 16.4 %conditional.1 = ((bf16[384,2048]{1,0:T(8,128)(2,1)}, bf16[384,2048]{1,0:T(8,128)(2,1)}, f32[2,8,128]{2,1,0:T(8,128)S(1)})) conditional(s32[]{:T(128)} %bitcast.10, (f32[2048]{0:T(1024)S(1)}, s32[3]{0:T(128)S(1)}, s32[1]{0:T(128)}, s32[40]{0:T(128)S(1)}, f32[1,768,1024]{2,1,0:T(8,128)}, /*index=5*/f32[2,768,1024]{2,1,0:T(8,128)}, ...), branch_computations={%region_0.0_spmd, %region_1.0_spmd, %region_2.0_spmd} | conditional | flops 8001769472 | bytes 50331776 | solution.py:711
  69.0 16.2 %finish.3 = (bf16[384,2048]{1,0:T(8,128)(2,1)}, bf16[384,2048]{1,0:T(8,128)(2,1)}, f32[2,8,128]{2,1,0:T(8,128)S(1)}) custom-call(s32[3]{0:T(128)S(1)} %get-tuple-element.119.where, s32[1]{0:T(128)} %get-tuple-element.120.count, s32[40]{0:T(128)S(1)} %get-tuple-element.121.table, f32[1,768,1024]{2,1,0:T(8,128)} %get-tuple-element.122.own, ...), custom_call_target="tpu_custom_call" | custom-call | flops 8000000000 | bytes 31457280 | tf_op jit(solution)/shard_map/cond/branch_0_fun/finish/pallas_call | solution.py:585
  85.4 4.3 %collective-permute-start.16 = (bf16[384,2048]{1,0:T(8,128)(2,1)}, bf16[384,2048]{1,0:T(8,128)(2,1)S(1)}, u32[]{:S(2)}, u32[]{:S(2)}) collective-permute-start(bf16[384,2048]{1,0:T(8,128)(2,1)} %get-tuple-element.227), channel_id=1, source_target_pairs={{0,4},{4,0},{1,5},{5,1},{2,6},{6,2},{3,7},{7,3},{8,12},{12,8},{9,1... | collective-permute-start | bytes 4718600 | tf_op jit(solution)/shard_map/ppermute | solution.py:713
  90.4 3.3 %collective-permute-start.18 = (f32[8,2]{1,0:T(8,128)S(1)}, f32[8,2]{1,0:T(8,128)S(1)}, u32[]{:S(2)}, u32[]{:S(2)}) collective-permute-start(f32[8,2]{1,0:T(8,128)S(1)} %broadcast_in_dim.62), channel_id=1, source_target_pairs={{0,2},{1,3},{2,0},{3,1},{4,6},{5,7},{6,4},{7,5},{8,10},{9,11},{10,... | collective-permute-start | bytes 200 | tf_op jit(solution)/shard_map/ppermute | solution.py:632
  93.7 1.0 collective-permute-done.18
  94.7 1.4 collective-permute-done.19
  96.3 2.0 %fusion = bf16[384,2048]{1,0:T(8,128)(2,1)S(1)} fusion(bf16[384,2048]{1,0:T(8,128)(2,1)} %get-tuple-element.226, bf16[384,2048]{1,0:T(8,128)(2,1)S(1)} %collective-permute-done.16), kind=kLoop, calls=%fused_computation.7 | loop fusion | flops 3145728 | bytes 4718592 | tf_op jit(solution)/shard_map/convert_element_type | solution.py:715
  98.6 24.9 %all_to_all.10 = bf16[16,24,2176]{2,1,0:T(8,128)(2,1)S(1)} all-to-all(bf16[16,24,2176]{2,1,0:T(8,128)(2,1)S(1)} %bitcast.31), channel_id=1, replica_groups=mesh['z'=4,'y'=4,'core'=2,'site'=4] {'z','y'}, dimensions={0} | all-to-all | bytes 3342336 | tf_op jit(solution)/shard_map/all_to_all | solution.py:726
  123.9 22.6 %all_to_all.11 = bf16[16,24,2048]{2,1,0:T(8,128)(2,1)S(1)} all-to-all(bf16[16,24,2048]{2,1,0:T(8,128)(2,1)S(1)} %broadcast_in_dim.68), channel_id=1, replica_groups=mesh['z'=4,'y'=4,'core'=2,'site'=4] {'z','y'}, dimensions={0} | all-to-all | bytes 3145728 | tf_op jit(solution)/shard_map/all_to_all | solution.py:729
  146.5 4.1 %collective-permute-start.20 = (bf16[2,192,2048]{2,1,0:T(8,128)(2,1)S(1)}, bf16[2,192,2048]{2,1,0:T(8,128)(2,1)S(1)}, u32[]{:S(2)}, u32[]{:S(2)}) collective-permute-start(bf16[2,192,2048]{2,1,0:T(8,128)(2,1)S(1)} %bitcast.32), channel_id=1, source_target_pairs={{0,4},{4,0},{1,5},{5,1},{2,6},{6,2},{3,7},{7,3},{8,12},{12,8},{9,1... | collective-permute-start | bytes 4718600 | tf_op jit(solution)/shard_map/ppermute | solution.py:734
  150.7 2.9 %collective-permute-done.21 = f32[8,2]{1,0:T(8,128)S(1)} collective-permute-done((f32[8,2]{1,0:T(8,128)S(1)}, f32[8,2]{1,0:T(8,128)S(1)}, u32[]{:S(2)}, u32[]{:S(2)}) %collective-permute-start.21) | collective-permute-done | bytes 96 | tf_op jit(solution)/shard_map/ppermute | solution.py:736
  154.2 2.6 %place.2.rest_0_ = bf16[4,192,2048]{2,1,0:T(8,128)(2,1)} custom-call(s32[3]{0:T(128)S(1)} %pad_add_fusion.where, bf16[2,192,2048]{2,1,0:T(8,128)(2,1)} %bitcast.33), custom_call_target="tpu_custom_call" | custom-call | flops 1000000000 | bytes 4194304 | tf_op jit(solution)/shard_map/place/pallas_call | solution.py:617
  156.9 1.2 copy-done.3
  158.0 2.6 %place.3 = bf16[4,192,2048]{2,1,0:T(8,128)(2,1)} custom-call(s32[3]{0:T(128)S(1)} %pad_add_fusion.where, bf16[2,192,2048]{2,1,0:T(8,128)(2,1)} %copy-done.3, bf16[4,192,2048]{2,1,0:T(8,128)(2,1)} %place.2.rest_0_), custom_call_target="tpu_custom_call", output_to_operand_aliasing={{}: (2, {})} | custom-call | flops 1000000000 | bytes 4194304 | tf_op jit(solution)/shard_map/place/pallas_call | solution.py:617
  (53 shorter events, 2.6 us)
Async XLA Ops:
  0.6 3.1 %copy-start.1 = (bf16[8,4,192,192]{3,2,1,0:T(8,128)(2,1)S(1)}, bf16[8,4,192,192]{3,2,1,0:T(8,128)(2,1)}, u32[]{:S(2)}) copy-start(bf16[8,4,192,192]{3,2,1,0:T(8,128)(2,1)} %left.4) | copy-start | bytes 7077892
  7.7 20.2 %collective-permute-start.3 = (bf16[13,192,128]{2,1,0:T(8,128)(2,1)}, bf16[13,192,128]{2,1,0:T(8,128)(2,1)S(1)}, u32[]{:S(2)}, u32[]{:S(2)}) collective-permute-start(bf16[13,192,128]{2,1,0:T(8,128)(2,1)} %get-tuple-element.196), channel_id=1, source_target_pairs={{0,8},{8,16},{16,24},{24,0},{1,9},{9,17},{17,25},{25,1},{2,10},{10... | collective-permute-start | bytes 1916936 | tf_op jit(solution)/shard_map/ppermute | solution.py:632
  9.9 15.4 %collective-permute-start.9 = (bf16[4,3,192,128]{3,2,1,0:T(8,128)(2,1)}, bf16[4,3,192,128]{3,2,1,0:T(8,128)(2,1)S(1)}, u32[]{:S(2)}, u32[]{:S(2)}) collective-permute-start(bf16[4,3,192,128]{3,2,1,0:T(8,128)(2,1)} %get-tuple-element.204.refs_0_), channel_id=1, source_target_pairs={{0,1},{1,2},{2,3},{3,0},{4,5},{5,6},{6,7},{7,4},{8,9},{9,10},{10,1... | collective-permute-start | bytes 1769480 | tf_op jit(solution)/shard_map/ppermute | solution.py:632
  11.1 14.2 %collective-permute-start.8 = (bf16[4,3,192,128]{3,2,1,0:T(8,128)(2,1)}, bf16[4,3,192,128]{3,2,1,0:T(8,128)(2,1)S(1)}, u32[]{:S(2)}, u32[]{:S(2)}) collective-permute-start(bf16[4,3,192,128]{3,2,1,0:T(8,128)(2,1)} %get-tuple-element.205.refs_1_), channel_id=1, source_target_pairs={{0,3},{1,0},{2,1},{3,2},{4,7},{5,4},{6,5},{7,6},{8,11},{9,8},{10,9... | collective-permute-start | bytes 1769480 | tf_op jit(solution)/shard_map/ppermute | solution.py:632
  12.5 27.8 %collective-permute-start.4 = (bf16[13,192,128]{2,1,0:T(8,128)(2,1)}, bf16[13,192,128]{2,1,0:T(8,128)(2,1)S(1)}, u32[]{:S(2)}, u32[]{:S(2)}) collective-permute-start(bf16[13,192,128]{2,1,0:T(8,128)(2,1)} %get-tuple-element.197), channel_id=1, source_target_pairs={{0,24},{8,0},{16,8},{24,16},{1,25},{9,1},{17,9},{25,17},{2,26},{10... | collective-permute-start | bytes 1916936 | tf_op jit(solution)/shard_map/ppermute | solution.py:632
  14.0 26.5 %collective-permute-start.5 = (bf16[13,192,128]{2,1,0:T(8,128)(2,1)}, bf16[13,192,128]{2,1,0:T(8,128)(2,1)S(1)}, u32[]{:S(2)}, u32[]{:S(2)}) collective-permute-start(bf16[13,192,128]{2,1,0:T(8,128)(2,1)} %get-tuple-element.198), channel_id=1, source_target_pairs={{0,32},{32,64},{64,96},{96,0},{1,33},{33,65},{65,97},{97,1},{2,34}... | collective-permute-start | bytes 1916936 | tf_op jit(solution)/shard_map/ppermute | solution.py:632
  25.2 6.4 %copy-start.5 = (bf16[4,3,192,128]{3,2,1,0:T(8,128)(2,1)}, bf16[4,3,192,128]{3,2,1,0:T(8,128)(2,1)S(1)}, u32[]{:S(2)}) copy-start(bf16[4,3,192,128]{3,2,1,0:T(8,128)(2,1)S(1)} %collective-permute-done.9.refs_2_) | copy-start | bytes 1769476
  25.2 26.4 %collective-permute-start.10 = (bf16[4,3,192,128]{3,2,1,0:T(8,128)(2,1)}, bf16[4,3,192,128]{3,2,1,0:T(8,128)(2,1)}, u32[]{:S(2)}, u32[]{:S(2)}) collective-permute-start(bf16[4,3,192,128]{3,2,1,0:T(8,128)(2,1)} %get-tuple-element.205.refs_1_), channel_id=1, source_target_pairs={{0,1},{1,2},{2,3},{3,0},{4,5},{5,6},{6,7},{7,4},{8,9},{9,10},{10,1... | collective-permute-start | bytes 1769480 | tf_op jit(solution)/shard_map/ppermute | solution.py:632
  25.2 6.4 %copy-start.6 = (bf16[4,3,192,128]{3,2,1,0:T(8,128)(2,1)}, bf16[4,3,192,128]{3,2,1,0:T(8,128)(2,1)S(1)}, u32[]{:S(2)}) copy-start(bf16[4,3,192,128]{3,2,1,0:T(8,128)(2,1)S(1)} %collective-permute-done.8.refs_1_) | copy-start | bytes 1769476
  25.2 27.1 %collective-permute-start.7 = (bf16[4,3,192,128]{3,2,1,0:T(8,128)(2,1)}, bf16[4,3,192,128]{3,2,1,0:T(8,128)(2,1)}, u32[]{:S(2)}, u32[]{:S(2)}) collective-permute-start(bf16[4,3,192,128]{3,2,1,0:T(8,128)(2,1)} %get-tuple-element.204.refs_0_), channel_id=1, source_target_pairs={{0,3},{1,0},{2,1},{3,2},{4,7},{5,4},{6,5},{7,6},{8,11},{9,8},{10,9... | collective-permute-start | bytes 1769480 | tf_op jit(solution)/shard_map/ppermute | solution.py:632
  27.9 21.0 %collective-permute-start.6 = (bf16[13,192,128]{2,1,0:T(8,128)(2,1)}, bf16[13,192,128]{2,1,0:T(8,128)(2,1)}, u32[]{:S(2)}, u32[]{:S(2)}) collective-permute-start(bf16[13,192,128]{2,1,0:T(8,128)(2,1)} %get-tuple-element.199), channel_id=1, source_target_pairs={{0,96},{32,0},{64,32},{96,64},{1,97},{33,1},{65,33},{97,65},{2,98}... | collective-permute-start | bytes 1916936 | tf_op jit(solution)/shard_map/ppermute | solution.py:632
  40.4 8.6 %copy-start = (bf16[4,768,1024]{2,1,0:T(8,128)(2,1)}, bf16[4,768,1024]{2,1,0:T(8,128)(2,1)S(1)}, u32[]{:S(2)}) copy-start(bf16[4,768,1024]{2,1,0:T(8,128)(2,1)S(1)} %get-tuple-element.202.psi) | copy-start | bytes 18874372
  40.4 22.0 %collective-permute-start.11 = (bf16[4,3,192,128]{3,2,1,0:T(8,128)(2,1)}, bf16[4,3,192,128]{3,2,1,0:T(8,128)(2,1)}, u32[]{:S(2)}, u32[]{:S(2)}) collective-permute-start(bf16[4,3,192,128]{3,2,1,0:T(8,128)(2,1)} %copy-done.5), channel_id=1, source_target_pairs={{0,1},{1,2},{2,3},{3,0},{4,5},{5,6},{6,7},{7,4},{8,9},{9,10},{10,1... | collective-permute-start | bytes 1769480 | tf_op jit(solution)/shard_map/ppermute | solution.py:632
  40.5 22.0 %collective-permute-start.12 = (bf16[4,3,192,128]{3,2,1,0:T(8,128)(2,1)}, bf16[4,3,192,128]{3,2,1,0:T(8,128)(2,1)}, u32[]{:S(2)}, u32[]{:S(2)}) collective-permute-start(bf16[4,3,192,128]{3,2,1,0:T(8,128)(2,1)} %copy-done.6), channel_id=1, source_target_pairs={{0,3},{1,0},{2,1},{3,2},{4,7},{5,4},{6,5},{7,6},{8,11},{9,8},{10,9... | collective-permute-start | bytes 1769480 | tf_op jit(solution)/shard_map/ppermute | solution.py:632
  51.5 17.5 %slice-start = ((s8[6291456]{0:T(1024)(128)(4,1)}), s8[4194304]{0:T(1024)(128)(4,1)S(1)}, s32[]{:S(2)}) async-start(s8[6291456]{0:T(1024)(128)(4,1)} %bitcast.29), calls=%async_computation.2 | async-start | bytes 8388608
  51.5 17.5 %slice-start.1 = ((s8[6291456]{0:T(1024)(128)(4,1)}), s8[2097152]{0:T(1024)(128)(4,1)S(1)}, s32[]{:S(2)}) async-start(s8[6291456]{0:T(1024)(128)(4,1)} %bitcast.29), calls=%async_computation.3 | async-start | bytes 4194304
  51.5 17.5 %copy-start.4 = (f32[2048]{0:T(1024)S(1)}, f32[2048]{0:T(1024)}, u32[]{:S(2)}) copy-start(f32[2048]{0:T(1024)} %param.19) | copy-start | bytes 24580
  51.6 10.9 %collective-permute-start.13 = (bf16[1,6,192,128]{3,2,1,0:T(8,128)(2,1)}, bf16[1,6,192,128]{3,2,1,0:T(8,128)(2,1)}, u32[]{:S(2)}, u32[]{:S(2)}) collective-permute-start(bf16[1,6,192,128]{3,2,1,0:T(8,128)(2,1)} %get-tuple-element.209), channel_id=1, source_target_pairs={{0,3},{1,0},{2,1},{3,2},{4,7},{5,4},{6,5},{7,6},{8,11},{9,8},{10,9... | collective-permute-start | bytes 884744 | tf_op jit(solution)/shard_map/ppermute | solution.py:632
  51.6 10.8 %collective-permute-start.14 = (bf16[1,6,192,128]{3,2,1,0:T(8,128)(2,1)}, bf16[1,6,192,128]{3,2,1,0:T(8,128)(2,1)}, u32[]{:S(2)}, u32[]{:S(2)}) collective-permute-start(bf16[1,6,192,128]{3,2,1,0:T(8,128)(2,1)} %get-tuple-element.209), channel_id=1, source_target_pairs={{0,2},{1,3},{2,0},{3,1},{4,6},{5,7},{6,4},{7,5},{8,10},{9,11},{10,... | collective-permute-start | bytes 884744 | tf_op jit(solution)/shard_map/ppermute | solution.py:632
  52.3 16.7 %collective-permute-start.15 = (bf16[1,6,192,128]{3,2,1,0:T(8,128)(2,1)}, bf16[1,6,192,128]{3,2,1,0:T(8,128)(2,1)}, u32[]{:S(2)}, u32[]{:S(2)}) collective-permute-start(bf16[1,6,192,128]{3,2,1,0:T(8,128)(2,1)} %get-tuple-element.209), channel_id=1, source_target_pairs={{0,1},{1,2},{2,3},{3,0},{4,5},{5,6},{6,7},{7,4},{8,9},{9,10},{10,1... | collective-permute-start | bytes 884744 | tf_op jit(solution)/shard_map/ppermute | solution.py:632
  85.4 10.8 %collective-permute-start.16 = (bf16[384,2048]{1,0:T(8,128)(2,1)}, bf16[384,2048]{1,0:T(8,128)(2,1)S(1)}, u32[]{:S(2)}, u32[]{:S(2)}) collective-permute-start(bf16[384,2048]{1,0:T(8,128)(2,1)} %get-tuple-element.227), channel_id=1, source_target_pairs={{0,4},{4,0},{1,5},{5,1},{2,6},{6,2},{3,7},{7,3},{8,12},{12,8},{9,1... | collective-permute-start | bytes 4718600 | tf_op jit(solution)/shard_map/ppermute | solution.py:713
  89.8 3.9 %collective-permute-start.17 = (f32[8,2]{1,0:T(8,128)S(1)}, f32[8,2]{1,0:T(8,128)S(1)}, u32[]{:S(2)}, u32[]{:S(2)}) collective-permute-start(f32[8,2]{1,0:T(8,128)S(1)} %broadcast_in_dim.62), channel_id=1, source_target_pairs={{0,1},{1,2},{2,3},{3,0},{4,5},{5,6},{6,7},{7,4},{8,9},{9,10},{10,1... | collective-permute-start | bytes 200 | tf_op jit(solution)/shard_map/ppermute | solution.py:632
  90.4 4.3 %collective-permute-start.18 = (f32[8,2]{1,0:T(8,128)S(1)}, f32[8,2]{1,0:T(8,128)S(1)}, u32[]{:S(2)}, u32[]{:S(2)}) collective-permute-start(f32[8,2]{1,0:T(8,128)S(1)} %broadcast_in_dim.62), channel_id=1, source_target_pairs={{0,2},{1,3},{2,0},{3,1},{4,6},{5,7},{6,4},{7,5},{8,10},{9,11},{10,... | collective-permute-start | bytes 200 | tf_op jit(solution)/shard_map/ppermute | solution.py:632
  93.7 2.5 %collective-permute-start.19 = (f32[8,2]{1,0:T(8,128)S(1)}, f32[8,2]{1,0:T(8,128)S(1)}, u32[]{:S(2)}, u32[]{:S(2)}) collective-permute-start(f32[8,2]{1,0:T(8,128)S(1)} %broadcast_in_dim.62), channel_id=1, source_target_pairs={{0,3},{1,0},{2,1},{3,2},{4,7},{5,4},{6,5},{7,6},{8,11},{9,8},{10,9... | collective-permute-start | bytes 200 | tf_op jit(solution)/shard_map/ppermute | solution.py:632
  146.5 7.7 %copy-start.2 = (bf16[16,24,2048]{2,1,0:T(8,128)(2,1)}, bf16[16,24,2048]{2,1,0:T(8,128)(2,1)S(1)}, u32[]{:S(2)}) copy-start(bf16[16,24,2048]{2,1,0:T(8,128)(2,1)S(1)} %all_to_all.11) | copy-start | bytes 4718596
  146.5 10.3 %collective-permute-start.20 = (bf16[2,192,2048]{2,1,0:T(8,128)(2,1)S(1)}, bf16[2,192,2048]{2,1,0:T(8,128)(2,1)S(1)}, u32[]{:S(2)}, u32[]{:S(2)}) collective-permute-start(bf16[2,192,2048]{2,1,0:T(8,128)(2,1)S(1)} %bitcast.32), channel_id=1, source_target_pairs={{0,4},{4,0},{1,5},{5,1},{2,6},{6,2},{3,7},{7,3},{8,12},{12,8},{9,1... | collective-permute-start | bytes 4718600 | tf_op jit(solution)/shard_map/ppermute | solution.py:734
  150.7 3.0 %collective-permute-start.21 = (f32[8,2]{1,0:T(8,128)S(1)}, f32[8,2]{1,0:T(8,128)S(1)}, u32[]{:S(2)}, u32[]{:S(2)}) collective-permute-start(f32[8,2]{1,0:T(8,128)S(1)} %slice_add_fusion), channel_id=1, source_target_pairs={{0,4},{4,0},{1,5},{5,1},{2,6},{6,2},{3,7},{7,3},{8,12},{12,8},{9,1... | collective-permute-start | bytes 200 | tf_op jit(solution)/shard_map/ppermute | solution.py:736
  156.8 1.2 copy-start.3

commit v4 on v3

--- a/solution.py
+++ b/solution.py
@@ -370,8 +370,11 @@
         for i in ((2, 0, 1, 3) if slots else (2,))
     }
     acc_copies = [
-        pltpu.make_async_copy(source, acc_v.at[rel], sem_acc.at[rel])
-        for rel, source in ((0, own.at[0]), (1, near.at[0]), (3, near.at[1]))
+        pltpu.make_async_copy(
+            source.at[at, pl.ds(192 * w, 192)], acc_v.at[rel, pl.ds(192 * w, 192)], sem_acc.at[rel, w]
+        )
+        for rel, source, at in ((0, own, 0), (1, near, 0), (3, near, 1))
+        for w in range(4)
     ]
     their = jnp.minimum(member, 768 // DIAGONAL_ROWS - 1)
     rows_copy = pltpu.make_async_copy(
@@ -570,7 +573,7 @@
         pltpu.SemaphoreType.DMA((2,)),
         pltpu.SemaphoreType.DMA((2,)),
         pltpu.SemaphoreType.DMA((4,)),
-        pltpu.SemaphoreType.DMA((4,)),
+        pltpu.SemaphoreType.DMA((4, 4)),
         pltpu.SemaphoreType.DMA(()),
         pltpu.SemaphoreType.DMA((4, 2)),
         pltpu.SemaphoreType.DMA((4,)),
@@ -599,11 +602,11 @@
     core = where[CORE] if which == 0 else 1 - where[CORE]
     copies = [
         pltpu.make_async_copy(
-            half.at[n // 2, pl.ds(96 * (n % 2), 96)],
-            out.at[2 * core + n // 2, pl.ds(96 * (n % 2), 96)],
+            half.at[n // 6, pl.ds(32 * (n % 6), 32)],
+            out.at[2 * core + n // 6, pl.ds(32 * (n % 6), 32)],
             sems.at[n],
         )
-        for n in range(4)
+        for n in range(12)
     ]
     for copy in copies:
         copy.start()
@@ -620,7 +623,7 @@
         + [hbm] * (len(args) - 2),
         out_specs=hbm,
         out_shape=jax.ShapeDtypeStruct((4,) + half.shape[1:], half.dtype),
-        scratch_shapes=[pltpu.SemaphoreType.DMA((4,))],
+        scratch_shapes=[pltpu.SemaphoreType.DMA((12,))],
         input_output_aliases={} if whole is None else {2: 0},
         cost_estimate=pl.CostEstimate(flops=10**9, bytes_accessed=2**22, transcendentals=0),
         name="place",

time: 161 us -> 162 us (level)
  no operation moved by 1% of the time
where the time goes in v4:
time: 162 us; the launch traced here: 161 us
  Pallas kernels  53.4 us (33%)
  blocking collectives  47.5 us (29%)
  starting transfers between devices  31.2 us (19%)
  waiting for transfers between devices  21.5 us (13%)
  other arithmetic  2.99 us (2%)
  between operations  2.4 us (1%)
  local copies, waits for them, and re-layouts  1.94 us (1%)
    all_to_all x1, blocking collectives, local(): lax.all_to_all(both.reshape(plane, share, bond + EXTRA), ('z', 'y'), 0, 0...  24.9 us
    ppermute x16, starting transfers between devices, shifted(): lax.ppermute(value, axis, [(i, (i + by) % size) for i in range(size)])  22.7 us
    all_to_all x1, blocking collectives, local(): lax.all_to_all(jnp.broadcast_to(summed[None], (plane, share, bond)), ('z'...  22.6 us
    ppermute x16, waiting for transfers between devices, shifted(): lax.ppermute(value, axis, [(i, (i + by) % size) for i in range(size)])  18.5 us
    pallas_call x1, Pallas kernels, finish(): pl.pallas_call(functools.partial(finish_body, slots), in_specs=[smem] * 3...  16.2 us
    pallas_call x2, Pallas kernels, products(): pl.pallas_call(functools.partial(products_body, tuple(rels)), in_specs=[s...  14.2 us
    pallas_call x1, Pallas kernels, select(): pl.pallas_call(select_body, grid=(4,), in_specs=[smem, ids, ids, pl.Block...  8.68 us
    pallas_call x2, Pallas kernels, place(): pl.pallas_call(functools.partial(place_body, which), in_specs=[pl.BlockSp...  5.3 us
  transfers between devices with their start and end apart: 19, of which 5 were waited for; matrix products, arithmetic and copies ran while one was open for 1% of the time, Pallas kernels for 17%

profile of v4, /device:TPU:1, one launch (start us, length us, event | category | flops | bytes accessed | tf_op | source)
XLA Modules:
  0.0 161.1 jit_solution(607842126229678348)
XLA Ops:
  0.6 2.5 %pack_early.1 = (bf16[4,3,192,128]{3,2,1,0:T(8,128)(2,1)}, bf16[4,3,192,128]{3,2,1,0:T(8,128)(2,1)}) custom-call(bf16[8,4,192,192]{3,2,1,0:T(8,128)(2,1)} %right), custom_call_target="tpu_custom_call" | custom-call | tf_op jit(solution)/shard_map/pack_early/pallas_call | solution.py:57
  3.8 4.0 %pack_late.1 = (bf16[13,192,128]{2,1,0:T(8,128)(2,1)}, bf16[13,192,128]{2,1,0:T(8,128)(2,1)}, bf16[13,192,128]{2,1,0:T(8,128)(2,1)}, bf16[13,192,128]{2,1,0:T(8,128)(2,1)}) custom-call(s32[1]{0:T(128)S(6)} %copy.22.count, bf16[8,4,192,192]{3,2,1,0:T(8,128)(2,1)S(1)} %copy-done.1, bf16[8,4,192,192]{3,2,1,0:T(8,128)(2,1)} %right), custom_call_target="tpu_custom_call" | custom-call | flops 2000000000 | bytes 4194304 | tf_op jit(solution)/shard_map/pack_late/pallas_call | solution.py:69
  7.7 2.1 %collective-permute-start.3 = (bf16[13,192,128]{2,1,0:T(8,128)(2,1)}, bf16[13,192,128]{2,1,0:T(8,128)(2,1)S(1)}, u32[]{:S(2)}, u32[]{:S(2)}) collective-permute-start(bf16[13,192,128]{2,1,0:T(8,128)(2,1)} %get-tuple-element.196), channel_id=1, source_target_pairs={{0,8},{8,16},{16,24},{24,0},{1,9},{9,17},{17,25},{25,1},{2,10},{10... | collective-permute-start | bytes 1916936 | tf_op jit(solution)/shard_map/ppermute | solution.py:635
  9.9 1.2 collective-permute-start.9
  11.1 1.5 collective-permute-start.8
  12.5 1.4 collective-permute-start.4
  14.0 1.6 %collective-permute-start.5 = (bf16[13,192,128]{2,1,0:T(8,128)(2,1)}, bf16[13,192,128]{2,1,0:T(8,128)(2,1)S(1)}, u32[]{:S(2)}, u32[]{:S(2)}) collective-permute-start(bf16[13,192,128]{2,1,0:T(8,128)(2,1)} %get-tuple-element.198), channel_id=1, source_target_pairs={{0,32},{32,64},{64,96},{96,0},{1,33},{33,65},{65,97},{97,1},{2,34}... | collective-permute-start | bytes 1916936 | tf_op jit(solution)/shard_map/ppermute | solution.py:635
  15.7 9.5 %collective-permute-done.9.refs_2_ = bf16[4,3,192,128]{3,2,1,0:T(8,128)(2,1)S(1)} collective-permute-done((bf16[4,3,192,128]{3,2,1,0:T(8,128)(2,1)}, bf16[4,3,192,128]{3,2,1,0:T(8,128)(2,1)S(1)}, u32[]{:S(2)}, u32[]{:S(2)}) %collective-permute-start.9) | collective-permute-done | bytes 589856 | tf_op jit(solution)/shard_map/ppermute | solution.py:635
  25.2 2.7 %collective-permute-start.7 = (bf16[4,3,192,128]{3,2,1,0:T(8,128)(2,1)}, bf16[4,3,192,128]{3,2,1,0:T(8,128)(2,1)}, u32[]{:S(2)}, u32[]{:S(2)}) collective-permute-start(bf16[4,3,192,128]{3,2,1,0:T(8,128)(2,1)} %get-tuple-element.204.refs_0_), channel_id=1, source_target_pairs={{0,3},{1,0},{2,1},{3,2},{4,7},{5,4},{6,5},{7,6},{8,11},{9,8},{10,9... | collective-permute-start | bytes 1769480 | tf_op jit(solution)/shard_map/ppermute | solution.py:635
  27.9 3.8 %collective-permute-start.6 = (bf16[13,192,128]{2,1,0:T(8,128)(2,1)}, bf16[13,192,128]{2,1,0:T(8,128)(2,1)}, u32[]{:S(2)}, u32[]{:S(2)}) collective-permute-start(bf16[13,192,128]{2,1,0:T(8,128)(2,1)} %get-tuple-element.199), channel_id=1, source_target_pairs={{0,96},{32,0},{64,32},{96,64},{1,97},{33,1},{65,33},{97,65},{2,98}... | collective-permute-start | bytes 1916936 | tf_op jit(solution)/shard_map/ppermute | solution.py:635
  31.7 8.7 %select.20 = (s32[40]{0:T(128)S(1)}, bf16[768,2048]{1,0:T(8,128)(2,1)}, bf16[4,768,1024]{2,1,0:T(8,128)(2,1)S(1)}, f32[768,1]{1,0:T(8,128)}) custom-call(s32[3]{0:T(128)S(1)} %pad_add_fusion.where, s32[16,128]{1,0:T(8,128)} %bitcast.37, s32[16,128]{1,0:T(8,128)} %bitcast.38, f32[1,2048]{1,0:T(1,128)} %bitcast.39, bf16[2048,2048]{1,0:T(8,128)(2,1)} %psi.1), custom_call_target="tpu_custom_call" | custom-call | flops 5000000000 | bytes 16777216 | tf_op jit(solution)/shard_map/select/pallas_call | solution.py:189
  40.5 2.7 %collective-permute-start.12 = (bf16[4,3,192,128]{3,2,1,0:T(8,128)(2,1)}, bf16[4,3,192,128]{3,2,1,0:T(8,128)(2,1)}, u32[]{:S(2)}, u32[]{:S(2)}) collective-permute-start(bf16[4,3,192,128]{3,2,1,0:T(8,128)(2,1)} %copy-done.6), channel_id=1, source_target_pairs={{0,3},{1,0},{2,1},{3,2},{4,7},{5,4},{6,5},{7,6},{8,11},{9,8},{10,9... | collective-permute-start | bytes 1769480 | tf_op jit(solution)/shard_map/ppermute | solution.py:635
  43.1 5.8 %products.2 = f32[1,768,1024]{2,1,0:T(8,128)} custom-call(s32[3]{0:T(128)S(1)} %pad_add_fusion.where, s32[1]{0:T(128)S(6)} %copy.22.count, bf16[8,4,192,192]{3,2,1,0:T(8,128)(2,1)} %left.4, bf16[4,768,1024]{2,1,0:T(8,128)(2,1)S(1)} %get-tuple-element.202.psi, bf16[4,3,192,128]{3,2,1,0:T(8,128)(2,1)} %get-tuple-element.204.refs_0_, ...), custom_call_target="tpu_custom_call" | custom-call | flops 2818572288 | bytes 8388608 | tf_op jit(solution)/shard_map/products/pallas_call | solution.py:323
  49.0 2.6 %pick.1 = (s32[5]{0:T(128)S(1)}, s32[1]{0:T(128)}, bf16[1,6,192,128]{3,2,1,0:T(8,128)(2,1)}) custom-call(bf16[13,192,128]{2,1,0:T(8,128)(2,1)S(1)} %collective-permute-done.3.refs_0_, bf16[13,192,128]{2,1,0:T(8,128)(2,1)S(1)} %collective-permute-done.4.refs_1_, bf16[13,192,128]{2,1,0:T(8,128)(2,1)S(1)} %collective-permute-done.5.refs_2_, ...), custom_call_target="tpu_custom_call" | custom-call | tf_op jit(solution)/shard_map/pick/pallas_call | solution.py:108
  51.6 0.6 collective-permute-start.14
  52.3 1.1 collective-permute-start.15
  53.4 8.4 %products.3 = f32[2,768,1024]{2,1,0:T(8,128)} custom-call(s32[3]{0:T(128)S(1)} %pad_add_fusion.where, s32[1]{0:T(128)S(6)} %copy.22.count, bf16[8,4,192,192]{3,2,1,0:T(8,128)(2,1)} %left.4, bf16[4,768,1024]{2,1,0:T(8,128)(2,1)} %copy-done, bf16[4,3,192,128]{3,2,1,0:T(8,128)(2,1)} %collective-permute-done.7.refs_0_, bf16[4,3,192,128]{3,2,1,0:T(8,128)(2,1)} %copy-done.6, ...), custom_call_target="tpu_custom_call" | custom-call | flops 5637144576 | bytes 8388608 | tf_op jit(solution)/shard_map/products/pallas_call | solution.py:323
  62.5 6.5 %collective-permute-done.15 = bf16[1,6,192,128]{3,2,1,0:T(8,128)(2,1)} collective-permute-done((bf16[1,6,192,128]{3,2,1,0:T(8,128)(2,1)}, bf16[1,6,192,128]{3,2,1,0:T(8,128)(2,1)}, u32[]{:S(2)}, u32[]{:S(2)}) %collective-permute-start.15) | collective-permute-done | bytes 294944 | tf_op jit(solution)/shard_map/ppermute | solution.py:635
  69.0 16.4 %conditional.1 = ((bf16[384,2048]{1,0:T(8,128)(2,1)}, bf16[384,2048]{1,0:T(8,128)(2,1)}, f32[2,8,128]{2,1,0:T(8,128)S(1)})) conditional(s32[]{:T(128)} %bitcast.10, (f32[2048]{0:T(1024)S(1)}, s32[3]{0:T(128)S(1)}, s32[1]{0:T(128)}, s32[40]{0:T(128)S(1)}, f32[1,768,1024]{2,1,0:T(8,128)}, /*index=5*/f32[2,768,1024]{2,1,0:T(8,128)}, ...), branch_computations={%region_0.0_spmd, %region_1.0_spmd, %region_2.0_spmd} | conditional | flops 8001769472 | bytes 50331776 | solution.py:714
  69.0 16.2 %finish.3 = (bf16[384,2048]{1,0:T(8,128)(2,1)}, bf16[384,2048]{1,0:T(8,128)(2,1)}, f32[2,8,128]{2,1,0:T(8,128)S(1)}) custom-call(s32[3]{0:T(128)S(1)} %get-tuple-element.119.where, s32[1]{0:T(128)} %get-tuple-element.120.count, s32[40]{0:T(128)S(1)} %get-tuple-element.121.table, f32[1,768,1024]{2,1,0:T(8,128)} %get-tuple-element.122.own, ...), custom_call_target="tpu_custom_call" | custom-call | flops 8000000000 | bytes 31457280 | tf_op jit(solution)/shard_map/cond/branch_0_fun/finish/pallas_call | solution.py:588
  85.5 4.4 %collective-permute-start.16 = (bf16[384,2048]{1,0:T(8,128)(2,1)}, bf16[384,2048]{1,0:T(8,128)(2,1)S(1)}, u32[]{:S(2)}, u32[]{:S(2)}) collective-permute-start(bf16[384,2048]{1,0:T(8,128)(2,1)} %get-tuple-element.227), channel_id=1, source_target_pairs={{0,4},{4,0},{1,5},{5,1},{2,6},{6,2},{3,7},{7,3},{8,12},{12,8},{9,1... | collective-permute-start | bytes 4718600 | tf_op jit(solution)/shard_map/ppermute | solution.py:716
  90.5 3.3 %collective-permute-start.18 = (f32[8,2]{1,0:T(8,128)S(1)}, f32[8,2]{1,0:T(8,128)S(1)}, u32[]{:S(2)}, u32[]{:S(2)}) collective-permute-start(f32[8,2]{1,0:T(8,128)S(1)} %broadcast_in_dim.62), channel_id=1, source_target_pairs={{0,2},{1,3},{2,0},{3,1},{4,6},{5,7},{6,4},{7,5},{8,10},{9,11},{10,... | collective-permute-start | bytes 200 | tf_op jit(solution)/shard_map/ppermute | solution.py:635
  93.8 1.0 collective-permute-done.18
  94.9 1.4 collective-permute-done.19
  96.4 2.0 %fusion = bf16[384,2048]{1,0:T(8,128)(2,1)S(1)} fusion(bf16[384,2048]{1,0:T(8,128)(2,1)} %get-tuple-element.226, bf16[384,2048]{1,0:T(8,128)(2,1)S(1)} %collective-permute-done.16), kind=kLoop, calls=%fused_computation.7 | loop fusion | flops 3145728 | bytes 4718592 | tf_op jit(solution)/shard_map/convert_element_type | solution.py:718
  98.8 24.9 %all_to_all.10 = bf16[16,24,2176]{2,1,0:T(8,128)(2,1)S(1)} all-to-all(bf16[16,24,2176]{2,1,0:T(8,128)(2,1)S(1)} %bitcast.31), channel_id=1, replica_groups=mesh['z'=4,'y'=4,'core'=2,'site'=4] {'z','y'}, dimensions={0} | all-to-all | bytes 3342336 | tf_op jit(solution)/shard_map/all_to_all | solution.py:729
  124.1 22.6 %all_to_all.11 = bf16[16,24,2048]{2,1,0:T(8,128)(2,1)S(1)} all-to-all(bf16[16,24,2048]{2,1,0:T(8,128)(2,1)S(1)} %broadcast_in_dim.68), channel_id=1, replica_groups=mesh['z'=4,'y'=4,'core'=2,'site'=4] {'z','y'}, dimensions={0} | all-to-all | bytes 3145728 | tf_op jit(solution)/shard_map/all_to_all | solution.py:732
  146.7 4.1 %collective-permute-start.20 = (bf16[2,192,2048]{2,1,0:T(8,128)(2,1)S(1)}, bf16[2,192,2048]{2,1,0:T(8,128)(2,1)S(1)}, u32[]{:S(2)}, u32[]{:S(2)}) collective-permute-start(bf16[2,192,2048]{2,1,0:T(8,128)(2,1)S(1)} %bitcast.32), channel_id=1, source_target_pairs={{0,4},{4,0},{1,5},{5,1},{2,6},{6,2},{3,7},{7,3},{8,12},{12,8},{9,1... | collective-permute-start | bytes 4718600 | tf_op jit(solution)/shard_map/ppermute | solution.py:737
  150.8 2.9 %collective-permute-done.21 = f32[8,2]{1,0:T(8,128)S(1)} collective-permute-done((f32[8,2]{1,0:T(8,128)S(1)}, f32[8,2]{1,0:T(8,128)S(1)}, u32[]{:S(2)}, u32[]{:S(2)}) %collective-permute-start.21) | collective-permute-done | bytes 96 | tf_op jit(solution)/shard_map/ppermute | solution.py:739
  154.4 2.7 %place.2.rest_0_ = bf16[4,192,2048]{2,1,0:T(8,128)(2,1)} custom-call(s32[3]{0:T(128)S(1)} %pad_add_fusion.where, bf16[2,192,2048]{2,1,0:T(8,128)(2,1)} %bitcast.33), custom_call_target="tpu_custom_call" | custom-call | flops 1000000000 | bytes 4194304 | tf_op jit(solution)/shard_map/place/pallas_call | solution.py:620
  157.1 1.2 copy-done.3
  158.2 2.7 %place.3 = bf16[4,192,2048]{2,1,0:T(8,128)(2,1)} custom-call(s32[3]{0:T(128)S(1)} %pad_add_fusion.where, bf16[2,192,2048]{2,1,0:T(8,128)(2,1)} %copy-done.3, bf16[4,192,2048]{2,1,0:T(8,128)(2,1)} %place.2.rest_0_), custom_call_target="tpu_custom_call", output_to_operand_aliasing={{}: (2, {})} | custom-call | flops 1000000000 | bytes 4194304 | tf_op jit(solution)/shard_map/place/pallas_call | solution.py:620
  (53 shorter events, 2.6 us)
Async XLA Ops:
  0.6 3.1 %copy-start.1 = (bf16[8,4,192,192]{3,2,1,0:T(8,128)(2,1)S(1)}, bf16[8,4,192,192]{3,2,1,0:T(8,128)(2,1)}, u32[]{:S(2)}) copy-start(bf16[8,4,192,192]{3,2,1,0:T(8,128)(2,1)} %left.4) | copy-start | bytes 7077892
  7.7 20.2 %collective-permute-start.3 = (bf16[13,192,128]{2,1,0:T(8,128)(2,1)}, bf16[13,192,128]{2,1,0:T(8,128)(2,1)S(1)}, u32[]{:S(2)}, u32[]{:S(2)}) collective-permute-start(bf16[13,192,128]{2,1,0:T(8,128)(2,1)} %get-tuple-element.196), channel_id=1, source_target_pairs={{0,8},{8,16},{16,24},{24,0},{1,9},{9,17},{17,25},{25,1},{2,10},{10... | collective-permute-start | bytes 1916936 | tf_op jit(solution)/shard_map/ppermute | solution.py:635
  9.9 15.4 %collective-permute-start.9 = (bf16[4,3,192,128]{3,2,1,0:T(8,128)(2,1)}, bf16[4,3,192,128]{3,2,1,0:T(8,128)(2,1)S(1)}, u32[]{:S(2)}, u32[]{:S(2)}) collective-permute-start(bf16[4,3,192,128]{3,2,1,0:T(8,128)(2,1)} %get-tuple-element.204.refs_0_), channel_id=1, source_target_pairs={{0,1},{1,2},{2,3},{3,0},{4,5},{5,6},{6,7},{7,4},{8,9},{9,10},{10,1... | collective-permute-start | bytes 1769480 | tf_op jit(solution)/shard_map/ppermute | solution.py:635
  11.1 14.2 %collective-permute-start.8 = (bf16[4,3,192,128]{3,2,1,0:T(8,128)(2,1)}, bf16[4,3,192,128]{3,2,1,0:T(8,128)(2,1)S(1)}, u32[]{:S(2)}, u32[]{:S(2)}) collective-permute-start(bf16[4,3,192,128]{3,2,1,0:T(8,128)(2,1)} %get-tuple-element.205.refs_1_), channel_id=1, source_target_pairs={{0,3},{1,0},{2,1},{3,2},{4,7},{5,4},{6,5},{7,6},{8,11},{9,8},{10,9... | collective-permute-start | bytes 1769480 | tf_op jit(solution)/shard_map/ppermute | solution.py:635
  12.5 27.8 %collective-permute-start.4 = (bf16[13,192,128]{2,1,0:T(8,128)(2,1)}, bf16[13,192,128]{2,1,0:T(8,128)(2,1)S(1)}, u32[]{:S(2)}, u32[]{:S(2)}) collective-permute-start(bf16[13,192,128]{2,1,0:T(8,128)(2,1)} %get-tuple-element.197), channel_id=1, source_target_pairs={{0,24},{8,0},{16,8},{24,16},{1,25},{9,1},{17,9},{25,17},{2,26},{10... | collective-permute-start | bytes 1916936 | tf_op jit(solution)/shard_map/ppermute | solution.py:635
  14.0 26.5 %collective-permute-start.5 = (bf16[13,192,128]{2,1,0:T(8,128)(2,1)}, bf16[13,192,128]{2,1,0:T(8,128)(2,1)S(1)}, u32[]{:S(2)}, u32[]{:S(2)}) collective-permute-start(bf16[13,192,128]{2,1,0:T(8,128)(2,1)} %get-tuple-element.198), channel_id=1, source_target_pairs={{0,32},{32,64},{64,96},{96,0},{1,33},{33,65},{65,97},{97,1},{2,34}... | collective-permute-start | bytes 1916936 | tf_op jit(solution)/shard_map/ppermute | solution.py:635
  25.2 6.4 %copy-start.5 = (bf16[4,3,192,128]{3,2,1,0:T(8,128)(2,1)}, bf16[4,3,192,128]{3,2,1,0:T(8,128)(2,1)S(1)}, u32[]{:S(2)}) copy-start(bf16[4,3,192,128]{3,2,1,0:T(8,128)(2,1)S(1)} %collective-permute-done.9.refs_2_) | copy-start | bytes 1769476
  25.2 26.4 %collective-permute-start.10 = (bf16[4,3,192,128]{3,2,1,0:T(8,128)(2,1)}, bf16[4,3,192,128]{3,2,1,0:T(8,128)(2,1)}, u32[]{:S(2)}, u32[]{:S(2)}) collective-permute-start(bf16[4,3,192,128]{3,2,1,0:T(8,128)(2,1)} %get-tuple-element.205.refs_1_), channel_id=1, source_target_pairs={{0,1},{1,2},{2,3},{3,0},{4,5},{5,6},{6,7},{7,4},{8,9},{9,10},{10,1... | collective-permute-start | bytes 1769480 | tf_op jit(solution)/shard_map/ppermute | solution.py:635
  25.2 6.4 %copy-start.6 = (bf16[4,3,192,128]{3,2,1,0:T(8,128)(2,1)}, bf16[4,3,192,128]{3,2,1,0:T(8,128)(2,1)S(1)}, u32[]{:S(2)}) copy-start(bf16[4,3,192,128]{3,2,1,0:T(8,128)(2,1)S(1)} %collective-permute-done.8.refs_1_) | copy-start | bytes 1769476
  25.2 27.1 %collective-permute-start.7 = (bf16[4,3,192,128]{3,2,1,0:T(8,128)(2,1)}, bf16[4,3,192,128]{3,2,1,0:T(8,128)(2,1)}, u32[]{:S(2)}, u32[]{:S(2)}) collective-permute-start(bf16[4,3,192,128]{3,2,1,0:T(8,128)(2,1)} %get-tuple-element.204.refs_0_), channel_id=1, source_target_pairs={{0,3},{1,0},{2,1},{3,2},{4,7},{5,4},{6,5},{7,6},{8,11},{9,8},{10,9... | collective-permute-start | bytes 1769480 | tf_op jit(solution)/shard_map/ppermute | solution.py:635
  27.9 21.0 %collective-permute-start.6 = (bf16[13,192,128]{2,1,0:T(8,128)(2,1)}, bf16[13,192,128]{2,1,0:T(8,128)(2,1)}, u32[]{:S(2)}, u32[]{:S(2)}) collective-permute-start(bf16[13,192,128]{2,1,0:T(8,128)(2,1)} %get-tuple-element.199), channel_id=1, source_target_pairs={{0,96},{32,0},{64,32},{96,64},{1,97},{33,1},{65,33},{97,65},{2,98}... | collective-permute-start | bytes 1916936 | tf_op jit(solution)/shard_map/ppermute | solution.py:635
  40.4 8.6 %copy-start = (bf16[4,768,1024]{2,1,0:T(8,128)(2,1)}, bf16[4,768,1024]{2,1,0:T(8,128)(2,1)S(1)}, u32[]{:S(2)}) copy-start(bf16[4,768,1024]{2,1,0:T(8,128)(2,1)S(1)} %get-tuple-element.202.psi) | copy-start | bytes 18874372
  40.4 22.0 %collective-permute-start.11 = (bf16[4,3,192,128]{3,2,1,0:T(8,128)(2,1)}, bf16[4,3,192,128]{3,2,1,0:T(8,128)(2,1)}, u32[]{:S(2)}, u32[]{:S(2)}) collective-permute-start(bf16[4,3,192,128]{3,2,1,0:T(8,128)(2,1)} %copy-done.5), channel_id=1, source_target_pairs={{0,1},{1,2},{2,3},{3,0},{4,5},{5,6},{6,7},{7,4},{8,9},{9,10},{10,1... | collective-permute-start | bytes 1769480 | tf_op jit(solution)/shard_map/ppermute | solution.py:635
  40.5 22.0 %collective-permute-start.12 = (bf16[4,3,192,128]{3,2,1,0:T(8,128)(2,1)}, bf16[4,3,192,128]{3,2,1,0:T(8,128)(2,1)}, u32[]{:S(2)}, u32[]{:S(2)}) collective-permute-start(bf16[4,3,192,128]{3,2,1,0:T(8,128)(2,1)} %copy-done.6), channel_id=1, source_target_pairs={{0,3},{1,0},{2,1},{3,2},{4,7},{5,4},{6,5},{7,6},{8,11},{9,8},{10,9... | collective-permute-start | bytes 1769480 | tf_op jit(solution)/shard_map/ppermute | solution.py:635
  51.5 17.5 %slice-start = ((s8[6291456]{0:T(1024)(128)(4,1)}), s8[4194304]{0:T(1024)(128)(4,1)S(1)}, s32[]{:S(2)}) async-start(s8[6291456]{0:T(1024)(128)(4,1)} %bitcast.29), calls=%async_computation.2 | async-start | bytes 8388608
  51.5 17.5 %slice-start.1 = ((s8[6291456]{0:T(1024)(128)(4,1)}), s8[2097152]{0:T(1024)(128)(4,1)S(1)}, s32[]{:S(2)}) async-start(s8[6291456]{0:T(1024)(128)(4,1)} %bitcast.29), calls=%async_computation.3 | async-start | bytes 4194304
  51.5 17.5 %copy-start.4 = (f32[2048]{0:T(1024)S(1)}, f32[2048]{0:T(1024)}, u32[]{:S(2)}) copy-start(f32[2048]{0:T(1024)} %param.19) | copy-start | bytes 24580
  51.6 10.9 %collective-permute-start.13 = (bf16[1,6,192,128]{3,2,1,0:T(8,128)(2,1)}, bf16[1,6,192,128]{3,2,1,0:T(8,128)(2,1)}, u32[]{:S(2)}, u32[]{:S(2)}) collective-permute-start(bf16[1,6,192,128]{3,2,1,0:T(8,128)(2,1)} %get-tuple-element.209), channel_id=1, source_target_pairs={{0,3},{1,0},{2,1},{3,2},{4,7},{5,4},{6,5},{7,6},{8,11},{9,8},{10,9... | collective-permute-start | bytes 884744 | tf_op jit(solution)/shard_map/ppermute | solution.py:635
  51.6 10.8 %collective-permute-start.14 = (bf16[1,6,192,128]{3,2,1,0:T(8,128)(2,1)}, bf16[1,6,192,128]{3,2,1,0:T(8,128)(2,1)}, u32[]{:S(2)}, u32[]{:S(2)}) collective-permute-start(bf16[1,6,192,128]{3,2,1,0:T(8,128)(2,1)} %get-tuple-element.209), channel_id=1, source_target_pairs={{0,2},{1,3},{2,0},{3,1},{4,6},{5,7},{6,4},{7,5},{8,10},{9,11},{10,... | collective-permute-start | bytes 884744 | tf_op jit(solution)/shard_map/ppermute | solution.py:635
  52.3 16.7 %collective-permute-start.15 = (bf16[1,6,192,128]{3,2,1,0:T(8,128)(2,1)}, bf16[1,6,192,128]{3,2,1,0:T(8,128)(2,1)}, u32[]{:S(2)}, u32[]{:S(2)}) collective-permute-start(bf16[1,6,192,128]{3,2,1,0:T(8,128)(2,1)} %get-tuple-element.209), channel_id=1, source_target_pairs={{0,1},{1,2},{2,3},{3,0},{4,5},{5,6},{6,7},{7,4},{8,9},{9,10},{10,1... | collective-permute-start | bytes 884744 | tf_op jit(solution)/shard_map/ppermute | solution.py:635
  85.5 10.9 %collective-permute-start.16 = (bf16[384,2048]{1,0:T(8,128)(2,1)}, bf16[384,2048]{1,0:T(8,128)(2,1)S(1)}, u32[]{:S(2)}, u32[]{:S(2)}) collective-permute-start(bf16[384,2048]{1,0:T(8,128)(2,1)} %get-tuple-element.227), channel_id=1, source_target_pairs={{0,4},{4,0},{1,5},{5,1},{2,6},{6,2},{3,7},{7,3},{8,12},{12,8},{9,1... | collective-permute-start | bytes 4718600 | tf_op jit(solution)/shard_map/ppermute | solution.py:716
  89.9 3.9 %collective-permute-start.17 = (f32[8,2]{1,0:T(8,128)S(1)}, f32[8,2]{1,0:T(8,128)S(1)}, u32[]{:S(2)}, u32[]{:S(2)}) collective-permute-start(f32[8,2]{1,0:T(8,128)S(1)} %broadcast_in_dim.62), channel_id=1, source_target_pairs={{0,1},{1,2},{2,3},{3,0},{4,5},{5,6},{6,7},{7,4},{8,9},{9,10},{10,1... | collective-permute-start | bytes 200 | tf_op jit(solution)/shard_map/ppermute | solution.py:635
  90.5 4.3 %collective-permute-start.18 = (f32[8,2]{1,0:T(8,128)S(1)}, f32[8,2]{1,0:T(8,128)S(1)}, u32[]{:S(2)}, u32[]{:S(2)}) collective-permute-start(f32[8,2]{1,0:T(8,128)S(1)} %broadcast_in_dim.62), channel_id=1, source_target_pairs={{0,2},{1,3},{2,0},{3,1},{4,6},{5,7},{6,4},{7,5},{8,10},{9,11},{10,... | collective-permute-start | bytes 200 | tf_op jit(solution)/shard_map/ppermute | solution.py:635
  93.8 2.5 %collective-permute-start.19 = (f32[8,2]{1,0:T(8,128)S(1)}, f32[8,2]{1,0:T(8,128)S(1)}, u32[]{:S(2)}, u32[]{:S(2)}) collective-permute-start(f32[8,2]{1,0:T(8,128)S(1)} %broadcast_in_dim.62), channel_id=1, source_target_pairs={{0,3},{1,0},{2,1},{3,2},{4,7},{5,4},{6,5},{7,6},{8,11},{9,8},{10,9... | collective-permute-start | bytes 200 | tf_op jit(solution)/shard_map/ppermute | solution.py:635
  146.7 7.7 %copy-start.2 = (bf16[16,24,2048]{2,1,0:T(8,128)(2,1)}, bf16[16,24,2048]{2,1,0:T(8,128)(2,1)S(1)}, u32[]{:S(2)}) copy-start(bf16[16,24,2048]{2,1,0:T(8,128)(2,1)S(1)} %all_to_all.11) | copy-start | bytes 4718596
  146.7 10.4 %collective-permute-start.20 = (bf16[2,192,2048]{2,1,0:T(8,128)(2,1)S(1)}, bf16[2,192,2048]{2,1,0:T(8,128)(2,1)S(1)}, u32[]{:S(2)}, u32[]{:S(2)}) collective-permute-start(bf16[2,192,2048]{2,1,0:T(8,128)(2,1)S(1)} %bitcast.32), channel_id=1, source_target_pairs={{0,4},{4,0},{1,5},{5,1},{2,6},{6,2},{3,7},{7,3},{8,12},{12,8},{9,1... | collective-permute-start | bytes 4718600 | tf_op jit(solution)/shard_map/ppermute | solution.py:737
  150.8 3.0 %collective-permute-start.21 = (f32[8,2]{1,0:T(8,128)S(1)}, f32[8,2]{1,0:T(8,128)S(1)}, u32[]{:S(2)}, u32[]{:S(2)}) collective-permute-start(f32[8,2]{1,0:T(8,128)S(1)} %slice_add_fusion), channel_id=1, source_target_pairs={{0,4},{4,0},{1,5},{5,1},{2,6},{6,2},{3,7},{7,3},{8,12},{12,8},{9,1... | collective-permute-start | bytes 200 | tf_op jit(solution)/shard_map/ppermute | solution.py:739
  157.1 1.2 copy-start.3
